TPU v7x, 16 devices: a whole 2x2x2 slice. The times are simulated.
16 devices in a mesh: graph: 16 (over z, y, x, core).
Axes of the slice: x: 2, y: 2, z: 2, core: 2. Of those that a mesh axis runs over, the one named last changes fastest.
Arguments:
- node_feats: bfloat16 [32768, 128], P('graph')
- w_one: float32 [128, 256], replicated
- w_two: float32 [256, 172], replicated
- send_idx: int32 [32, 1024], P('graph')
- edge_src: int32 [131072], P('graph')
- edge_dst: int32 [131072], P('graph')
- edge_w: float32 [131072], P('graph')
- labels: int32 [32768], P('graph')
- label_mask: int32 [32768], P('graph')
Outputs:
- output 1: float32 [], replicated
- output 2: float32 [128, 256], replicated
- output 3: float32 [256, 172], replicated
All inputs are finite; a program needn't handle non-finite values.
Results may differ from a plain program's by a relative error of at most 0.001.
Values are sent between devices in bfloat16 or wider.
A program may use at most 1 GiB of HBM per device.

v0:
```python
import functools

import jax
import jax.numpy as jnp
from jax import lax
from jax.experimental import pallas as pl
from jax.experimental.pallas import tpu as pltpu
from jax.sharding import PartitionSpec as P

AXIS = "graph"
LANES = 128
ROWS_A = (((0,), (0,)), ((), ()))
COLS_A = (((1,), (1,)), ((), ()))
F32, BF16 = jnp.float32, jnp.bfloat16
VMEM = pl.BlockSpec(memory_space=pltpu.VMEM)
SMEM = pl.BlockSpec(memory_space=pltpu.SMEM)
ANY = pl.BlockSpec(memory_space=pl.ANY)
STEP = 512
PREP_CHUNK = 64
SEGMENT = 1024
MESH = pl.DeviceIdType.MESH


def dot(a, b, dims=(((1,), (0,)), ((), ()))):
    return lax.dot_general(a, b, dims, preferred_element_type=F32)


def fill_zero(ref):
    zero = jnp.zeros((STEP, LANES), F32)

    @pl.loop(0, ref.shape[0], step=STEP)
    def _(i):
        ref[pl.ds(i, STEP), :] = zero


def copy_in(dst, src):
    @pl.loop(0, dst.shape[0], step=STEP)
    def _(i):
        dst[pl.ds(i, STEP), :] = src[pl.ds(i, STEP), :].astype(F32)


class Edges:
    def __init__(self, first, last, src, dst, w, src_s, dst_s, sems):
        self.first, self.last, self.w = first, last, w
        self.src, self.dst = src_s, dst_s
        self.pairs = ((src, src_s), (dst, dst_s))
        self.sems = sems

    def copies(self, seg):
        part = pl.ds(pl.multiple_of(seg * SEGMENT, SEGMENT), SEGMENT)
        return [pltpu.make_async_copy(a.at[part], b.at[part], self.sems.at[i, seg]) for i, (a, b) in enumerate(self.pairs)]

    def fetch(self):
        per = SEGMENT // PREP_CHUNK
        for seg in range(self.src.shape[0] // SEGMENT):

            @pl.when(jnp.logical_and(seg * per < self.last, (seg + 1) * per > self.first))
            def _():
                for c in self.copies(seg):
                    c.start()

    def walk(self, chunk, from_idx, to_idx, table, accs, wait):
        group, per, ratio = len(accs), SEGMENT // chunk, PREP_CHUNK // chunk
        first, last = self.first * ratio, self.last * ratio

        def body(c, _):
            base = c * chunk
            w_chunk = self.w.at[pl.ds(pl.multiple_of(base, chunk), chunk)]
            for g in range(0, chunk, group):
                pend = []
                for u in range(group):
                    k = base + g + u
                    s = pl.multiple_of(from_idx[k], 2)
                    d = pl.multiple_of(to_idx[k], 2)
                    pend.append((d, accs[u][pl.ds(d, 2), :] + table[pl.ds(s, 2), :] * w_chunk[g + u : g + u + 1, :]))
                for u in range(group):
                    accs[u][pl.ds(pend[u][0], 2), :] = pend[u][1]
            return 0

        if not wait:
            lax.fori_loop(first, last, body, 0)
            return

        def segment(seg, _):
            for c in self.copies(seg):
                c.wait()
            lax.fori_loop(jnp.maximum(first, seg * per), jnp.minimum(last, (seg + 1) * per), body, 0)
            return 0

        lax.fori_loop(first // per, (last + per - 1) // per, segment, 0)


def one_hot_rows(idx, which, start, table):
    lane = lax.broadcasted_iota(jnp.int32, (LANES, LANES), 1)
    hot = []
    for q in range(2):
        want = spread(idx[which : which + 1, pl.ds(pl.multiple_of(start + q * LANES, LANES), LANES)])
        hot.append(
            jnp.concatenate([jnp.where(want == lane + LANES * j, 1.0, 0.0).astype(BF16) for j in range(table.shape[0] // LANES)], axis=1)
        )
    return dot(jnp.concatenate(hot, axis=0), table[...])


def low_lanes(rows):
    return lax.broadcasted_iota(jnp.int32, (rows, LANES), 1) < LANES // 2


def swap_lanes(v):
    return pltpu.roll(v, LANES // 2, 1)


def fetch_index(send, idx, sems):
    parts = [pl.ds(i, LANES) for i in range(0, send.shape[1], LANES)]
    return [pltpu.make_async_copy(send.at[1, p], idx.at[p], sems.at[i]) for i, p in enumerate(parts)]


def gather_block(send, idx, i, table_b, table, buf):
    got = one_hot_rows(send, 0, i, table_b)
    out = buf.at[pl.ds(pl.multiple_of(2 * i, 512), 512)]
    for u in range(256):
        s = pl.multiple_of(idx[i + u] * 2, 2)
        out[2 * u : 2 * u + 2, :] = table[pl.ds(s, 2), :]
    return got


def gather_rows(send, idx, table_b, table, buf, to_prev, to_next):
    @pl.loop(0, to_prev.shape[0], step=256)
    def _(i):
        i = pl.multiple_of(i, 256)
        to_prev[pl.ds(i, 256), :] = gather_block(send, idx, i, table_b, table, buf).astype(BF16)

    @pl.loop(0, to_next.shape[0], step=256)
    def _(i):
        to_next[pl.ds(pl.multiple_of(i, 256), 256), :] = jnp.concatenate(halves([buf], i, 256), axis=1).astype(BF16)


def pack_rows(out, i, a_even, a_odd, b_even, b_odd):
    halo = out.shape[0] * 2 // 3
    out[pl.ds(i, 256), :] = a_even.astype(out.dtype)
    out[pl.ds(halo // 2 + i, 256), :] = b_even.astype(out.dtype)
    out[pl.ds(halo + i, 256), :] = jnp.where(low_lanes(256), a_odd, swap_lanes(b_odd)).astype(out.dtype)


def gather_packed(send, idx, table_b, table, buf, to_prev, to_next):
    half = to_prev.shape[0] // 3

    @pl.loop(0, half, step=256)
    def _(i):
        i = pl.multiple_of(i, 256)
        a = gather_block(send, idx, i, table_b, table, buf)
        b = gather_block(send, idx, half + i, table_b, table, buf)
        pack_rows(to_prev, i, a[:, :LANES], a[:, LANES:], b[:, :LANES], b[:, LANES:])

    @pl.loop(0, half, step=256)
    def _(i):
        i = pl.multiple_of(i, 256)
        pack_rows(to_next, i, *halves([buf], i, 256), *halves([buf], half + i, 256))


def unpack_rows(got, table, start):
    halo = got.shape[0] * 2 // 3

    @pl.loop(0, halo // 2, step=256)
    def _(i):
        i = pl.multiple_of(i, 256)
        a, b, both = (got[pl.ds(k + i, 256), :].astype(F32) for k in (0, halo // 2, halo))
        put_halves(table, start + i, 256, a, jnp.where(low_lanes(256), both, 0.0))
        put_halves(table, start + halo // 2 + i, 256, b, jnp.where(low_lanes(256), swap_lanes(both), 0.0))


def unpack_plain(got, table, start):
    @pl.loop(0, got.shape[0], step=256)
    def _(i):
        t = got[pl.ds(i, 256), :].astype(F32)
        put_halves(table, start + i, 256, t[:, :LANES], t[:, LANES:])


def spread(row):
    return jnp.transpose(jnp.broadcast_to(row, (LANES, LANES)))


def return_rows(idx, start, vals, accs, chunk=32):
    group = len(accs)

    @pl.loop(0, vals.shape[0] // (2 * chunk))
    def _(c):
        block = vals.at[pl.ds(pl.multiple_of(c * 2 * chunk, 2 * chunk), 2 * chunk)]
        for g in range(0, chunk, group):
            pend = []
            for u in range(group):
                d = pl.multiple_of(idx[start + c * chunk + g + u], 2)
                pend.append((d, accs[u][pl.ds(d, 2), :] + block[2 * (g + u) : 2 * (g + u) + 2, :]))
            for u in range(group):
                accs[u][pl.ds(pend[u][0], 2), :] = pend[u][1]


def halves(accs, i, n):
    even = functools.reduce(jnp.add, [a[pl.ds(2 * i, n, stride=2), :] for a in accs])
    odd = functools.reduce(jnp.add, [a[pl.ds(2 * i + 1, n, stride=2), :] for a in accs])
    return even, odd


def put_halves(table, i, n, even, odd):
    table[pl.ds(2 * i, n, stride=2), :] = even
    table[pl.ds(2 * i + 1, n, stride=2), :] = odd


def greet(n):
    me = lax.axis_index(AXIS)
    barrier = pltpu.get_barrier_semaphore()
    for o in range(1, n):
        pl.semaphore_signal(barrier, inc=1, device_id=(lax.rem(me + o, n),), device_id_type=MESH)
    return me, lambda: pl.semaphore_wait(barrier, n - 1)


def remote(src, dst, send_sem, recv_sem, peer):
    return pltpu.make_async_remote_copy(
        src_ref=src, dst_ref=dst, send_sem=send_sem, recv_sem=recv_sem, device_id=(peer,), device_id_type=MESH
    )


def first_kernel(x, w1, send, after, tab, to_prev, to_next, tab_b, buf, idx, sems):
    fetch = fetch_index(send, idx, sems)
    for c in fetch:
        c.start()
    rows = x.shape[0]
    w = w1[...].astype(BF16)

    @pl.loop(0, rows, step=256)
    def _(i):
        t = dot(x[pl.ds(i, 256), :], w).astype(BF16)
        tab_b[pl.ds(i, 256), :] = t
        t = t.astype(F32)
        put_halves(tab, i, 256, t[:, :LANES], t[:, LANES:])

    for c in fetch:
        c.wait()
    gather_rows(send, idx, tab_b, tab, buf, to_prev, to_next)


def count_kernel(n, mask, after, count, mine, theirs, send_sem, recv_sem):
    me, met = greet(n)
    mine[...] = jnp.sum(mask[...].astype(F32).reshape(-1, 8, LANES), axis=0)
    met()
    copies = [remote(mine, theirs.at[o - 1], send_sem.at[o - 1], recv_sem.at[o - 1], lax.rem(me + o, n)) for o in range(1, n)]
    for c in copies:
        c.start()
    for c in copies:
        c.wait()
    every = jnp.sum(mine[...] + jnp.sum(theirs[...], axis=0), keepdims=True)
    count[...] = jnp.maximum(jnp.broadcast_to(every, count.shape), 1.0)


def reduce_kernel(n, one, two, loss, count, one_out, two_out, mean, work, full, got_pair, got_rest, sems):
    me = lax.axis_index(AXIS)
    chips, core = n // 2, lax.rem(me, 2)
    chip = lax.div(me, 2)
    pair = me + 1 - 2 * core
    others = [lax.rem(chip + o, chips) for o in range(1, chips)]
    barrier = pltpu.get_barrier_semaphore()
    for p in [pair] + [2 * c + core for c in others]:
        pl.semaphore_signal(barrier, inc=1, device_id=(p,), device_id_type=MESH)
    classes = two_out.shape[0]
    lines = -(-classes // 8) * 8
    top, wide = one.shape
    work[0:top, :] = one[:, :LANES]
    work[top : 2 * top, :] = one[:, LANES:]
    work[2 * top : 2 * top + lines, :] = two[:lines, :LANES]
    work[2 * top + lines : 2 * top + 2 * lines, :] = two[:lines, LANES:]
    tail = 2 * top + 2 * lines
    work[tail : tail + 8, :] = loss[...]
    work[tail + 8 :, :] = jnp.zeros((work.shape[0] - tail - 8, LANES), F32)
    pl.semaphore_wait(barrier, chips)

    half = work.shape[0] // 2
    piece = half // chips
    rows = lambda start, size: pl.ds(pl.multiple_of(start, 8), size)
    mine, other = rows(core * half, half), rows((1 - core) * half, half)
    swap = remote(work.at[other], got_pair, sems.at[0, 0], sems.at[1, 0], pair)
    swap.start()
    swap.wait()
    work[mine, :] += got_pair[...]
    scatter = [
        remote(work.at[rows(core * half + c * piece, piece)], got_rest.at[o], sems.at[0, 1 + o], sems.at[1, 1 + o], 2 * c + core)
        for o, c in enumerate(others)
    ]
    for c in scatter:
        c.start()
    for c in scatter:
        c.wait()
    own = rows(core * half + chip * piece, piece)
    work[own, :] += jnp.sum(got_rest[...], axis=0)
    full[own, :] = work[own, :]
    gather = [
        remote(work.at[own], full.at[own], sems.at[0, chips + o], sems.at[1, chips + o], 2 * c + core) for o, c in enumerate(others)
    ]
    for c in gather:
        c.start()
    for c in gather:
        c.wait()
    last = remote(full.at[mine], full.at[mine], sems.at[0, 2 * chips - 1], sems.at[1, 2 * chips - 1], pair)
    last.start()
    last.wait()
    one_out[:, :LANES] = full[0:top, :]
    one_out[:, LANES:] = full[top : 2 * top, :]
    two_out[:, :LANES] = full[2 * top : 2 * top + classes, :]
    two_out[:, LANES:] = full[2 * top + lines : 2 * top + lines + classes, :]
    mean[...] = jnp.sum(full[tail : tail + 8, :], keepdims=True) / count[0:1, 0:1]


def prep_kernel(chunk, rows, src, dst, w, src_out, dst_out, w_out, counts, total):
    lines = src.shape[0]
    slots = src_out.shape[0]
    live = w[...] != 0.0
    halo = src[...] >= rows
    at = lambda shape, axis: lax.broadcasted_iota(jnp.int32, shape, axis)
    before = (at((LANES, LANES), 0) < at((LANES, LANES), 1)).astype(BF16)
    above = (at((lines, lines), 1) < at((lines, lines), 0)).astype(BF16)
    ones = jnp.ones((LANES, LANES), BF16)

    def rank(mask):
        m = mask.astype(F32).astype(BF16)
        return dot(m, before) + dot(above, dot(m, ones).astype(BF16))

    is_local, is_halo = jnp.logical_and(live, jnp.logical_not(halo)), jnp.logical_and(live, halo)
    n_local = jnp.sum(is_local.astype(F32)).astype(jnp.int32)
    n_halo = jnp.sum(is_halo.astype(F32)).astype(jnp.int32)
    local_chunks = (n_local + chunk - 1) // chunk
    counts[0] = local_chunks
    counts[1] = local_chunks + (n_halo + chunk - 1) // chunk
    pos = jnp.where(
        is_local, rank(is_local).astype(jnp.int32), jnp.where(is_halo, rank(is_halo).astype(jnp.int32) + local_chunks * chunk, -1)
    )
    line, lane = pos >> 7, pos & (LANES - 1)
    s = jnp.where(halo, src[...] - rows, src[...])
    d = dst[...]
    half_w = w[...] * 0.5
    w_a = half_w.astype(BF16).astype(F32)
    w_b = (half_w - w_a).astype(BF16).astype(F32)
    w_c = half_w - w_a - w_b
    high = ((s >> 8) * 8 + (d >> 8)).astype(F32)
    planes = [(s & 255).astype(F32), (d & 255).astype(F32), high, w_a, w_b, w_c]
    acc = jnp.zeros((len(planes) * slots, LANES), F32)
    for r in range(0, lines, 2):
        lhs, rhs = [], []
        for q in (r, r + 1):
            pick = at((slots, LANES), 0) == line[q : q + 1, :]
            lhs.append(jnp.concatenate([jnp.where(pick, p[q : q + 1, :], 0.0) for p in planes], axis=0))
            rhs.append((at((LANES, LANES), 0) == lane[q : q + 1, :]).astype(F32))
        acc += dot(jnp.concatenate(lhs, axis=1).astype(BF16), jnp.concatenate(rhs, axis=1).astype(BF16), COLS_A)
    total[...] = acc
    plane = lambda i: total[i * slots : (i + 1) * slots, :]
    high = plane(2).astype(jnp.int32)
    src_out[...] = ((high >> 3) * 256 + plane(0).astype(jnp.int32)) * 2
    dst_out[...] = ((high & 7) * 256 + plane(1).astype(jnp.int32)) * 2
    total[0:slots, :] = (plane(3) + plane(4) + plane(5)) * 2.0

    @pl.loop(0, slots // 8)
    def _(r):
        for q in range(8):
            w_out[pl.ds(pl.multiple_of((r * 8 + q) * LANES, LANES), LANES), :] = spread(total[pl.ds(r * 8 + q, 1), :])


def local_kernel(chunk, backward, counts, src, dst, w, table, out, src_s, dst_s, sems, *accs):
    edges = Edges(0, counts[0], src, dst, w, src_s, dst_s, sems)
    edges.fetch()
    for a in accs:
        fill_zero(a)
    edges.walk(chunk, *((dst_s, src_s) if backward else (src_s, dst_s)), table, accs, True)

    @pl.loop(0, out.shape[0], step=STEP)
    def _(i):
        out[pl.ds(i, STEP), :] = functools.reduce(jnp.add, [a[pl.ds(i, STEP), :] for a in accs])


def forward_halo(chunk, edges, from_prev, from_next, part, htab, accs, unpack):
    edges.fetch()
    unpack(from_prev, htab, 0)
    unpack(from_next, htab, htab.shape[0] // 4)
    copy_in(accs[0], part)
    for a in accs[1:]:
        fill_zero(a)
    edges.walk(chunk, edges.src, edges.dst, htab, accs, True)


def backward_halo(chunk, edges, grad, back_prev, back_next, accs, wait):
    for a in accs:
        fill_zero(a)
    edges.walk(chunk, edges.dst, edges.src, grad, accs, wait)
    split = accs[0].shape[0] // 2
    if back_prev.shape[0] == split:

        @pl.loop(0, split, step=STEP)
        def _(i):
            back_prev[pl.ds(i, STEP), :] = functools.reduce(jnp.add, [a[pl.ds(i, STEP), :] for a in accs])
            back_next[pl.ds(i, STEP), :] = functools.reduce(jnp.add, [a[pl.ds(split + i, STEP), :] for a in accs])
        return
    halo = split // 2

    @pl.loop(0, halo // 2, step=256)
    def _(i):
        i = pl.multiple_of(i, 256)
        for start, out in ((0, back_prev), (halo, back_next)):
            pack_rows(out, i, *halves(accs, start + i, 256), *halves(accs, start + halo // 2 + i, 256))


def padded(w, buf):
    low = w.shape[0] // 8 * 8
    buf[low:, :] = jnp.zeros((buf.shape[0] - low, buf.shape[1]), F32)
    buf[0 : w.shape[0], :] = w[...]
    return buf[...].astype(BF16)


def hidden_kernel(chunk, counts, src, dst, w, send, from_prev, from_next, part, w2, hid, tab, to_prev, to_next, back, htab, tab_b, w2_pad, buf, idx, idx_sems, src_s, dst_s, sems, *accs):
    fetch = fetch_index(send, idx, idx_sems)
    for c in fetch:
        c.start()
    edges = Edges(counts[0], counts[1], src, dst, w, src_s, dst_s, sems)
    w2_b = padded(w2, w2_pad)
    per = send.shape[1] // LANES
    for i in range(2 * per):
        back[i : i + 1, :] = send[i // per : i // per + 1, (i % per) * LANES : (i % per + 1) * LANES] * 2
    forward_halo(chunk, edges, from_prev, from_next, part, htab, accs, unpack_plain)

    @pl.loop(0, hid.shape[0], step=256)
    def _(i):
        even, odd = halves(accs, i, 256)
        h = jnp.concatenate([jnp.maximum(even, 0.0), jnp.maximum(odd, 0.0)], axis=1).astype(BF16)
        hid[pl.ds(i, 256), :] = h
        t = dot(h, w2_b, COLS_A).astype(BF16)
        tab_b[pl.ds(i, 256), :] = t
        t = t.astype(F32)
        put_halves(tab, i, 256, t[:, :LANES], t[:, LANES:])

    for c in fetch:
        c.wait()
    gather_packed(send, idx, tab_b, tab, buf, to_prev, to_next)


def loss_kernel(chunk, classes, counts, src, dst, w, count, from_prev, from_next, part, labels, mask, loss, grad, back_prev, back_next, htab, src_s, dst_s, sems, *accs):
    edges = Edges(counts[0], counts[1], src, dst, w, src_s, dst_s, sems)
    forward_halo(chunk, edges, from_prev, from_next, part, htab, accs, unpack_rows)
    lane = lax.broadcasted_iota(jnp.int32, (LANES, LANES), 1)
    live = lane < classes - LANES
    scale = 1.0 / count[0:1, :]
    loss[...] = jnp.zeros_like(loss)

    @pl.loop(0, labels.shape[0] // 2)
    def _(pair):
        for b in (pair * 2, pair * 2 + 1):
            even, odd = halves(accs, b * LANES, LANES)
            label = spread(labels[pl.ds(b, 1), :])
            keep = spread(mask[pl.ds(b, 1), :]).astype(F32)
            odd = jnp.where(live, odd, -jnp.inf)
            top = jnp.max(jnp.maximum(even, odd), axis=1, keepdims=True)
            total = jnp.sum(jnp.exp(even - top) + jnp.exp(odd - top), axis=1, keepdims=True)
            norm = top + jnp.log(total)
            hit_even, hit_odd = lane == label, lane + LANES == label
            picked = jnp.where(hit_even, even, 0.0) + jnp.where(hit_odd, odd, 0.0)
            per_row = jnp.where(lane == 0, norm, 0.0) - picked
            loss[...] += jnp.sum((keep * per_row).reshape(LANES // 8, 8, LANES), axis=0)
            d_even = (jnp.exp(even - norm) - hit_even.astype(F32)) * (keep * scale)
            d_odd = (jnp.exp(odd - norm) - hit_odd.astype(F32)) * (keep * scale)
            put_halves(grad, b * LANES, LANES, d_even, d_odd)

    backward_halo(chunk, edges, grad, back_prev, back_next, accs, False)


def take_returns(send, part, got_prev, got_next, accs):
    copy_in(accs[0], part)
    for a in accs[1:]:
        fill_zero(a)
    return_rows(send, send.shape[0] // 2, got_prev, accs)
    return_rows(send, 0, got_next, accs)


def middle_kernel(chunk, counts, src, dst, w, send, got_prev, got_next, part, hid, w2, grad_two, grad, back_prev, back_next, returned, w2_pad, src_s, dst_s, sems, *accs):
    edges = Edges(counts[0], counts[1], src, dst, w, src_s, dst_s, sems)
    edges.fetch()
    w2_b = padded(w2, w2_pad)
    split = returned.shape[0] // 2
    unpack_rows(got_prev, returned, 0)
    unpack_rows(got_next, returned, split // 2)
    take_returns(send, part, returned.at[pl.ds(0, split)], returned.at[pl.ds(split, split)], accs)
    grad_two[...] = jnp.zeros_like(grad_two)

    @pl.loop(0, hid.shape[0], step=256)
    def _(i):
        even, odd = halves(accs, i, 256)
        d_tab = jnp.concatenate([even, odd], axis=1).astype(BF16)
        h = hid[pl.ds(i, 256), :]
        grad_two[...] += dot(d_tab, h, ROWS_A)
        d_hid = dot(d_tab, w2_b)
        d_pre = jnp.where(h > 0, d_hid, 0.0)
        put_halves(grad, i, 256, d_pre[:, :LANES], d_pre[:, LANES:])

    backward_halo(chunk, edges, grad, back_prev, back_next, accs, True)


def last_kernel(send, got_prev, got_next, part, x, grad_one, *accs):
    take_returns(send, part, got_prev, got_next, accs)
    grad_one[...] = jnp.zeros_like(grad_one)

    @pl.loop(0, x.shape[0], step=256)
    def _(i):
        even, odd = halves(accs, i, 256)
        d_tab = jnp.concatenate([even, odd], axis=1).astype(BF16)
        grad_one[...] += dot(x[pl.ds(i, 256), :], d_tab, ROWS_A)


def call(body, name, outs, ins, scratch, flops=10**9, out_specs=None, collective=None, vmem=14):
    extra = {} if collective is None else dict(collective_id=collective, has_side_effects=True)
    return pl.pallas_call(
        body, name=name, out_shape=outs, in_specs=ins, out_specs=out_specs or jax.tree.map(lambda _: VMEM, outs),
        scratch_shapes=[pltpu.VMEM(s, F32) if isinstance(s, tuple) else s for s in scratch],
        compiler_params=pltpu.CompilerParams(vmem_limit_bytes=vmem * 2**20, **extra),
        cost_estimate=pl.CostEstimate(flops=flops, bytes_accessed=8 * 2**20, transcendentals=0),
    )


def solution(mesh):
    num_dev = mesh.shape[AXIS]
    to_next = [(d, (d + 1) % num_dev) for d in range(num_dev)]
    to_prev = [(d, (d - 1) % num_dev) for d in range(num_dev)]

    def step(x, w_one, w_two, send, edge_src, edge_dst, edge_w, labels, mask):
        rows, halo, edges, classes = x.shape[0], send.shape[1], edge_src.shape[0], w_two.shape[1]
        tab = (2 * rows, LANES)
        half = (2 * halo, LANES)
        sds = jax.ShapeDtypeStruct
        tab_f, half_f, half_b = sds(tab, F32), sds(half, F32), sds((halo, 2 * LANES), BF16)
        pack_f, pack_b = sds((3 * halo // 2, LANES), F32), sds((3 * halo // 2, LANES), BF16)
        tab_b = pltpu.VMEM((rows, 2 * LANES), BF16)
        one = sds((8, LANES), F32)
        dma = pltpu.SemaphoreType.DMA
        chunk_l, chunk_h = 64, 32
        lines = edges // LANES
        slots = lines + 8
        w2 = w_two.T
        w2_pad = (2 * LANES, 2 * LANES)
        mask = mask.reshape(-1, LANES)

        lined = lambda a: a.reshape(lines, LANES)
        ints = sds((slots, LANES), jnp.int32)
        src, dst, w, counts = call(
            functools.partial(prep_kernel, PREP_CHUNK, rows), "prep", [ints, ints, sds((slots * LANES, LANES), F32), sds((2,), jnp.int32)], [VMEM] * 3,
            [(6 * slots, LANES)], out_specs=[VMEM] * 3 + [SMEM], vmem=8,
        )(lined(edge_src), lined(edge_dst), lined(edge_w))
        src, dst = src.reshape(-1), dst.reshape(-1)

        list_s = [pltpu.SMEM((halo,), jnp.int32), dma((halo // LANES,))]
        tab_one, to_p, to_n = call(first_kernel, "first", [tab_f, half_b, half_b], [VMEM] * 3 + [SMEM], [tab_b, half] + list_s, vmem=8)(x, w_one, send, counts)
        from_prev = lax.ppermute(to_n, AXIS, to_next)
        from_next = lax.ppermute(to_p, AXIS, to_prev)

        walk = [SMEM, ANY, ANY, VMEM]
        index = pltpu.SMEM((slots * LANES,), jnp.int32)
        walk_s = [index, index, dma((2, slots * LANES // SEGMENT))]
        local, local_back = (
            call(functools.partial(local_kernel, chunk_l, back), "local_edges", tab_f, walk + [VMEM], walk_s + [tab] * 4, 10**10)
            for back in (False, True)
        )
        part = local(counts, src, dst, w, tab_one)
        count = call(
            functools.partial(count_kernel, num_dev), "count", one, [VMEM, ANY],
            [(8, LANES), (num_dev - 1, 8, LANES), dma((num_dev - 1,)), dma((num_dev - 1,))], vmem=2, collective=0, flops=10**9,
        )(mask, part)
        hid, tab_two, to_p, to_n, back = call(
            functools.partial(hidden_kernel, chunk_h), "hidden", [sds((rows, 2 * LANES), BF16), tab_f, pack_b, pack_b, sds((2 * halo // LANES, LANES), jnp.int32)],
            walk + [VMEM] * 5, [tab, tab_b, w2_pad, half] + list_s + walk_s + [tab] * 4,
        )(counts, src, dst, w, send, from_prev, from_next, part, w2)
        from_prev = lax.ppermute(to_n, AXIS, to_next)
        from_next = lax.ppermute(to_p, AXIS, to_prev)
        back = back.reshape(-1)
        part = local(counts, src, dst, w, tab_two)
        loss, grad, to_p, to_n = call(
            functools.partial(loss_kernel, chunk_h, classes), "loss", [sds((8, LANES), F32), tab_f, pack_f, pack_f],
            walk + [VMEM] * 6, [tab] + walk_s + [tab] * 4,
        )(counts, src, dst, w, count, from_prev, from_next, part, labels.reshape(-1, LANES), mask)
        got_prev = lax.ppermute(to_p, AXIS, to_prev)
        got_next = lax.ppermute(to_n, AXIS, to_next)
        part = local_back(counts, src, dst, w, grad)
        grad_two, grad, to_p, to_n = call(
            functools.partial(middle_kernel, chunk_h), "middle", [sds((2 * LANES, 2 * LANES), F32), tab_f, half_f, half_f],
            walk + [SMEM] + [VMEM] * 5, [tab, w2_pad] + walk_s + [tab] * 4,
        )(counts, src, dst, w, back, got_prev, got_next, part, hid, w2)
        got_prev = lax.ppermute(to_p, AXIS, to_prev)
        got_next = lax.ppermute(to_n, AXIS, to_next)
        part = local_back(counts, src, dst, w, grad)

        grad_one = call(last_kernel, "last", sds((x.shape[1], 2 * LANES), F32), [SMEM] + [VMEM] * 4, [tab] * 4)(back, got_prev, got_next, part, x)
        lines = 2 * x.shape[1] + 2 * (-(-classes // 8) * 8) + 8
        lines = -(-lines // (8 * num_dev)) * 8 * num_dev
        grad_one, grad_two, mean = call(
            functools.partial(reduce_kernel, num_dev), "reduce", [sds(grad_one.shape, F32), sds((classes, 2 * LANES), F32), sds((1, 1), F32)],
            [VMEM] * 4, [(lines, LANES), (lines, LANES), (lines // 2, LANES), (num_dev // 2 - 1, lines // num_dev, LANES), dma((2, num_dev))],
            collective=1, vmem=8,
        )(grad_one, grad_two, loss, count)
        return mean.reshape(()), grad_one, grad_two.T

    row = P(AXIS)
    return jax.shard_map(
        step, mesh=mesh, in_specs=(row, P(), P(), row, row, row, row, row, row), out_specs=(P(), P(), P()), check_vma=False
    )
```

profile of v0, /device:TPU:0, one launch (start us, length us, event | category | flops | bytes accessed | tf_op | source)
XLA Modules:
  0.0 137.4 jit_solution(5817734348149472737)
XLA Ops:
  0.6 0.0 copy-start.2
  0.6 0.0 copy-start.1
  0.7 0.0 copy-start.5
  0.7 0.0 copy-start.6
  0.7 0.8 copy-done.6
  1.5 0.0 copy-start.7
  1.5 0.8 copy-done.7
  2.2 0.0 copy-start.8
  2.2 0.8 copy-done.8
  3.0 4.6 %prep.1 = (s32[72,128]{1,0:T(8,128)S(1)}, s32[72,128]{1,0:T(8,128)S(1)}, f32[9216,128]{1,0:T(8,128)S(1)}, s32[2]{0:T(128)S(1)}) custom-call(s32[64,128]{1,0:T(8,128)S(1)} %bitcast.33, s32[64,128]{1,0:T(8,128)S(1)} %bitcast.34, f32[64,128]{1,0:T(8,128)S(1)} %bitcast.35), custom_call_target="tpu_custom_call" | custom-call | flops 1000000000 | bytes 8388608 | tf_op jit(solution)/shard_map/prep/pallas_call | solution.py:545
  7.6 0.0 copy-done.2
  7.6 0.0 copy-done.1
  7.6 0.0 copy-done.5
  7.6 4.1 %first.1 = (f32[4096,128]{1,0:T(8,128)S(1)}, bf16[1024,256]{1,0:T(8,128)(2,1)S(1)}, bf16[1024,256]{1,0:T(8,128)(2,1)S(1)}) custom-call(bf16[2048,128]{1,0:T(8,128)(2,1)S(1)} %copy-done.1, f32[128,256]{1,0:T(8,128)S(1)} %copy-done.5, s32[2,1024]{1,0:T(2,128)S(1)} %copy-done.2, s32[2]{0:T(128)S(1)} %get-tuple-element.26.after.counts), custom_call_target="tpu_custom_call" | custom-call | flops 1000000000 | bytes 8388608 | tf_op jit(solution)/shard_map/first/pallas_call | solution.py:552
  11.8 0.8 collective-permute-start
  12.6 3.9 %collective-permute-start.1 = (bf16[1024,256]{1,0:T(8,128)(2,1)S(1)}, bf16[1024,256]{1,0:T(8,128)(2,1)S(1)}, u32[]{:S(2)}, u32[]{:S(2)}) collective-permute-start(bf16[1024,256]{1,0:T(8,128)(2,1)S(1)} %get-tuple-element.31), channel_id=1, source_target_pairs={{0,15},{1,0},{2,1},{3,2},{4,3},{5,4},{6,5},{7,6},{8,7},{9,8},{10,9... | collective-permute-start | bytes 1572872 | tf_op jit(solution)/shard_map/ppermute | solution.py:554
  16.5 0.0 copy-start.3
  16.5 4.7 %local_edges.4.part.after = f32[4096,128]{1,0:T(8,128)S(1)} custom-call(s32[2]{0:T(128)S(1)} %get-tuple-element.26.after.counts, s32[9216]{0:T(1024)S(1)} %bitcast.13, s32[9216]{0:T(1024)S(1)} %bitcast.20, f32[9216,128]{1,0:T(8,128)S(1)} %get-tuple-element.29.w, f32[4096,128]{1,0:T(8,128)S(1)} %get-tuple-element.32.table), custom_call_target="tpu_custom_call" | custom-call | flops 10000000000 | bytes 8388608 | tf_op jit(solution)/shard_map/local_edges/pallas_call | solution.py:563
  21.2 0.0 copy-start
  21.2 0.0 copy-done.3
  21.2 11.6 %count.1 = f32[8,128]{1,0:T(8,128)S(1)} custom-call(s32[16,128]{1,0:T(8,128)S(1)} %bitcast.30, f32[4096,128]{1,0:T(8,128)S(1)} %local_edges.4.part.after), custom_call_target="tpu_custom_call" | custom-call | flops 1000000000 | bytes 8388608 | tf_op jit(solution)/shard_map/count/pallas_call | solution.py:564
  32.9 0.0 collective-permute-done.from_prev
  32.9 0.0 collective-permute-done.1.from_next
  32.9 0.0 copy-done
  32.9 6.5 %hidden.1 = (bf16[2048,256]{1,0:T(8,128)(2,1)S(1)}, f32[4096,128]{1,0:T(8,128)S(1)}, bf16[1536,128]{1,0:T(8,128)(2,1)S(1)}, bf16[1536,128]{1,0:T(8,128)(2,1)S(1)}, s32[16,128]{1,0:T(8,128)S(1)}) custom-call(s32[2]{0:T(128)S(1)} %get-tuple-element.26.after.counts, s32[9216]{0:T(1024)S(1)} %bitcast.14, s32[9216]{0:T(1024)S(1)} %bitcast.21, ...), custom_call_target="tpu_custom_call" | custom-call | flops 1000000000 | bytes 8388608 | tf_op jit(solution)/shard_map/hidden/pallas_call | solution.py:568
  39.4 0.5 collective-permute-start.2
  39.9 3.1 %collective-permute-start.3 = (bf16[1536,128]{1,0:T(8,128)(2,1)S(1)}, bf16[1536,128]{1,0:T(8,128)(2,1)S(1)}, u32[]{:S(2)}, u32[]{:S(2)}) collective-permute-start(bf16[1536,128]{1,0:T(8,128)(2,1)S(1)} %get-tuple-element.35), channel_id=1, source_target_pairs={{0,15},{1,0},{2,1},{3,2},{4,3},{5,4},{6,5},{7,6},{8,7},{9,8},{10,9... | collective-permute-start | bytes 1179656 | tf_op jit(solution)/shard_map/ppermute | solution.py:573
  43.0 0.0 copy-start.4
  43.0 4.7 %local_edges.5.part = f32[4096,128]{1,0:T(8,128)S(1)} custom-call(s32[2]{0:T(128)S(1)} %get-tuple-element.26.after.counts, s32[9216]{0:T(1024)S(1)} %bitcast.15, s32[9216]{0:T(1024)S(1)} %bitcast.22, f32[9216,128]{1,0:T(8,128)S(1)} %get-tuple-element.29.w, f32[4096,128]{1,0:T(8,128)S(1)} %get-tuple-element.36.table), custom_call_target="tpu_custom_call" | custom-call | flops 10000000000 | bytes 8388608 | tf_op jit(solution)/shard_map/local_edges/pallas_call | solution.py:575
  47.7 3.5 %collective-permute-done.2.from_prev = bf16[1536,128]{1,0:T(8,128)(2,1)S(1)} collective-permute-done((bf16[1536,128]{1,0:T(8,128)(2,1)S(1)}, bf16[1536,128]{1,0:T(8,128)(2,1)S(1)}, u32[]{:S(2)}, u32[]{:S(2)}) %collective-permute-start.2) | collective-permute-done | bytes 393248 | tf_op jit(solution)/shard_map/ppermute | solution.py:572
  51.2 0.0 collective-permute-done.3.from_next
  51.2 0.0 copy-done.4
  51.2 5.9 %loss.1 = (f32[8,128]{1,0:T(8,128)S(1)}, f32[4096,128]{1,0:T(8,128)S(1)}, f32[1536,128]{1,0:T(8,128)S(1)}, f32[1536,128]{1,0:T(8,128)S(1)}) custom-call(s32[2]{0:T(128)S(1)} %get-tuple-element.26.after.counts, s32[9216]{0:T(1024)S(1)} %bitcast.16, s32[9216]{0:T(1024)S(1)} %bitcast.23, f32[9216,128]{1,0:T(8,128)S(1)} %get-tuple-element.29.w, ...), custom_call_target="tpu_custom_call" | custom-call | flops 1000000000 | bytes 8388608 | tf_op jit(solution)/shard_map/loss/pallas_call | solution.py:576
  57.1 4.3 %collective-permute-start.4 = (f32[1536,128]{1,0:T(8,128)S(1)}, f32[1536,128]{1,0:T(8,128)S(1)}, u32[]{:S(2)}, u32[]{:S(2)}) collective-permute-start(f32[1536,128]{1,0:T(8,128)S(1)} %get-tuple-element.37), channel_id=1, source_target_pairs={{0,15},{1,0},{2,1},{3,2},{4,3},{5,4},{6,5},{7,6},{8,7},{9,8},{10,9... | collective-permute-start | bytes 2359304 | tf_op jit(solution)/shard_map/ppermute | solution.py:580
  61.4 0.0 collective-permute-start.5
  61.4 4.7 %local_edges.6.part = f32[4096,128]{1,0:T(8,128)S(1)} custom-call(s32[2]{0:T(128)S(1)} %get-tuple-element.26.after.counts, s32[9216]{0:T(1024)S(1)} %bitcast.17, s32[9216]{0:T(1024)S(1)} %bitcast.24, f32[9216,128]{1,0:T(8,128)S(1)} %get-tuple-element.29.w, f32[4096,128]{1,0:T(8,128)S(1)} %get-tuple-element.39.table), custom_call_target="tpu_custom_call" | custom-call | flops 10000000000 | bytes 8388608 | tf_op jit(solution)/shard_map/local_edges/pallas_call | solution.py:582
  66.1 13.0 %collective-permute-done.4.got_prev = f32[1536,128]{1,0:T(8,128)S(1)} collective-permute-done((f32[1536,128]{1,0:T(8,128)S(1)}, f32[1536,128]{1,0:T(8,128)S(1)}, u32[]{:S(2)}, u32[]{:S(2)}) %collective-permute-start.4) | collective-permute-done | bytes 786464 | tf_op jit(solution)/shard_map/ppermute | solution.py:580
  79.0 1.6 %collective-permute-done.5.got_next = f32[1536,128]{1,0:T(8,128)S(1)} collective-permute-done((f32[1536,128]{1,0:T(8,128)S(1)}, f32[1536,128]{1,0:T(8,128)S(1)}, u32[]{:S(2)}, u32[]{:S(2)}) %collective-permute-start.5) | collective-permute-done | bytes 786464 | tf_op jit(solution)/shard_map/ppermute | solution.py:581
  80.6 8.1 %middle.1 = (f32[256,256]{1,0:T(8,128)S(1)}, f32[4096,128]{1,0:T(8,128)S(1)}, f32[2048,128]{1,0:T(8,128)S(1)}, f32[2048,128]{1,0:T(8,128)S(1)}) custom-call(s32[2]{0:T(128)S(1)} %get-tuple-element.26.after.counts, s32[9216]{0:T(1024)S(1)} %bitcast.18, s32[9216]{0:T(1024)S(1)} %bitcast.25, f32[9216,128]{1,0:T(8,128)S(1)} %get-tuple-element.29.w, ...), custom_call_target="tpu_custom_call" | custom-call | flops 1000000000 | bytes 8388608 | tf_op jit(solution)/shard_map/middle/pallas_call | solution.py:583
  88.7 2.8 %collective-permute-start.6 = (f32[2048,128]{1,0:T(8,128)S(1)}, f32[2048,128]{1,0:T(8,128)S(1)}, u32[]{:S(2)}, u32[]{:S(2)}) collective-permute-start(f32[2048,128]{1,0:T(8,128)S(1)} %get-tuple-element.41), channel_id=1, source_target_pairs={{0,15},{1,0},{2,1},{3,2},{4,3},{5,4},{6,5},{7,6},{8,7},{9,8},{10,9... | collective-permute-start | bytes 3145736 | tf_op jit(solution)/shard_map/ppermute | solution.py:587
  91.5 0.0 collective-permute-start.7
  91.5 4.7 %local_edges.7.part = f32[4096,128]{1,0:T(8,128)S(1)} custom-call(s32[2]{0:T(128)S(1)} %get-tuple-element.26.after.counts, s32[9216]{0:T(1024)S(1)} %bitcast.19, s32[9216]{0:T(1024)S(1)} %bitcast.26, f32[9216,128]{1,0:T(8,128)S(1)} %get-tuple-element.29.w, f32[4096,128]{1,0:T(8,128)S(1)} %get-tuple-element.43.table), custom_call_target="tpu_custom_call" | custom-call | flops 10000000000 | bytes 8388608 | tf_op jit(solution)/shard_map/local_edges/pallas_call | solution.py:589
  96.2 17.4 %collective-permute-done.6.got_prev = f32[2048,128]{1,0:T(8,128)S(1)} collective-permute-done((f32[2048,128]{1,0:T(8,128)S(1)}, f32[2048,128]{1,0:T(8,128)S(1)}, u32[]{:S(2)}, u32[]{:S(2)}) %collective-permute-start.6) | collective-permute-done | bytes 1048608 | tf_op jit(solution)/shard_map/ppermute | solution.py:587
  113.7 1.0 collective-permute-done.7.got_next
  114.7 5.6 %last.1.one = f32[128,256]{1,0:T(8,128)S(1)} custom-call(s32[2048]{0:T(1024)S(1)} %bitcast.29, f32[2048,128]{1,0:T(8,128)S(1)} %collective-permute-done.6.got_prev, f32[2048,128]{1,0:T(8,128)S(1)} %collective-permute-done.7.got_next, f32[4096,128]{1,0:T(8,128)S(1)} %local_edges.7.part, bf16[2048,128]{1,0:T(8,128)(2,1)S(1)} %copy-done.1), custom_call_target="tpu_custom_call" | custom-call | flops 1000000000 | bytes 8388608 | tf_op jit(solution)/shard_map/last/pallas_call | solution.py:591
  120.2 14.1 %reduce.1 = (f32[128,256]{1,0:T(8,128)S(1)}, f32[172,256]{1,0:T(8,128)S(1)}, f32[1,1]{1,0:T(1,128)}) custom-call(f32[128,256]{1,0:T(8,128)S(1)} %last.1.one, f32[256,256]{1,0:T(8,128)S(1)} %get-tuple-element.44.two, f32[8,128]{1,0:T(8,128)S(1)} %get-tuple-element.45.loss, f32[8,128]{1,0:T(8,128)S(1)} %count.1), custom_call_target="tpu_custom_call" | custom-call | flops 1000000000 | bytes 8388608 | tf_op jit(solution)/shard_map/reduce/pallas_call | solution.py:594
  135.0 0.7 copy.16
  135.6 0.7 copy.17
Async XLA Ops:
  0.6 7.0 %copy-start.2 = (s32[2,1024]{1,0:T(2,128)S(1)}, s32[2,1024]{1,0:T(2,128)}, u32[]{:S(2)}) copy-start(s32[2,1024]{1,0:T(2,128)} %send.3) | copy-start | bytes 24580
  0.6 7.0 %copy-start.1 = (bf16[2048,128]{1,0:T(8,128)(2,1)S(1)}, bf16[2048,128]{1,0:T(8,128)(2,1)}, u32[]{:S(2)}) copy-start(bf16[2048,128]{1,0:T(8,128)(2,1)} %x.3) | copy-start | bytes 1572868
  0.7 7.0 %copy-start.5 = (f32[128,256]{1,0:T(8,128)S(1)}, f32[128,256]{1,0:T(8,128)}, u32[]{:S(2)}) copy-start(f32[128,256]{1,0:T(8,128)} %w1.1) | copy-start | bytes 393220
  0.7 0.8 copy-start.6
  1.5 0.8 copy-start.7
  2.2 0.8 copy-start.8
  11.8 21.1 %collective-permute-start = (bf16[1024,256]{1,0:T(8,128)(2,1)S(1)}, bf16[1024,256]{1,0:T(8,128)(2,1)S(1)}, u32[]{:S(2)}, u32[]{:S(2)}) collective-permute-start(bf16[1024,256]{1,0:T(8,128)(2,1)S(1)} %get-tuple-element.30), channel_id=1, source_target_pairs={{0,1},{1,2},{2,3},{3,4},{4,5},{5,6},{6,7},{7,8},{8,9},{9,10},{10,1... | collective-permute-start | bytes 1572872 | tf_op jit(solution)/shard_map/ppermute | solution.py:553
  12.6 20.3 %collective-permute-start.1 = (bf16[1024,256]{1,0:T(8,128)(2,1)S(1)}, bf16[1024,256]{1,0:T(8,128)(2,1)S(1)}, u32[]{:S(2)}, u32[]{:S(2)}) collective-permute-start(bf16[1024,256]{1,0:T(8,128)(2,1)S(1)} %get-tuple-element.31), channel_id=1, source_target_pairs={{0,15},{1,0},{2,1},{3,2},{4,3},{5,4},{6,5},{7,6},{8,7},{9,8},{10,9... | collective-permute-start | bytes 1572872 | tf_op jit(solution)/shard_map/ppermute | solution.py:554
  16.5 4.7 %copy-start.3 = (s32[2048]{0:T(1024)S(1)}, s32[2048]{0:T(1024)}, u32[]{:S(2)}) copy-start(s32[2048]{0:T(1024)} %param.17) | copy-start | bytes 24580
  21.2 11.7 %copy-start = (f32[256,172]{0,1:T(8,128)S(1)}, f32[256,172]{0,1:T(8,128)}, u32[]{:S(2)}) copy-start(f32[256,172]{0,1:T(8,128)} %param.11) | copy-start | bytes 528388
  39.4 11.8 %collective-permute-start.2 = (bf16[1536,128]{1,0:T(8,128)(2,1)S(1)}, bf16[1536,128]{1,0:T(8,128)(2,1)S(1)}, u32[]{:S(2)}, u32[]{:S(2)}) collective-permute-start(bf16[1536,128]{1,0:T(8,128)(2,1)S(1)} %get-tuple-element.34), channel_id=1, source_target_pairs={{0,1},{1,2},{2,3},{3,4},{4,5},{5,6},{6,7},{7,8},{8,9},{9,10},{10,1... | collective-permute-start | bytes 1179656 | tf_op jit(solution)/shard_map/ppermute | solution.py:572
  39.9 11.4 %collective-permute-start.3 = (bf16[1536,128]{1,0:T(8,128)(2,1)S(1)}, bf16[1536,128]{1,0:T(8,128)(2,1)S(1)}, u32[]{:S(2)}, u32[]{:S(2)}) collective-permute-start(bf16[1536,128]{1,0:T(8,128)(2,1)S(1)} %get-tuple-element.35), channel_id=1, source_target_pairs={{0,15},{1,0},{2,1},{3,2},{4,3},{5,4},{6,5},{7,6},{8,7},{9,8},{10,9... | collective-permute-start | bytes 1179656 | tf_op jit(solution)/shard_map/ppermute | solution.py:573
  43.0 8.2 %copy-start.4 = (s32[2048]{0:T(1024)S(1)}, s32[2048]{0:T(1024)}, u32[]{:S(2)}) copy-start(s32[2048]{0:T(1024)} %param.16) | copy-start | bytes 24580
  57.1 21.9 %collective-permute-start.4 = (f32[1536,128]{1,0:T(8,128)S(1)}, f32[1536,128]{1,0:T(8,128)S(1)}, u32[]{:S(2)}, u32[]{:S(2)}) collective-permute-start(f32[1536,128]{1,0:T(8,128)S(1)} %get-tuple-element.37), channel_id=1, source_target_pairs={{0,15},{1,0},{2,1},{3,2},{4,3},{5,4},{6,5},{7,6},{8,7},{9,8},{10,9... | collective-permute-start | bytes 2359304 | tf_op jit(solution)/shard_map/ppermute | solution.py:580
  61.4 19.2 %collective-permute-start.5 = (f32[1536,128]{1,0:T(8,128)S(1)}, f32[1536,128]{1,0:T(8,128)S(1)}, u32[]{:S(2)}, u32[]{:S(2)}) collective-permute-start(f32[1536,128]{1,0:T(8,128)S(1)} %get-tuple-element.38), channel_id=1, source_target_pairs={{0,1},{1,2},{2,3},{3,4},{4,5},{5,6},{6,7},{7,8},{8,9},{9,10},{10,1... | collective-permute-start | bytes 2359304 | tf_op jit(solution)/shard_map/ppermute | solution.py:581
  88.7 24.9 %collective-permute-start.6 = (f32[2048,128]{1,0:T(8,128)S(1)}, f32[2048,128]{1,0:T(8,128)S(1)}, u32[]{:S(2)}, u32[]{:S(2)}) collective-permute-start(f32[2048,128]{1,0:T(8,128)S(1)} %get-tuple-element.41), channel_id=1, source_target_pairs={{0,15},{1,0},{2,1},{3,2},{4,3},{5,4},{6,5},{7,6},{8,7},{9,8},{10,9... | collective-permute-start | bytes 3145736 | tf_op jit(solution)/shard_map/ppermute | solution.py:587
  91.5 23.2 %collective-permute-start.7 = (f32[2048,128]{1,0:T(8,128)S(1)}, f32[2048,128]{1,0:T(8,128)S(1)}, u32[]{:S(2)}, u32[]{:S(2)}) collective-permute-start(f32[2048,128]{1,0:T(8,128)S(1)} %get-tuple-element.42), channel_id=1, source_target_pairs={{0,1},{1,2},{2,3},{3,4},{4,5},{5,6},{6,7},{7,8},{8,9},{9,10},{10,1... | collective-permute-start | bytes 3145736 | tf_op jit(solution)/shard_map/ppermute | solution.py:588
where the time goes:
time: 139 us; the launch traced here: 137 us
  Pallas kernels  79.2 us (57%)
  waiting for transfers between devices  36.5 us (26%)
  starting transfers between devices  15.5 us (11%)
  local copies, waits for them, and re-layouts  3.68 us (3%)
  between operations  2.58 us (2%)
    ppermute x2, waiting for transfers between devices, step(): got_prev = lax.ppermute(to_p, AXIS, to_prev)  30.4 us
    pallas_call x1, Pallas kernels, step(): call(functools.partial(reduce_kernel, num_dev), 'reduce', [sds(grad_one.s...  14.1 us
    pallas_call x1, Pallas kernels, step(): call(functools.partial(count_kernel, num_dev), 'count', one, [VMEM, ANY],...  11.6 us
    pallas_call x2, Pallas kernels, step(): part = local_back(counts, src, dst, w, grad)  9.37 us
    pallas_call x1, Pallas kernels, step(): call(functools.partial(middle_kernel, chunk_h), 'middle', [sds((2 * LANES...  8.08 us
    ppermute x2, starting transfers between devices, step(): got_prev = lax.ppermute(to_p, AXIS, to_prev)  7.1 us
    ppermute x2, starting transfers between devices, step(): from_next = lax.ppermute(to_p, AXIS, to_prev)  7.07 us
    pallas_call x1, Pallas kernels, step(): call(functools.partial(hidden_kernel, chunk_h), 'hidden', [sds((rows, 2 *...  6.51 us
  transfers between devices with their start and end apart: 8, of which 5 were waited for; matrix products, arithmetic and copies ran while one was open for 0% of the time, Pallas kernels for 22%

commit v1 on v0

--- a/solution.py
+++ b/solution.py
@@ -236,19 +236,6 @@
     for c in fetch:
         c.wait()
     gather_rows(send, idx, tab_b, tab, buf, to_prev, to_next)
-
-
-def count_kernel(n, mask, after, count, mine, theirs, send_sem, recv_sem):
-    me, met = greet(n)
-    mine[...] = jnp.sum(mask[...].astype(F32).reshape(-1, 8, LANES), axis=0)
-    met()
-    copies = [remote(mine, theirs.at[o - 1], send_sem.at[o - 1], recv_sem.at[o - 1], lax.rem(me + o, n)) for o in range(1, n)]
-    for c in copies:
-        c.start()
-    for c in copies:
-        c.wait()
-    every = jnp.sum(mine[...] + jnp.sum(theirs[...], axis=0), keepdims=True)
-    count[...] = jnp.maximum(jnp.broadcast_to(every, count.shape), 1.0)
 
 
 def reduce_kernel(n, one, two, loss, count, one_out, two_out, mean, work, full, got_pair, got_rest, sems):
@@ -308,11 +295,15 @@
     mean[...] = jnp.sum(full[tail : tail + 8, :], keepdims=True) / count[0:1, 0:1]
 
 
-def prep_kernel(chunk, rows, src, dst, w, src_out, dst_out, w_out, counts, total):
-    lines = src.shape[0]
+def prep_kernel(n, chunk, rows, packed, mask, src_out, dst_out, w_out, counts, count, total, mine, theirs, send_sem, recv_sem):
+    me, met = greet(n)
+    mine[...] = jnp.sum(mask[...].astype(F32).reshape(-1, 8, LANES), axis=0)
+    lines = packed.shape[0] // 2
     slots = src_out.shape[0]
-    live = w[...] != 0.0
-    halo = src[...] >= rows
+    both = packed[:lines, :].astype(jnp.int32)
+    src, d, w = both >> 11, both & 2047, packed[lines:, :]
+    live = w != 0.0
+    halo = src >= rows
     at = lambda shape, axis: lax.broadcasted_iota(jnp.int32, shape, axis)
     before = (at((LANES, LANES), 0) < at((LANES, LANES), 1)).astype(BF16)
     above = (at((lines, lines), 1) < at((lines, lines), 0)).astype(BF16)
@@ -332,14 +323,17 @@
         is_local, rank(is_local).astype(jnp.int32), jnp.where(is_halo, rank(is_halo).astype(jnp.int32) + local_chunks * chunk, -1)
     )
     line, lane = pos >> 7, pos & (LANES - 1)
-    s = jnp.where(halo, src[...] - rows, src[...])
-    d = dst[...]
-    half_w = w[...] * 0.5
+    s = jnp.where(halo, src - rows, src)
+    half_w = w * 0.5
     w_a = half_w.astype(BF16).astype(F32)
     w_b = (half_w - w_a).astype(BF16).astype(F32)
     w_c = half_w - w_a - w_b
     high = ((s >> 8) * 8 + (d >> 8)).astype(F32)
     planes = [(s & 255).astype(F32), (d & 255).astype(F32), high, w_a, w_b, w_c]
+    met()
+    copies = [remote(mine, theirs.at[o - 1], send_sem.at[o - 1], recv_sem.at[o - 1], lax.rem(me + o, n)) for o in range(1, n)]
+    for c in copies:
+        c.start()
     acc = jnp.zeros((len(planes) * slots, LANES), F32)
     for r in range(0, lines, 2):
         lhs, rhs = [], []
@@ -359,6 +353,11 @@
     def _(r):
         for q in range(8):
             w_out[pl.ds(pl.multiple_of((r * 8 + q) * LANES, LANES), LANES), :] = spread(total[pl.ds(r * 8 + q, 1), :])
+
+    for c in copies:
+        c.wait()
+    every = jnp.sum(mine[...] + jnp.sum(theirs[...], axis=0), keepdims=True)
+    count[...] = jnp.maximum(jnp.broadcast_to(every, count.shape), 1.0)
 
 
 def local_kernel(chunk, backward, counts, src, dst, w, table, out, src_s, dst_s, sems, *accs):
@@ -540,12 +539,13 @@
         w2_pad = (2 * LANES, 2 * LANES)
         mask = mask.reshape(-1, LANES)
 
-        lined = lambda a: a.reshape(lines, LANES)
+        packed = jnp.concatenate([(edge_src * 2048 + edge_dst).astype(F32), edge_w]).reshape(2 * lines, LANES)
         ints = sds((slots, LANES), jnp.int32)
-        src, dst, w, counts = call(
-            functools.partial(prep_kernel, PREP_CHUNK, rows), "prep", [ints, ints, sds((slots * LANES, LANES), F32), sds((2,), jnp.int32)], [VMEM] * 3,
-            [(6 * slots, LANES)], out_specs=[VMEM] * 3 + [SMEM], vmem=8,
-        )(lined(edge_src), lined(edge_dst), lined(edge_w))
+        src, dst, w, counts, count = call(
+            functools.partial(prep_kernel, num_dev, PREP_CHUNK, rows), "prep", [ints, ints, sds((slots * LANES, LANES), F32), sds((2,), jnp.int32), one], [VMEM] * 2,
+            [(6 * slots, LANES), (8, LANES), (num_dev - 1, 8, LANES), dma((num_dev - 1,)), dma((num_dev - 1,))],
+            out_specs=[VMEM] * 3 + [SMEM, VMEM], vmem=8, collective=0,
+        )(packed, mask)
         src, dst = src.reshape(-1), dst.reshape(-1)
 
         list_s = [pltpu.SMEM((halo,), jnp.int32), dma((halo // LANES,))]
@@ -561,10 +561,6 @@
             for back in (False, True)
         )
         part = local(counts, src, dst, w, tab_one)
-        count = call(
-            functools.partial(count_kernel, num_dev), "count", one, [VMEM, ANY],
-            [(8, LANES), (num_dev - 1, 8, LANES), dma((num_dev - 1,)), dma((num_dev - 1,))], vmem=2, collective=0, flops=10**9,
-        )(mask, part)
         hid, tab_two, to_p, to_n, back = call(
             functools.partial(hidden_kernel, chunk_h), "hidden", [sds((rows, 2 * LANES), BF16), tab_f, pack_b, pack_b, sds((2 * halo // LANES, LANES), jnp.int32)],
             walk + [VMEM] * 5, [tab, tab_b, w2_pad, half] + list_s + walk_s + [tab] * 4,

time: 139 us -> 140 us (level)
  waiting for transfers between devices: 36.5 us -> 47.1 us
  Pallas kernels: 79.2 us -> 74.1 us
  starting transfers between devices: 15.5 us -> 11.1 us
  local copies, waits for them, and re-layouts: 3.68 us -> 2.05 us
  other arithmetic: 0 us -> 1.6 us
    ppermute x2, waiting for transfers between devices: 2.6 us -> 9.9 us  [step(): got_next = lax.ppermute(to_n, AXIS, to_next)]
    pallas_call x2 -> x1, Pallas kernels: 16.2 us -> 10.4 us  [step(): call(functools.partial(prep_kernel, num_dev, PREP_CHUNK, rows), 'prep', [...]
    ppermute x2, waiting for transfers between devices: 3.55 us -> 8.07 us  [step(): from_prev = lax.ppermute(to_n, AXIS, to_next)]
    ppermute x2, starting transfers between devices: 7.1 us -> 3.38 us  [step(): got_prev = lax.ppermute(to_p, AXIS, to_prev)]
    unnamed x20 -> x16, local copies, waits for them, and re-layouts: 3.68 us -> 2.05 us
    concatenate x0 -> x2, other arithmetic: none -> 1.6 us  [step(): jnp.concatenate([(edge_src * 2048 + edge_dst).astype(F32), edge_w])]
  transfers between devices with their start and end apart: 8 -> 8, of which waited for: 5 -> 6; matrix products, arithmetic and copies ran while one was open for 0% -> 0% of each run, Pallas kernels for 22% -> 14%
where the time goes in v1:
time: 140 us; the launch traced here: 138 us
  Pallas kernels  74.1 us (53%)
  waiting for transfers between devices  47.1 us (34%)
  starting transfers between devices  11.1 us (8%)
  between operations  2.46 us (2%)
  local copies, waits for them, and re-layouts  2.05 us (1%)
  other arithmetic  1.6 us (1%)
    ppermute x2, waiting for transfers between devices, step(): got_prev = lax.ppermute(to_p, AXIS, to_prev)  29.1 us
    pallas_call x1, Pallas kernels, step(): call(functools.partial(reduce_kernel, num_dev), 'reduce', [sds(grad_one.s...  12.8 us
    pallas_call x1, Pallas kernels, step(): call(functools.partial(prep_kernel, num_dev, PREP_CHUNK, rows), 'prep', [...  10.4 us
    pallas_call x2, Pallas kernels, step(): part = local_back(counts, src, dst, w, grad)  9.99 us
    ppermute x2, waiting for transfers between devices, step(): got_next = lax.ppermute(to_n, AXIS, to_next)  9.9 us
    pallas_call x1, Pallas kernels, step(): call(functools.partial(middle_kernel, chunk_h), 'middle', [sds((2 * LANES...  8.28 us
    ppermute x2, waiting for transfers between devices, step(): from_prev = lax.ppermute(to_n, AXIS, to_next)  8.07 us
    pallas_call x1, Pallas kernels, step(): call(functools.partial(hidden_kernel, chunk_h), 'hidden', [sds((rows, 2 *...  6.7 us
  transfers between devices with their start and end apart: 8, of which 6 were waited for; matrix products, arithmetic and copies ran while one was open for 0% of the time, Pallas kernels for 14%

profile of v1, /device:TPU:0, one launch (start us, length us, event | category | flops | bytes accessed | tf_op | source)
XLA Modules:
  0.0 138.3 jit_solution(2382875208076964036)
XLA Ops:
  0.6 0.0 copy-start.2
  0.6 0.0 copy-start.1
  0.7 0.8 convert_bitcast_fusion
  1.5 0.8 pad_maximum_fusion.packed
  2.3 0.0 copy-start.3
  2.3 0.7 copy-done.3
  3.0 0.0 copy-start.6
  3.0 10.4 %prep.1 = (s32[72,128]{1,0:T(8,128)S(1)}, s32[72,128]{1,0:T(8,128)S(1)}, f32[9216,128]{1,0:T(8,128)S(1)}, s32[2]{0:T(128)S(1)}, f32[8,128]{1,0:T(8,128)S(1)}) custom-call(f32[128,128]{1,0:T(8,128)S(1)} %pad_maximum_fusion.packed, s32[16,128]{1,0:T(8,128)S(1)} %bitcast.30), custom_call_target="tpu_custom_call" | custom-call | flops 1000000000 | bytes 8388608 | tf_op jit(solution)/shard_map/prep/pallas_call | solution.py:544
  13.3 0.0 copy-done.2
  13.3 0.0 copy-done.1
  13.3 0.0 copy-done.6
  13.3 4.1 %first.1 = (f32[4096,128]{1,0:T(8,128)S(1)}, bf16[1024,256]{1,0:T(8,128)(2,1)S(1)}, bf16[1024,256]{1,0:T(8,128)(2,1)S(1)}) custom-call(bf16[2048,128]{1,0:T(8,128)(2,1)S(1)} %copy-done.1, f32[128,256]{1,0:T(8,128)S(1)} %copy-done.6, s32[2,1024]{1,0:T(2,128)S(1)} %copy-done.2, s32[2]{0:T(128)S(1)} %get-tuple-element.27.after.counts), custom_call_target="tpu_custom_call" | custom-call | flops 1000000000 | bytes 8388608 | tf_op jit(solution)/shard_map/first/pallas_call | solution.py:552
  17.5 0.1 collective-permute-start
  17.6 3.5 %collective-permute-start.1 = (bf16[1024,256]{1,0:T(8,128)(2,1)S(1)}, bf16[1024,256]{1,0:T(8,128)(2,1)S(1)}, u32[]{:S(2)}, u32[]{:S(2)}) collective-permute-start(bf16[1024,256]{1,0:T(8,128)(2,1)S(1)} %get-tuple-element.32), channel_id=1, source_target_pairs={{0,15},{1,0},{2,1},{3,2},{4,3},{5,4},{6,5},{7,6},{8,7},{9,8},{10,9... | collective-permute-start | bytes 1572872 | tf_op jit(solution)/shard_map/ppermute | solution.py:554
  21.1 0.0 copy-start
  21.1 5.0 %local_edges.4.part = f32[4096,128]{1,0:T(8,128)S(1)} custom-call(s32[2]{0:T(128)S(1)} %get-tuple-element.27.after.counts, s32[9216]{0:T(1024)S(1)} %bitcast.13, s32[9216]{0:T(1024)S(1)} %bitcast.20, f32[9216,128]{1,0:T(8,128)S(1)} %get-tuple-element.30.w, f32[4096,128]{1,0:T(8,128)S(1)} %get-tuple-element.33.table), custom_call_target="tpu_custom_call" | custom-call | flops 10000000000 | bytes 8388608 | tf_op jit(solution)/shard_map/local_edges/pallas_call | solution.py:563
  26.1 5.7 %collective-permute-done.from_prev = bf16[1024,256]{1,0:T(8,128)(2,1)S(1)} collective-permute-done((bf16[1024,256]{1,0:T(8,128)(2,1)S(1)}, bf16[1024,256]{1,0:T(8,128)(2,1)S(1)}, u32[]{:S(2)}, u32[]{:S(2)}) %collective-permute-start) | collective-permute-done | bytes 524320 | tf_op jit(solution)/shard_map/ppermute | solution.py:553
  31.8 0.0 collective-permute-done.1.from_next
  31.8 0.0 copy-done
  31.8 6.7 %hidden.1 = (bf16[2048,256]{1,0:T(8,128)(2,1)S(1)}, f32[4096,128]{1,0:T(8,128)S(1)}, bf16[1536,128]{1,0:T(8,128)(2,1)S(1)}, bf16[1536,128]{1,0:T(8,128)(2,1)S(1)}, s32[16,128]{1,0:T(8,128)S(1)}) custom-call(s32[2]{0:T(128)S(1)} %get-tuple-element.27.after.counts, s32[9216]{0:T(1024)S(1)} %bitcast.14, s32[9216]{0:T(1024)S(1)} %bitcast.21, ...), custom_call_target="tpu_custom_call" | custom-call | flops 1000000000 | bytes 8388608 | tf_op jit(solution)/shard_map/hidden/pallas_call | solution.py:564
  38.5 0.9 collective-permute-start.2
  39.4 2.7 %collective-permute-start.3 = (bf16[1536,128]{1,0:T(8,128)(2,1)S(1)}, bf16[1536,128]{1,0:T(8,128)(2,1)S(1)}, u32[]{:S(2)}, u32[]{:S(2)}) collective-permute-start(bf16[1536,128]{1,0:T(8,128)(2,1)S(1)} %get-tuple-element.37), channel_id=1, source_target_pairs={{0,15},{1,0},{2,1},{3,2},{4,3},{5,4},{6,5},{7,6},{8,7},{9,8},{10,9... | collective-permute-start | bytes 1179656 | tf_op jit(solution)/shard_map/ppermute | solution.py:569
  42.1 0.0 copy-start.4
  42.1 0.0 copy-start.5
  42.1 5.0 %local_edges.5.part = f32[4096,128]{1,0:T(8,128)S(1)} custom-call(s32[2]{0:T(128)S(1)} %get-tuple-element.27.after.counts, s32[9216]{0:T(1024)S(1)} %bitcast.15, s32[9216]{0:T(1024)S(1)} %bitcast.22, f32[9216,128]{1,0:T(8,128)S(1)} %get-tuple-element.30.w, f32[4096,128]{1,0:T(8,128)S(1)} %get-tuple-element.38.table), custom_call_target="tpu_custom_call" | custom-call | flops 10000000000 | bytes 8388608 | tf_op jit(solution)/shard_map/local_edges/pallas_call | solution.py:571
  47.1 2.3 %collective-permute-done.2.from_prev = bf16[1536,128]{1,0:T(8,128)(2,1)S(1)} collective-permute-done((bf16[1536,128]{1,0:T(8,128)(2,1)S(1)}, bf16[1536,128]{1,0:T(8,128)(2,1)S(1)}, u32[]{:S(2)}, u32[]{:S(2)}) %collective-permute-start.2) | collective-permute-done | bytes 393248 | tf_op jit(solution)/shard_map/ppermute | solution.py:568
  49.5 0.0 collective-permute-done.3.from_next
  49.5 0.0 copy-done.4
  49.5 0.0 copy-done.5
  49.5 6.3 %loss.1 = (f32[8,128]{1,0:T(8,128)S(1)}, f32[4096,128]{1,0:T(8,128)S(1)}, f32[1536,128]{1,0:T(8,128)S(1)}, f32[1536,128]{1,0:T(8,128)S(1)}) custom-call(s32[2]{0:T(128)S(1)} %get-tuple-element.27.after.counts, s32[9216]{0:T(1024)S(1)} %bitcast.16, s32[9216]{0:T(1024)S(1)} %bitcast.23, f32[9216,128]{1,0:T(8,128)S(1)} %get-tuple-element.30.w, ...), custom_call_target="tpu_custom_call" | custom-call | flops 1000000000 | bytes 8388608 | tf_op jit(solution)/shard_map/loss/pallas_call | solution.py:572
  55.8 3.3 %collective-permute-start.4 = (f32[1536,128]{1,0:T(8,128)S(1)}, f32[1536,128]{1,0:T(8,128)S(1)}, u32[]{:S(2)}, u32[]{:S(2)}) collective-permute-start(f32[1536,128]{1,0:T(8,128)S(1)} %get-tuple-element.39), channel_id=1, source_target_pairs={{0,15},{1,0},{2,1},{3,2},{4,3},{5,4},{6,5},{7,6},{8,7},{9,8},{10,9... | collective-permute-start | bytes 2359304 | tf_op jit(solution)/shard_map/ppermute | solution.py:576
  59.1 0.0 collective-permute-start.5
  59.1 5.0 %local_edges.6.part = f32[4096,128]{1,0:T(8,128)S(1)} custom-call(s32[2]{0:T(128)S(1)} %get-tuple-element.27.after.counts, s32[9216]{0:T(1024)S(1)} %bitcast.17, s32[9216]{0:T(1024)S(1)} %bitcast.24, f32[9216,128]{1,0:T(8,128)S(1)} %get-tuple-element.30.w, f32[4096,128]{1,0:T(8,128)S(1)} %get-tuple-element.41.table), custom_call_target="tpu_custom_call" | custom-call | flops 10000000000 | bytes 8388608 | tf_op jit(solution)/shard_map/local_edges/pallas_call | solution.py:578
  64.1 11.3 %collective-permute-done.4.got_prev = f32[1536,128]{1,0:T(8,128)S(1)} collective-permute-done((f32[1536,128]{1,0:T(8,128)S(1)}, f32[1536,128]{1,0:T(8,128)S(1)}, u32[]{:S(2)}, u32[]{:S(2)}) %collective-permute-start.4) | collective-permute-done | bytes 786464 | tf_op jit(solution)/shard_map/ppermute | solution.py:576
  75.4 7.3 %collective-permute-done.5.got_next = f32[1536,128]{1,0:T(8,128)S(1)} collective-permute-done((f32[1536,128]{1,0:T(8,128)S(1)}, f32[1536,128]{1,0:T(8,128)S(1)}, u32[]{:S(2)}, u32[]{:S(2)}) %collective-permute-start.5) | collective-permute-done | bytes 786464 | tf_op jit(solution)/shard_map/ppermute | solution.py:577
  82.7 8.3 %middle.1 = (f32[256,256]{1,0:T(8,128)S(1)}, f32[4096,128]{1,0:T(8,128)S(1)}, f32[2048,128]{1,0:T(8,128)S(1)}, f32[2048,128]{1,0:T(8,128)S(1)}) custom-call(s32[2]{0:T(128)S(1)} %get-tuple-element.27.after.counts, s32[9216]{0:T(1024)S(1)} %bitcast.18, s32[9216]{0:T(1024)S(1)} %bitcast.25, f32[9216,128]{1,0:T(8,128)S(1)} %get-tuple-element.30.w, ...), custom_call_target="tpu_custom_call" | custom-call | flops 1000000000 | bytes 8388608 | tf_op jit(solution)/shard_map/middle/pallas_call | solution.py:579
  91.0 0.1 collective-permute-start.6
  91.0 0.5 collective-permute-start.7
  91.5 5.0 %local_edges.7.part = f32[4096,128]{1,0:T(8,128)S(1)} custom-call(s32[2]{0:T(128)S(1)} %get-tuple-element.27.after.counts, s32[9216]{0:T(1024)S(1)} %bitcast.19, s32[9216]{0:T(1024)S(1)} %bitcast.26, f32[9216,128]{1,0:T(8,128)S(1)} %get-tuple-element.30.w, f32[4096,128]{1,0:T(8,128)S(1)} %get-tuple-element.45.table), custom_call_target="tpu_custom_call" | custom-call | flops 10000000000 | bytes 8388608 | tf_op jit(solution)/shard_map/local_edges/pallas_call | solution.py:585
  96.5 17.8 %collective-permute-done.6.got_prev = f32[2048,128]{1,0:T(8,128)S(1)} collective-permute-done((f32[2048,128]{1,0:T(8,128)S(1)}, f32[2048,128]{1,0:T(8,128)S(1)}, u32[]{:S(2)}, u32[]{:S(2)}) %collective-permute-start.6) | collective-permute-done | bytes 1048608 | tf_op jit(solution)/shard_map/ppermute | solution.py:583
  114.4 2.6 %collective-permute-done.7.got_next = f32[2048,128]{1,0:T(8,128)S(1)} collective-permute-done((f32[2048,128]{1,0:T(8,128)S(1)}, f32[2048,128]{1,0:T(8,128)S(1)}, u32[]{:S(2)}, u32[]{:S(2)}) %collective-permute-start.7) | collective-permute-done | bytes 1048608 | tf_op jit(solution)/shard_map/ppermute | solution.py:584
  117.0 5.6 %last.1.one = f32[128,256]{1,0:T(8,128)S(1)} custom-call(s32[2048]{0:T(1024)S(1)} %bitcast.29, f32[2048,128]{1,0:T(8,128)S(1)} %collective-permute-done.6.got_prev, f32[2048,128]{1,0:T(8,128)S(1)} %collective-permute-done.7.got_next, f32[4096,128]{1,0:T(8,128)S(1)} %local_edges.7.part, bf16[2048,128]{1,0:T(8,128)(2,1)S(1)} %copy-done.1), custom_call_target="tpu_custom_call" | custom-call | flops 1000000000 | bytes 8388608 | tf_op jit(solution)/shard_map/last/pallas_call | solution.py:587
  122.5 12.8 %reduce.1 = (f32[128,256]{1,0:T(8,128)S(1)}, f32[172,256]{1,0:T(8,128)S(1)}, f32[1,1]{1,0:T(1,128)}) custom-call(f32[128,256]{1,0:T(8,128)S(1)} %last.1.one, f32[256,256]{1,0:T(8,128)S(1)} %get-tuple-element.46.two, f32[8,128]{1,0:T(8,128)S(1)} %get-tuple-element.47.loss, f32[8,128]{1,0:T(8,128)S(1)} %get-tuple-element.35.count), custom_call_target="tpu_custom_call" | custom-call | flops 1000000000 | bytes 8388608 | tf_op jit(solution)/shard_map/reduce/pallas_call | solution.py:590
  135.9 0.7 copy.16
  136.5 0.7 copy.17
Async XLA Ops:
  0.6 12.7 %copy-start.2 = (s32[2,1024]{1,0:T(2,128)S(1)}, s32[2,1024]{1,0:T(2,128)}, u32[]{:S(2)}) copy-start(s32[2,1024]{1,0:T(2,128)} %send.3) | copy-start | bytes 24580
  0.6 12.7 %copy-start.1 = (bf16[2048,128]{1,0:T(8,128)(2,1)S(1)}, bf16[2048,128]{1,0:T(8,128)(2,1)}, u32[]{:S(2)}) copy-start(bf16[2048,128]{1,0:T(8,128)(2,1)} %x.3) | copy-start | bytes 1572868
  2.3 0.7 copy-start.3
  3.0 10.4 %copy-start.6 = (f32[128,256]{1,0:T(8,128)S(1)}, f32[128,256]{1,0:T(8,128)}, u32[]{:S(2)}) copy-start(f32[128,256]{1,0:T(8,128)} %w1.1) | copy-start | bytes 393220
  17.5 14.3 %collective-permute-start = (bf16[1024,256]{1,0:T(8,128)(2,1)S(1)}, bf16[1024,256]{1,0:T(8,128)(2,1)S(1)}, u32[]{:S(2)}, u32[]{:S(2)}) collective-permute-start(bf16[1024,256]{1,0:T(8,128)(2,1)S(1)} %get-tuple-element.31), channel_id=1, source_target_pairs={{0,1},{1,2},{2,3},{3,4},{4,5},{5,6},{6,7},{7,8},{8,9},{9,10},{10,1... | collective-permute-start | bytes 1572872 | tf_op jit(solution)/shard_map/ppermute | solution.py:553
  17.6 14.2 %collective-permute-start.1 = (bf16[1024,256]{1,0:T(8,128)(2,1)S(1)}, bf16[1024,256]{1,0:T(8,128)(2,1)S(1)}, u32[]{:S(2)}, u32[]{:S(2)}) collective-permute-start(bf16[1024,256]{1,0:T(8,128)(2,1)S(1)} %get-tuple-element.32), channel_id=1, source_target_pairs={{0,15},{1,0},{2,1},{3,2},{4,3},{5,4},{6,5},{7,6},{8,7},{9,8},{10,9... | collective-permute-start | bytes 1572872 | tf_op jit(solution)/shard_map/ppermute | solution.py:554
  21.1 10.7 %copy-start = (f32[256,172]{0,1:T(8,128)S(1)}, f32[256,172]{0,1:T(8,128)}, u32[]{:S(2)}) copy-start(f32[256,172]{0,1:T(8,128)} %param.11) | copy-start | bytes 528388
  38.5 10.9 %collective-permute-start.2 = (bf16[1536,128]{1,0:T(8,128)(2,1)S(1)}, bf16[1536,128]{1,0:T(8,128)(2,1)S(1)}, u32[]{:S(2)}, u32[]{:S(2)}) collective-permute-start(bf16[1536,128]{1,0:T(8,128)(2,1)S(1)} %get-tuple-element.36), channel_id=1, source_target_pairs={{0,1},{1,2},{2,3},{3,4},{4,5},{5,6},{6,7},{7,8},{8,9},{9,10},{10,1... | collective-permute-start | bytes 1179656 | tf_op jit(solution)/shard_map/ppermute | solution.py:568
  39.4 10.1 %collective-permute-start.3 = (bf16[1536,128]{1,0:T(8,128)(2,1)S(1)}, bf16[1536,128]{1,0:T(8,128)(2,1)S(1)}, u32[]{:S(2)}, u32[]{:S(2)}) collective-permute-start(bf16[1536,128]{1,0:T(8,128)(2,1)S(1)} %get-tuple-element.37), channel_id=1, source_target_pairs={{0,15},{1,0},{2,1},{3,2},{4,3},{5,4},{6,5},{7,6},{8,7},{9,8},{10,9... | collective-permute-start | bytes 1179656 | tf_op jit(solution)/shard_map/ppermute | solution.py:569
  42.1 7.4 %copy-start.4 = (s32[2048]{0:T(1024)S(1)}, s32[2048]{0:T(1024)}, u32[]{:S(2)}) copy-start(s32[2048]{0:T(1024)} %param.17) | copy-start | bytes 24580
  42.1 7.4 %copy-start.5 = (s32[2048]{0:T(1024)S(1)}, s32[2048]{0:T(1024)}, u32[]{:S(2)}) copy-start(s32[2048]{0:T(1024)} %param.16) | copy-start | bytes 24580
  55.8 19.6 %collective-permute-start.4 = (f32[1536,128]{1,0:T(8,128)S(1)}, f32[1536,128]{1,0:T(8,128)S(1)}, u32[]{:S(2)}, u32[]{:S(2)}) collective-permute-start(f32[1536,128]{1,0:T(8,128)S(1)} %get-tuple-element.39), channel_id=1, source_target_pairs={{0,15},{1,0},{2,1},{3,2},{4,3},{5,4},{6,5},{7,6},{8,7},{9,8},{10,9... | collective-permute-start | bytes 2359304 | tf_op jit(solution)/shard_map/ppermute | solution.py:576
  59.1 23.6 %collective-permute-start.5 = (f32[1536,128]{1,0:T(8,128)S(1)}, f32[1536,128]{1,0:T(8,128)S(1)}, u32[]{:S(2)}, u32[]{:S(2)}) collective-permute-start(f32[1536,128]{1,0:T(8,128)S(1)} %get-tuple-element.40), channel_id=1, source_target_pairs={{0,1},{1,2},{2,3},{3,4},{4,5},{5,6},{6,7},{7,8},{8,9},{9,10},{10,1... | collective-permute-start | bytes 2359304 | tf_op jit(solution)/shard_map/ppermute | solution.py:577
  91.0 23.4 %collective-permute-start.6 = (f32[2048,128]{1,0:T(8,128)S(1)}, f32[2048,128]{1,0:T(8,128)S(1)}, u32[]{:S(2)}, u32[]{:S(2)}) collective-permute-start(f32[2048,128]{1,0:T(8,128)S(1)} %get-tuple-element.43), channel_id=1, source_target_pairs={{0,15},{1,0},{2,1},{3,2},{4,3},{5,4},{6,5},{7,6},{8,7},{9,8},{10,9... | collective-permute-start | bytes 3145736 | tf_op jit(solution)/shard_map/ppermute | solution.py:583
  91.0 25.9 %collective-permute-start.7 = (f32[2048,128]{1,0:T(8,128)S(1)}, f32[2048,128]{1,0:T(8,128)S(1)}, u32[]{:S(2)}, u32[]{:S(2)}) collective-permute-start(f32[2048,128]{1,0:T(8,128)S(1)} %get-tuple-element.44), channel_id=1, source_target_pairs={{0,1},{1,2},{2,3},{3,4},{4,5},{5,6},{6,7},{7,8},{8,9},{9,10},{10,1... | collective-permute-start | bytes 3145736 | tf_op jit(solution)/shard_map/ppermute | solution.py:584

commit v2 on v1

--- a/solution.py
+++ b/solution.py
@@ -295,7 +295,7 @@
     mean[...] = jnp.sum(full[tail : tail + 8, :], keepdims=True) / count[0:1, 0:1]
 
 
-def prep_kernel(n, chunk, rows, packed, mask, src_out, dst_out, w_out, counts, count, total, mine, theirs, send_sem, recv_sem):
+def prep_kernel(n, chunk, rows, packed, mask, src_out, dst_out, w_out, counts, count, total, values, places, mine, theirs, send_sem, recv_sem):
     me, met = greet(n)
     mine[...] = jnp.sum(mask[...].astype(F32).reshape(-1, 8, LANES), axis=0)
     lines = packed.shape[0] // 2
@@ -330,19 +330,30 @@
     w_c = half_w - w_a - w_b
     high = ((s >> 8) * 8 + (d >> 8)).astype(F32)
     planes = [(s & 255).astype(F32), (d & 255).astype(F32), high, w_a, w_b, w_c]
+    for i, p in enumerate(planes):
+        values[i * lines : (i + 1) * lines, :] = p
+    places[:lines, :] = line
+    places[lines:, :] = lane
     met()
     copies = [remote(mine, theirs.at[o - 1], send_sem.at[o - 1], recv_sem.at[o - 1], lax.rem(me + o, n)) for o in range(1, n)]
     for c in copies:
         c.start()
-    acc = jnp.zeros((len(planes) * slots, LANES), F32)
-    for r in range(0, lines, 2):
-        lhs, rhs = [], []
-        for q in (r, r + 1):
-            pick = at((slots, LANES), 0) == line[q : q + 1, :]
-            lhs.append(jnp.concatenate([jnp.where(pick, p[q : q + 1, :], 0.0) for p in planes], axis=0))
-            rhs.append((at((LANES, LANES), 0) == lane[q : q + 1, :]).astype(F32))
-        acc += dot(jnp.concatenate(lhs, axis=1).astype(BF16), jnp.concatenate(rhs, axis=1).astype(BF16), COLS_A)
-    total[...] = acc
+    total[...] = jnp.zeros_like(total)
+
+    @pl.loop(0, lines, step=8)
+    def _(base):
+        acc = None
+        for r in range(0, 8, 2):
+            lhs, rhs = [], []
+            for q in (r, r + 1):
+                row = lambda i: pl.ds(i * lines + base + q, 1)
+                pick = at((slots, LANES), 0) == places[row(0), :]
+                lhs.append(jnp.concatenate([jnp.where(pick, values[row(i), :], 0.0) for i in range(len(planes))], axis=0))
+                rhs.append((at((LANES, LANES), 0) == places[row(1), :]).astype(F32))
+            part = dot(jnp.concatenate(lhs, axis=1).astype(BF16), jnp.concatenate(rhs, axis=1).astype(BF16), COLS_A)
+            acc = part if acc is None else acc + part
+        total[...] += acc
+
     plane = lambda i: total[i * slots : (i + 1) * slots, :]
     high = plane(2).astype(jnp.int32)
     src_out[...] = ((high >> 3) * 256 + plane(0).astype(jnp.int32)) * 2
@@ -543,7 +554,8 @@
         ints = sds((slots, LANES), jnp.int32)
         src, dst, w, counts, count = call(
             functools.partial(prep_kernel, num_dev, PREP_CHUNK, rows), "prep", [ints, ints, sds((slots * LANES, LANES), F32), sds((2,), jnp.int32), one], [VMEM] * 2,
-            [(6 * slots, LANES), (8, LANES), (num_dev - 1, 8, LANES), dma((num_dev - 1,)), dma((num_dev - 1,))],
+            [(6 * slots, LANES), (6 * lines, LANES), pltpu.VMEM((2 * lines, LANES), jnp.int32), (8, LANES), (num_dev - 1, 8, LANES)]
+            + [dma((num_dev - 1,))] * 2,
             out_specs=[VMEM] * 3 + [SMEM, VMEM], vmem=8, collective=0,
         )(packed, mask)
         src, dst = src.reshape(-1), dst.reshape(-1)

time: 140 us -> 140 us (level); the launches traced: 138 us -> 141 us
  Pallas kernels: 74.1 us -> 104 us
  waiting for transfers between devices: 47.1 us -> 20.5 us
    ppermute x2, waiting for transfers between devices: 29.1 us -> 19 us  [step(): got_prev = lax.ppermute(to_p, AXIS, to_prev)]
    pallas_call x2, Pallas kernels: 9.99 us -> 20.1 us  [step(): part = local_back(counts, src, dst, w, grad)]
    ppermute x2, waiting for transfers between devices: 9.9 us -> 0.01 us  [step(): got_next = lax.ppermute(to_n, AXIS, to_next)]
    ppermute x2, waiting for transfers between devices: 8.07 us -> 1.49 us  [step(): from_prev = lax.ppermute(to_n, AXIS, to_next)]
    pallas_call x1, Pallas kernels: 4.99 us -> 10 us  [step(): part = local(counts, src, dst, w, tab_one)]
    pallas_call x1, Pallas kernels: 4.99 us -> 10 us  [step(): part = local(counts, src, dst, w, tab_two)]
    pallas_call x1, Pallas kernels: 6.27 us -> 9.77 us  [step(): call(functools.partial(loss_kernel, chunk_h, classes), 'loss', [sds((8, L...]
    pallas_call x1, Pallas kernels: 12.8 us -> 15.1 us  [step(): call(functools.partial(reduce_kernel, num_dev), 'reduce', [sds(grad_one.s...]
  transfers between devices with their start and end apart: 8 -> 8, of which waited for: 6 -> 3; matrix products, arithmetic and copies ran while one was open for 0% -> 0% of each run, Pallas kernels for 14% -> 28%
where the time goes in v2:
time: 140 us; the launch traced here: 141 us
  Pallas kernels  104 us (74%)
  waiting for transfers between devices  20.5 us (15%)
  starting transfers between devices  10.2 us (7%)
  between operations  2.5 us (2%)
  local copies, waits for them, and re-layouts  2.05 us (1%)
  other arithmetic  1.6 us (1%)
    pallas_call x2, Pallas kernels, step(): part = local_back(counts, src, dst, w, grad)  20.1 us
    ppermute x2, waiting for transfers between devices, step(): got_prev = lax.ppermute(to_p, AXIS, to_prev)  19 us
    pallas_call x1, Pallas kernels, step(): call(functools.partial(reduce_kernel, num_dev), 'reduce', [sds(grad_one.s...  15.1 us
    pallas_call x1, Pallas kernels, step(): call(functools.partial(prep_kernel, num_dev, PREP_CHUNK, rows), 'prep', [...  11.2 us
    pallas_call x1, Pallas kernels, step(): call(functools.partial(middle_kernel, chunk_h), 'middle', [sds((2 * LANES...  10 us
    pallas_call x1, Pallas kernels, step(): part = local(counts, src, dst, w, tab_one)  10 us
    pallas_call x1, Pallas kernels, step(): part = local(counts, src, dst, w, tab_two)  10 us
    pallas_call x1, Pallas kernels, step(): call(functools.partial(loss_kernel, chunk_h, classes), 'loss', [sds((8, L...  9.77 us
  transfers between devices with their start and end apart: 8, of which 3 were waited for; matrix products, arithmetic and copies ran while one was open for 0% of the time, Pallas kernels for 28%

profile of v2, /device:TPU:0, one launch (start us, length us, event | category | flops | bytes accessed | tf_op | source)
XLA Modules:
  0.0 141.2 jit_solution(17612709945068244498)
XLA Ops:
  0.6 0.0 copy-start.2
  0.6 0.0 copy-start.1
  0.7 0.8 convert_bitcast_fusion
  1.5 0.8 pad_maximum_fusion.packed
  2.3 0.0 copy-start.3
  2.3 0.7 copy-done.3
  3.0 0.0 copy-start.6
  3.0 11.2 %prep.1 = (s32[72,128]{1,0:T(8,128)S(1)}, s32[72,128]{1,0:T(8,128)S(1)}, f32[9216,128]{1,0:T(8,128)S(1)}, s32[2]{0:T(128)S(1)}, f32[8,128]{1,0:T(8,128)S(1)}) custom-call(f32[128,128]{1,0:T(8,128)S(1)} %pad_maximum_fusion.packed, s32[16,128]{1,0:T(8,128)S(1)} %bitcast.30), custom_call_target="tpu_custom_call" | custom-call | flops 1000000000 | bytes 8388608 | tf_op jit(solution)/shard_map/prep/pallas_call | solution.py:555
  14.1 0.0 copy-done.2
  14.1 0.0 copy-done.1
  14.2 0.0 copy-done.6
  14.2 4.1 %first.1 = (f32[4096,128]{1,0:T(8,128)S(1)}, bf16[1024,256]{1,0:T(8,128)(2,1)S(1)}, bf16[1024,256]{1,0:T(8,128)(2,1)S(1)}) custom-call(bf16[2048,128]{1,0:T(8,128)(2,1)S(1)} %copy-done.1, f32[128,256]{1,0:T(8,128)S(1)} %copy-done.6, s32[2,1024]{1,0:T(2,128)S(1)} %copy-done.2, s32[2]{0:T(128)S(1)} %get-tuple-element.27.after.counts), custom_call_target="tpu_custom_call" | custom-call | flops 1000000000 | bytes 8388608 | tf_op jit(solution)/shard_map/first/pallas_call | solution.py:564
  18.3 0.2 collective-permute-start
  18.5 3.4 %collective-permute-start.1 = (bf16[1024,256]{1,0:T(8,128)(2,1)S(1)}, bf16[1024,256]{1,0:T(8,128)(2,1)S(1)}, u32[]{:S(2)}, u32[]{:S(2)}) collective-permute-start(bf16[1024,256]{1,0:T(8,128)(2,1)S(1)} %get-tuple-element.32), channel_id=1, source_target_pairs={{0,15},{1,0},{2,1},{3,2},{4,3},{5,4},{6,5},{7,6},{8,7},{9,8},{10,9... | collective-permute-start | bytes 1572872 | tf_op jit(solution)/shard_map/ppermute | solution.py:566
  21.9 0.0 copy-start
  21.9 10.0 %local_edges.4.part = f32[4096,128]{1,0:T(8,128)S(1)} custom-call(s32[2]{0:T(128)S(1)} %get-tuple-element.27.after.counts, s32[9216]{0:T(1024)S(1)} %bitcast.13, s32[9216]{0:T(1024)S(1)} %bitcast.20, f32[9216,128]{1,0:T(8,128)S(1)} %get-tuple-element.30.w, f32[4096,128]{1,0:T(8,128)S(1)} %get-tuple-element.33.table), custom_call_target="tpu_custom_call" | custom-call | flops 10000000000 | bytes 8388608 | tf_op jit(solution)/shard_map/local_edges/pallas_call | solution.py:575
  31.9 1.5 %collective-permute-done.from_prev = bf16[1024,256]{1,0:T(8,128)(2,1)S(1)} collective-permute-done((bf16[1024,256]{1,0:T(8,128)(2,1)S(1)}, bf16[1024,256]{1,0:T(8,128)(2,1)S(1)}, u32[]{:S(2)}, u32[]{:S(2)}) %collective-permute-start) | collective-permute-done | bytes 524320 | tf_op jit(solution)/shard_map/ppermute | solution.py:565
  33.4 0.0 collective-permute-done.1.from_next
  33.4 0.0 copy-done
  33.4 8.5 %hidden.1 = (bf16[2048,256]{1,0:T(8,128)(2,1)S(1)}, f32[4096,128]{1,0:T(8,128)S(1)}, bf16[1536,128]{1,0:T(8,128)(2,1)S(1)}, bf16[1536,128]{1,0:T(8,128)(2,1)S(1)}, s32[16,128]{1,0:T(8,128)S(1)}) custom-call(s32[2]{0:T(128)S(1)} %get-tuple-element.27.after.counts, s32[9216]{0:T(1024)S(1)} %bitcast.14, s32[9216]{0:T(1024)S(1)} %bitcast.21, ...), custom_call_target="tpu_custom_call" | custom-call | flops 1000000000 | bytes 8388608 | tf_op jit(solution)/shard_map/hidden/pallas_call | solution.py:576
  41.9 0.1 collective-permute-start.2
  42.0 3.5 %collective-permute-start.3 = (bf16[1536,128]{1,0:T(8,128)(2,1)S(1)}, bf16[1536,128]{1,0:T(8,128)(2,1)S(1)}, u32[]{:S(2)}, u32[]{:S(2)}) collective-permute-start(bf16[1536,128]{1,0:T(8,128)(2,1)S(1)} %get-tuple-element.37), channel_id=1, source_target_pairs={{0,15},{1,0},{2,1},{3,2},{4,3},{5,4},{6,5},{7,6},{8,7},{9,8},{10,9... | collective-permute-start | bytes 1179656 | tf_op jit(solution)/shard_map/ppermute | solution.py:581
  45.5 0.0 copy-start.4
  45.5 0.0 copy-start.5
  45.5 10.0 %local_edges.5.part = f32[4096,128]{1,0:T(8,128)S(1)} custom-call(s32[2]{0:T(128)S(1)} %get-tuple-element.27.after.counts, s32[9216]{0:T(1024)S(1)} %bitcast.15, s32[9216]{0:T(1024)S(1)} %bitcast.22, f32[9216,128]{1,0:T(8,128)S(1)} %get-tuple-element.30.w, f32[4096,128]{1,0:T(8,128)S(1)} %get-tuple-element.38.table), custom_call_target="tpu_custom_call" | custom-call | flops 10000000000 | bytes 8388608 | tf_op jit(solution)/shard_map/local_edges/pallas_call | solution.py:583
  55.5 0.0 collective-permute-done.2.from_prev
  55.5 0.0 collective-permute-done.3.from_next
  55.5 0.0 copy-done.4
  55.5 0.0 copy-done.5
  55.6 9.8 %loss.1 = (f32[8,128]{1,0:T(8,128)S(1)}, f32[4096,128]{1,0:T(8,128)S(1)}, f32[1536,128]{1,0:T(8,128)S(1)}, f32[1536,128]{1,0:T(8,128)S(1)}) custom-call(s32[2]{0:T(128)S(1)} %get-tuple-element.27.after.counts, s32[9216]{0:T(1024)S(1)} %bitcast.16, s32[9216]{0:T(1024)S(1)} %bitcast.23, f32[9216,128]{1,0:T(8,128)S(1)} %get-tuple-element.30.w, ...), custom_call_target="tpu_custom_call" | custom-call | flops 1000000000 | bytes 8388608 | tf_op jit(solution)/shard_map/loss/pallas_call | solution.py:584
  65.3 0.1 collective-permute-start.4
  65.4 0.5 collective-permute-start.5
  65.9 10.0 %local_edges.6.part = f32[4096,128]{1,0:T(8,128)S(1)} custom-call(s32[2]{0:T(128)S(1)} %get-tuple-element.27.after.counts, s32[9216]{0:T(1024)S(1)} %bitcast.17, s32[9216]{0:T(1024)S(1)} %bitcast.24, f32[9216,128]{1,0:T(8,128)S(1)} %get-tuple-element.30.w, f32[4096,128]{1,0:T(8,128)S(1)} %get-tuple-element.41.table), custom_call_target="tpu_custom_call" | custom-call | flops 10000000000 | bytes 8388608 | tf_op jit(solution)/shard_map/local_edges/pallas_call | solution.py:590
  75.9 7.2 %collective-permute-done.4.got_prev = f32[1536,128]{1,0:T(8,128)S(1)} collective-permute-done((f32[1536,128]{1,0:T(8,128)S(1)}, f32[1536,128]{1,0:T(8,128)S(1)}, u32[]{:S(2)}, u32[]{:S(2)}) %collective-permute-start.4) | collective-permute-done | bytes 786464 | tf_op jit(solution)/shard_map/ppermute | solution.py:588
  83.1 0.0 collective-permute-done.5.got_next
  83.1 10.0 %middle.1 = (f32[256,256]{1,0:T(8,128)S(1)}, f32[4096,128]{1,0:T(8,128)S(1)}, f32[2048,128]{1,0:T(8,128)S(1)}, f32[2048,128]{1,0:T(8,128)S(1)}) custom-call(s32[2]{0:T(128)S(1)} %get-tuple-element.27.after.counts, s32[9216]{0:T(1024)S(1)} %bitcast.18, s32[9216]{0:T(1024)S(1)} %bitcast.25, f32[9216,128]{1,0:T(8,128)S(1)} %get-tuple-element.30.w, ...), custom_call_target="tpu_custom_call" | custom-call | flops 1000000000 | bytes 8388608 | tf_op jit(solution)/shard_map/middle/pallas_call | solution.py:591
  93.2 2.5 %collective-permute-start.6 = (f32[2048,128]{1,0:T(8,128)S(1)}, f32[2048,128]{1,0:T(8,128)S(1)}, u32[]{:S(2)}, u32[]{:S(2)}) collective-permute-start(f32[2048,128]{1,0:T(8,128)S(1)} %get-tuple-element.43), channel_id=1, source_target_pairs={{0,15},{1,0},{2,1},{3,2},{4,3},{5,4},{6,5},{7,6},{8,7},{9,8},{10,9... | collective-permute-start | bytes 3145736 | tf_op jit(solution)/shard_map/ppermute | solution.py:595
  95.7 0.0 collective-permute-start.7
  95.7 10.0 %local_edges.7.part = f32[4096,128]{1,0:T(8,128)S(1)} custom-call(s32[2]{0:T(128)S(1)} %get-tuple-element.27.after.counts, s32[9216]{0:T(1024)S(1)} %bitcast.19, s32[9216]{0:T(1024)S(1)} %bitcast.26, f32[9216,128]{1,0:T(8,128)S(1)} %get-tuple-element.30.w, f32[4096,128]{1,0:T(8,128)S(1)} %get-tuple-element.45.table), custom_call_target="tpu_custom_call" | custom-call | flops 10000000000 | bytes 8388608 | tf_op jit(solution)/shard_map/local_edges/pallas_call | solution.py:597
  105.7 11.8 %collective-permute-done.6.got_prev = f32[2048,128]{1,0:T(8,128)S(1)} collective-permute-done((f32[2048,128]{1,0:T(8,128)S(1)}, f32[2048,128]{1,0:T(8,128)S(1)}, u32[]{:S(2)}, u32[]{:S(2)}) %collective-permute-start.6) | collective-permute-done | bytes 1048608 | tf_op jit(solution)/shard_map/ppermute | solution.py:595
  117.5 0.0 collective-permute-done.7.got_next
  117.5 5.6 %last.1.one = f32[128,256]{1,0:T(8,128)S(1)} custom-call(s32[2048]{0:T(1024)S(1)} %bitcast.29, f32[2048,128]{1,0:T(8,128)S(1)} %collective-permute-done.6.got_prev, f32[2048,128]{1,0:T(8,128)S(1)} %collective-permute-done.7.got_next, f32[4096,128]{1,0:T(8,128)S(1)} %local_edges.7.part, bf16[2048,128]{1,0:T(8,128)(2,1)S(1)} %copy-done.1), custom_call_target="tpu_custom_call" | custom-call | flops 1000000000 | bytes 8388608 | tf_op jit(solution)/shard_map/last/pallas_call | solution.py:599
  123.1 15.1 %reduce.1 = (f32[128,256]{1,0:T(8,128)S(1)}, f32[172,256]{1,0:T(8,128)S(1)}, f32[1,1]{1,0:T(1,128)}) custom-call(f32[128,256]{1,0:T(8,128)S(1)} %last.1.one, f32[256,256]{1,0:T(8,128)S(1)} %get-tuple-element.46.two, f32[8,128]{1,0:T(8,128)S(1)} %get-tuple-element.47.loss, f32[8,128]{1,0:T(8,128)S(1)} %get-tuple-element.35.count), custom_call_target="tpu_custom_call" | custom-call | flops 1000000000 | bytes 8388608 | tf_op jit(solution)/shard_map/reduce/pallas_call | solution.py:602
  138.7 0.7 copy.16
  139.4 0.7 copy.17
Async XLA Ops:
  0.6 13.5 %copy-start.2 = (s32[2,1024]{1,0:T(2,128)S(1)}, s32[2,1024]{1,0:T(2,128)}, u32[]{:S(2)}) copy-start(s32[2,1024]{1,0:T(2,128)} %send.3) | copy-start | bytes 24580
  0.6 13.5 %copy-start.1 = (bf16[2048,128]{1,0:T(8,128)(2,1)S(1)}, bf16[2048,128]{1,0:T(8,128)(2,1)}, u32[]{:S(2)}) copy-start(bf16[2048,128]{1,0:T(8,128)(2,1)} %x.3) | copy-start | bytes 1572868
  2.3 0.7 copy-start.3
  3.0 11.2 %copy-start.6 = (f32[128,256]{1,0:T(8,128)S(1)}, f32[128,256]{1,0:T(8,128)}, u32[]{:S(2)}) copy-start(f32[128,256]{1,0:T(8,128)} %w1.1) | copy-start | bytes 393220
  18.3 15.1 %collective-permute-start = (bf16[1024,256]{1,0:T(8,128)(2,1)S(1)}, bf16[1024,256]{1,0:T(8,128)(2,1)S(1)}, u32[]{:S(2)}, u32[]{:S(2)}) collective-permute-start(bf16[1024,256]{1,0:T(8,128)(2,1)S(1)} %get-tuple-element.31), channel_id=1, source_target_pairs={{0,1},{1,2},{2,3},{3,4},{4,5},{5,6},{6,7},{7,8},{8,9},{9,10},{10,1... | collective-permute-start | bytes 1572872 | tf_op jit(solution)/shard_map/ppermute | solution.py:565
  18.5 15.0 %collective-permute-start.1 = (bf16[1024,256]{1,0:T(8,128)(2,1)S(1)}, bf16[1024,256]{1,0:T(8,128)(2,1)S(1)}, u32[]{:S(2)}, u32[]{:S(2)}) collective-permute-start(bf16[1024,256]{1,0:T(8,128)(2,1)S(1)} %get-tuple-element.32), channel_id=1, source_target_pairs={{0,15},{1,0},{2,1},{3,2},{4,3},{5,4},{6,5},{7,6},{8,7},{9,8},{10,9... | collective-permute-start | bytes 1572872 | tf_op jit(solution)/shard_map/ppermute | solution.py:566
  21.9 11.5 %copy-start = (f32[256,172]{0,1:T(8,128)S(1)}, f32[256,172]{0,1:T(8,128)}, u32[]{:S(2)}) copy-start(f32[256,172]{0,1:T(8,128)} %param.11) | copy-start | bytes 528388
  41.9 13.6 %collective-permute-start.2 = (bf16[1536,128]{1,0:T(8,128)(2,1)S(1)}, bf16[1536,128]{1,0:T(8,128)(2,1)S(1)}, u32[]{:S(2)}, u32[]{:S(2)}) collective-permute-start(bf16[1536,128]{1,0:T(8,128)(2,1)S(1)} %get-tuple-element.36), channel_id=1, source_target_pairs={{0,1},{1,2},{2,3},{3,4},{4,5},{5,6},{6,7},{7,8},{8,9},{9,10},{10,1... | collective-permute-start | bytes 1179656 | tf_op jit(solution)/shard_map/ppermute | solution.py:580
  42.0 13.6 %collective-permute-start.3 = (bf16[1536,128]{1,0:T(8,128)(2,1)S(1)}, bf16[1536,128]{1,0:T(8,128)(2,1)S(1)}, u32[]{:S(2)}, u32[]{:S(2)}) collective-permute-start(bf16[1536,128]{1,0:T(8,128)(2,1)S(1)} %get-tuple-element.37), channel_id=1, source_target_pairs={{0,15},{1,0},{2,1},{3,2},{4,3},{5,4},{6,5},{7,6},{8,7},{9,8},{10,9... | collective-permute-start | bytes 1179656 | tf_op jit(solution)/shard_map/ppermute | solution.py:581
  45.5 10.1 %copy-start.4 = (s32[2048]{0:T(1024)S(1)}, s32[2048]{0:T(1024)}, u32[]{:S(2)}) copy-start(s32[2048]{0:T(1024)} %param.17) | copy-start | bytes 24580
  45.5 10.1 %copy-start.5 = (s32[2048]{0:T(1024)S(1)}, s32[2048]{0:T(1024)}, u32[]{:S(2)}) copy-start(s32[2048]{0:T(1024)} %param.16) | copy-start | bytes 24580
  65.3 17.8 %collective-permute-start.4 = (f32[1536,128]{1,0:T(8,128)S(1)}, f32[1536,128]{1,0:T(8,128)S(1)}, u32[]{:S(2)}, u32[]{:S(2)}) collective-permute-start(f32[1536,128]{1,0:T(8,128)S(1)} %get-tuple-element.39), channel_id=1, source_target_pairs={{0,15},{1,0},{2,1},{3,2},{4,3},{5,4},{6,5},{7,6},{8,7},{9,8},{10,9... | collective-permute-start | bytes 2359304 | tf_op jit(solution)/shard_map/ppermute | solution.py:588
  65.4 17.7 %collective-permute-start.5 = (f32[1536,128]{1,0:T(8,128)S(1)}, f32[1536,128]{1,0:T(8,128)S(1)}, u32[]{:S(2)}, u32[]{:S(2)}) collective-permute-start(f32[1536,128]{1,0:T(8,128)S(1)} %get-tuple-element.40), channel_id=1, source_target_pairs={{0,1},{1,2},{2,3},{3,4},{4,5},{5,6},{6,7},{7,8},{8,9},{9,10},{10,1... | collective-permute-start | bytes 2359304 | tf_op jit(solution)/shard_map/ppermute | solution.py:589
  93.2 24.3 %collective-permute-start.6 = (f32[2048,128]{1,0:T(8,128)S(1)}, f32[2048,128]{1,0:T(8,128)S(1)}, u32[]{:S(2)}, u32[]{:S(2)}) collective-permute-start(f32[2048,128]{1,0:T(8,128)S(1)} %get-tuple-element.43), channel_id=1, source_target_pairs={{0,15},{1,0},{2,1},{3,2},{4,3},{5,4},{6,5},{7,6},{8,7},{9,8},{10,9... | collective-permute-start | bytes 3145736 | tf_op jit(solution)/shard_map/ppermute | solution.py:595
  95.7 21.9 %collective-permute-start.7 = (f32[2048,128]{1,0:T(8,128)S(1)}, f32[2048,128]{1,0:T(8,128)S(1)}, u32[]{:S(2)}, u32[]{:S(2)}) collective-permute-start(f32[2048,128]{1,0:T(8,128)S(1)} %get-tuple-element.44), channel_id=1, source_target_pairs={{0,1},{1,2},{2,3},{3,4},{4,5},{5,6},{6,7},{7,8},{8,9},{9,10},{10,1... | collective-permute-start | bytes 3145736 | tf_op jit(solution)/shard_map/ppermute | solution.py:596

commit v3 on v2

v3 whole, which is shorter than its diff:
```python
import functools

import jax
import jax.numpy as jnp
from jax import lax
from jax.experimental import pallas as pl
from jax.experimental.pallas import tpu as pltpu
from jax.sharding import PartitionSpec as P

AXIS = "graph"
LANES = 128
ROWS_A = (((0,), (0,)), ((), ()))
COLS_A = (((1,), (1,)), ((), ()))
F32, BF16 = jnp.float32, jnp.bfloat16
VMEM = pl.BlockSpec(memory_space=pltpu.VMEM)
SMEM = pl.BlockSpec(memory_space=pltpu.SMEM)
ANY = pl.BlockSpec(memory_space=pl.ANY)
STEP = 512
BLOCK = 256
BYTE = 256
SUB = 8
TILE = (SUB, LANES)
SQUARE = (LANES, LANES)
PREP_CHUNK = 64
SEGMENT = 1024
MESH = pl.DeviceIdType.MESH


def dot(a, b, dims=(((1,), (0,)), ((), ()))):
    return lax.dot_general(a, b, dims, preferred_element_type=F32)


def fill_zero(ref):
    zero = jnp.zeros((STEP, LANES), F32)

    @pl.loop(0, ref.shape[0], step=STEP)
    def _(i):
        ref[pl.ds(i, STEP), :] = zero


def copy_in(dst, src):
    @pl.loop(0, dst.shape[0], step=STEP)
    def _(i):
        dst[pl.ds(i, STEP), :] = src[pl.ds(i, STEP), :].astype(F32)


class Edges:
    def __init__(self, first, last, w, arrays, smem, sems):
        self.first, self.last, self.w = first, last, w
        self.pairs = tuple(zip(arrays, smem))
        self.sems = sems

    def copies(self, seg):
        part = pl.ds(pl.multiple_of(seg * SEGMENT, SEGMENT), SEGMENT)
        return [pltpu.make_async_copy(a.at[part], b.at[part], self.sems.at[i, seg]) for i, (a, b) in enumerate(self.pairs)]

    def fetch(self):
        per = SEGMENT // PREP_CHUNK
        for seg in range(self.pairs[0][1].shape[0] // SEGMENT):

            @pl.when(jnp.logical_and(seg * per < self.last, (seg + 1) * per > self.first))
            def _():
                for c in self.copies(seg):
                    c.start()

    def walk(self, chunk, from_idx, to_idx, table, accs, wait):
        group, per, ratio = len(accs), SEGMENT // chunk, PREP_CHUNK // chunk
        first, last = self.first * ratio, self.last * ratio

        def body(c, _):
            base = c * chunk
            w_chunk = self.w.at[pl.ds(pl.multiple_of(base, chunk), chunk)]
            for g in range(0, chunk, group):
                pend = []
                for u in range(group):
                    k = base + g + u
                    s = pl.multiple_of(from_idx[k], 2)
                    d = pl.multiple_of(to_idx[k], 2)
                    pend.append((d, accs[u][pl.ds(d, 2), :] + table[pl.ds(s, 2), :] * w_chunk[g + u : g + u + 1, :]))
                for u in range(group):
                    accs[u][pl.ds(pend[u][0], 2), :] = pend[u][1]
            return 0

        if not wait:
            lax.fori_loop(first, last, body, 0)
            return

        def segment(seg, _):
            for c in self.copies(seg):
                c.wait()
            lax.fori_loop(jnp.maximum(first, seg * per), jnp.minimum(last, (seg + 1) * per), body, 0)
            return 0

        lax.fori_loop(first // per, (last + per - 1) // per, segment, 0)


def one_hot_rows(idx, which, start, table):
    lane = across(SQUARE)
    hot = []
    for q in range(2):
        want = spread(idx[which : which + 1, pl.ds(pl.multiple_of(start + q * LANES, LANES), LANES)])
        hot.append(
            stack_lanes([jnp.where(want == lane + LANES * j, 1.0, 0.0).astype(BF16) for j in range(table.shape[0] // LANES)])
        )
    return dot(stack_rows(hot), table[...])


def low_lanes(rows):
    return across((rows, LANES)) < LANES // 2


def swap_lanes(v):
    return pltpu.roll(v, LANES // 2, 1)


def fetch_index(send, idx, sems):
    parts = [pl.ds(i, LANES) for i in range(0, send.shape[1], LANES)]
    return [pltpu.make_async_copy(send.at[1, p], idx.at[p], sems.at[i]) for i, p in enumerate(parts)]


def gather_block(send, idx, i, table_b, table, buf):
    got = one_hot_rows(send, 0, i, table_b)
    out = buf.at[pl.ds(pl.multiple_of(2 * i, 512), 512)]
    for u in range(BLOCK):
        s = pl.multiple_of(idx[i + u] * 2, 2)
        out[2 * u : 2 * u + 2, :] = table[pl.ds(s, 2), :]
    return got


def gather_rows(send, idx, table_b, table, buf, to_prev, to_next):
    @pl.loop(0, to_prev.shape[0], step=BLOCK)
    def _(i):
        i = pl.multiple_of(i, BLOCK)
        to_prev[pl.ds(i, BLOCK), :] = gather_block(send, idx, i, table_b, table, buf).astype(BF16)

    @pl.loop(0, to_next.shape[0], step=BLOCK)
    def _(i):
        to_next[pl.ds(pl.multiple_of(i, BLOCK), BLOCK), :] = stack_lanes(halves([buf], i, BLOCK)).astype(BF16)


def pack_rows(out, i, half, a_even, a_odd, b_even, b_odd):
    n = a_even.shape[0]
    out[pl.ds(i, n), :] = a_even.astype(out.dtype)
    out[pl.ds(half + i, n), :] = b_even.astype(out.dtype)
    out[pl.ds(2 * half + i, n), :] = jnp.where(low_lanes(n), a_odd, swap_lanes(b_odd)).astype(out.dtype)


def gather_packed(send, idx, table_b, table, buf, to_prev, to_next):
    half = to_prev.shape[0] // 3

    @pl.loop(0, half, step=BLOCK)
    def _(i):
        i = pl.multiple_of(i, BLOCK)
        a = gather_block(send, idx, i, table_b, table, buf)
        b = gather_block(send, idx, half + i, table_b, table, buf)
        pack_rows(to_prev, i, half, a[:, :LANES], a[:, LANES:], b[:, :LANES], b[:, LANES:])

    @pl.loop(0, half, step=BLOCK)
    def _(i):
        i = pl.multiple_of(i, BLOCK)
        pack_rows(to_next, i, half, *halves([buf], i, BLOCK), *halves([buf], half + i, BLOCK))


def unpack_rows(got, table, start, half=None):
    half = got.shape[0] // 3 if half is None else half
    n = half // 2

    @pl.loop(0, half, step=n)
    def _(i):
        i = pl.multiple_of(i, n)
        a, b, both = (got[pl.ds(k + i, n), :].astype(F32) for k in (0, half, 2 * half))
        put_halves(table, start + i, n, a, jnp.where(low_lanes(n), both, 0.0))
        put_halves(table, start + half + i, n, b, jnp.where(low_lanes(n), swap_lanes(both), 0.0))


def unpack_plain(got, table, start):
    @pl.loop(0, got.shape[0], step=BLOCK)
    def _(i):
        t = got[pl.ds(i, BLOCK), :].astype(F32)
        put_halves(table, start + i, BLOCK, t[:, :LANES], t[:, LANES:])


def spread(row):
    return jnp.transpose(jnp.broadcast_to(row, SQUARE))


def return_rows(back, slots, start, count, vals, accs, chunk=32):
    group = len(accs)

    def body(c, _):
        block = vals.at[pl.ds(pl.multiple_of(c * 2 * chunk, 2 * chunk), 2 * chunk)]
        for g in range(0, chunk, group):
            pend = []
            for u in range(group):
                d = pl.multiple_of(back[slots[start + c * chunk + g + u]], 2)
                pend.append((d, accs[u][pl.ds(d, 2), :] + block[2 * (g + u) : 2 * (g + u) + 2, :]))
            for u in range(group):
                accs[u][pl.ds(pend[u][0], 2), :] = pend[u][1]
        return 0

    lax.fori_loop(0, (count + chunk - 1) // chunk, body, 0)


def group(i, n, which):
    return pl.ds(2 * i + which, n, stride=2), slice(None)


def halves(accs, i, n):
    return [functools.reduce(jnp.add, [a[group(i, n, k)] for a in accs]) for k in range(2)]


def put_halves(table, i, n, *parts):
    for k, part in enumerate(parts):
        table[group(i, n, k)] = part


def stack_rows(parts):
    return jnp.concatenate(parts, axis=0)


def stack_lanes(parts):
    return jnp.concatenate(parts, axis=1)


def down(shape):
    return lax.broadcasted_iota(jnp.int32, shape, 0)


def across(shape):
    return lax.broadcasted_iota(jnp.int32, shape, 1)


def prefix(mask, above):
    m = mask.astype(BF16)
    before = (down(SQUARE) < across(SQUARE)).astype(BF16)
    return dot(m, before) + dot(above, dot(m, jnp.ones(SQUARE, BF16)).astype(BF16))


def rank_halo(halo, counts, src, used, src_back, lists):
    lines = used.shape[0]
    side = lines // 2
    i, j = down((lines, lines)), across((lines, lines))
    above = jnp.logical_and(j < i, (j >= side) == (i >= side)).astype(F32).astype(BF16)
    rank = prefix(used[...], above).astype(jnp.int32)
    low, high = rank & (LANES - 1), rank >> 7
    table = stack_rows([low.astype(F32), high.astype(F32)]).astype(BF16)

    def line(r, _):
        slot = src[pl.ds(r, 1), :] >> 1
        h, l = slot >> 7, slot & (LANES - 1)
        got = dot(table, (down(SQUARE) == l).astype(F32).astype(BF16))
        got = jnp.where(down((lines, LANES)) == h, got[:lines] + LANES * got[lines:], 0.0)
        got = jnp.sum(got, axis=0, keepdims=True).astype(jnp.int32)
        src_back[pl.ds(r, 1), :] = (got + jnp.where(h >= side, halo, 0)) * 2
        return 0

    ratio = LANES // PREP_CHUNK
    lax.fori_loop(counts[0] // ratio, (counts[1] + ratio - 1) // ratio, line, 0)
    for k in range(2):
        acc = jnp.zeros((24, LANES), F32)
        for hh in range(side):
            q = k * side + hh
            pick = jnp.where(down(TILE) == high[q : q + 1, :], used[q : q + 1, :], 0.0)
            lhs = stack_rows([pick * across(TILE).astype(F32), pick * hh, pick]).astype(BF16)
            acc += dot(lhs, (down(SQUARE) == low[q : q + 1, :]).astype(F32).astype(BF16), COLS_A)
        slots = acc[0:8] + LANES * acc[8:16]
        lists[k * side : (k + 1) * side, :] = jnp.where(acc[16:24] > 0.0, slots[:side], -1.0)


def first_kernel(compact, halo, x, w1, send, counts, src, w, used, tab, to_prev, to_next, w_out, src_back, lists, tab_b, buf, idx, sems):
    fetch = fetch_index(send, idx, sems)
    for c in fetch:
        c.start()
    rows = x.shape[0]
    w1_b = w1[...].astype(BF16)

    @pl.loop(0, rows, step=BLOCK)
    def _(i):
        t = dot(x[pl.ds(i, BLOCK), :], w1_b).astype(BF16)
        tab_b[pl.ds(i, BLOCK), :] = t
        t = t.astype(F32)
        put_halves(tab, i, BLOCK, t[:, :LANES], t[:, LANES:])

    @pl.loop(0, w.shape[0] // SUB)
    def _(r):
        for q in range(SUB):
            w_out[pl.ds(pl.multiple_of((r * SUB + q) * LANES, LANES), LANES), :] = spread(w[pl.ds(r * SUB + q, 1), :])

    src_back[...] = src[...]
    if compact:
        rank_halo(halo, counts, src, used, src_back, lists)
    else:
        line = down(lists.shape)
        line = jnp.where(line >= lists.shape[0] // 2, line - lists.shape[0] // 2, line)
        lists[...] = (line * LANES + across(lists.shape)).astype(F32)
    for c in fetch:
        c.wait()
    gather_rows(send, idx, tab_b, tab, buf, to_prev, to_next)


def greet(n):
    me = lax.axis_index(AXIS)
    barrier = pltpu.get_barrier_semaphore()
    for o in range(1, n):
        pl.semaphore_signal(barrier, inc=1, device_id=(lax.rem(me + o, n),), device_id_type=MESH)
    return me, lambda: pl.semaphore_wait(barrier, n - 1)


def remote(src, dst, send_sem, recv_sem, peer):
    return pltpu.make_async_remote_copy(
        src_ref=src, dst_ref=dst, send_sem=send_sem, recv_sem=recv_sem, device_id=(peer,), device_id_type=MESH
    )


def reduce_kernel(n, one, two, loss, count, one_out, two_out, mean, work, full, got_pair, got_rest, sems):
    me = lax.axis_index(AXIS)
    chips, core = n // 2, lax.rem(me, 2)
    chip = lax.div(me, 2)
    pair = me + 1 - 2 * core
    others = [lax.rem(chip + o, chips) for o in range(1, chips)]
    barrier = pltpu.get_barrier_semaphore()
    for p in [pair] + [2 * c + core for c in others]:
        pl.semaphore_signal(barrier, inc=1, device_id=(p,), device_id_type=MESH)
    classes = two_out.shape[0]
    lines = -(-classes // SUB) * SUB
    top, wide = one.shape
    work[0:top, :] = one[:, :LANES]
    work[top : 2 * top, :] = one[:, LANES:]
    work[2 * top : 2 * top + lines, :] = two[:lines, :LANES]
    work[2 * top + lines : 2 * top + 2 * lines, :] = two[:lines, LANES:]
    tail = 2 * top + 2 * lines
    work[tail : tail + SUB, :] = loss[...]
    work[tail + SUB :, :] = jnp.zeros((work.shape[0] - tail - SUB, LANES), F32)
    pl.semaphore_wait(barrier, chips)

    half = work.shape[0] // 2
    piece = half // chips
    rows = lambda start, size: pl.ds(pl.multiple_of(start, SUB), size)
    mine, other = rows(core * half, half), rows((1 - core) * half, half)
    swap = remote(work.at[other], got_pair, sems.at[0, 0], sems.at[1, 0], pair)
    swap.start()
    swap.wait()
    work[mine, :] += got_pair[...]
    scatter = [
        remote(work.at[rows(core * half + c * piece, piece)], got_rest.at[o], sems.at[0, 1 + o], sems.at[1, 1 + o], 2 * c + core)
        for o, c in enumerate(others)
    ]
    for c in scatter:
        c.start()
    for c in scatter:
        c.wait()
    own = rows(core * half + chip * piece, piece)
    work[own, :] += jnp.sum(got_rest[...], axis=0)
    full[own, :] = work[own, :]
    gather = [
        remote(work.at[own], full.at[own], sems.at[0, chips + o], sems.at[1, chips + o], 2 * c + core) for o, c in enumerate(others)
    ]
    for c in gather:
        c.start()
    for c in gather:
        c.wait()
    last = remote(full.at[mine], full.at[mine], sems.at[0, 2 * chips - 1], sems.at[1, 2 * chips - 1], pair)
    last.start()
    last.wait()
    one_out[:, :LANES] = full[0:top, :]
    one_out[:, LANES:] = full[top : 2 * top, :]
    two_out[:, :LANES] = full[2 * top : 2 * top + classes, :]
    two_out[:, LANES:] = full[2 * top + lines : 2 * top + lines + classes, :]
    mean[...] = jnp.sum(full[tail : tail + SUB, :], keepdims=True) / count[0:1, 0:1]


def prep_kernel(n, chunk, rows, packed, mask, src_out, dst_out, w_out, used, counts, count, need, total, values, places, hits, mine, theirs, send_sem, recv_sem):
    me, met = greet(n)
    lines = packed.shape[0] // 2
    slots = src_out.shape[0]
    both = packed[:lines, :].astype(jnp.int32)
    src, d, w = both >> 11, both & 2047, packed[lines:, :]
    live = w != 0.0
    halo = src >= rows
    above = (across((lines, lines)) < down((lines, lines))).astype(F32).astype(BF16)
    is_local, is_halo = jnp.logical_and(live, jnp.logical_not(halo)), jnp.logical_and(live, halo)
    rank = lambda m: prefix(m.astype(F32), above).astype(jnp.int32)
    n_local = jnp.sum(is_local.astype(F32)).astype(jnp.int32)
    n_halo = jnp.sum(is_halo.astype(F32)).astype(jnp.int32)
    local_chunks = (n_local + chunk - 1) // chunk
    counts[0] = local_chunks
    counts[1] = local_chunks + (n_halo + chunk - 1) // chunk
    pos = jnp.where(is_local, rank(is_local), jnp.where(is_halo, rank(is_halo) + local_chunks * chunk, -1))
    s = jnp.where(halo, src - rows, src)
    half_w = w * 0.5
    w_a = half_w.astype(BF16).astype(F32)
    w_b = (half_w - w_a).astype(BF16).astype(F32)
    w_c = half_w - w_a - w_b
    high = ((s >> 8) * 8 + (d >> 8)).astype(F32)
    planes = [(s % BYTE).astype(F32), (d % BYTE).astype(F32), high, w_a, w_b, w_c]
    for i, p in enumerate(planes):
        values[i * lines : (i + 1) * lines, :] = p
    for i, p in enumerate((pos >> 7, pos & (LANES - 1), jnp.where(is_halo, s >> 7, -1), s & (LANES - 1))):
        places[i * lines : (i + 1) * lines, :] = p
    row = lambda i, q: pl.ds(i * lines + q, 1)
    spot = lambda size, i, q: (down((size, LANES)) == places[row(i, q), :]).astype(F32)
    hits[...] = jnp.zeros_like(hits)

    @pl.loop(0, lines, step=SUB)
    def _(base):
        acc = None
        for r in range(0, SUB, 2):
            lhs = stack_lanes([spot(hits.shape[0], 2, base + q) for q in (r, r + 1)]).astype(BF16)
            rhs = stack_lanes([spot(LANES, 3, base + q) for q in (r, r + 1)]).astype(BF16)
            part = dot(lhs, rhs, COLS_A)
            acc = part if acc is None else acc + part
        hits[...] += acc

    flags = (hits[...] > 0.0).astype(F32)
    used[...] = flags
    side = hits.shape[0] // 2
    most = jnp.maximum(jnp.sum(flags[:side], keepdims=True), jnp.sum(flags[side:], keepdims=True))
    mine[:SUB, :] = jnp.sum(mask[...].astype(F32).reshape(-1, *TILE), axis=0)
    mine[SUB:, :] = jnp.broadcast_to(most, TILE)
    met()
    copies = [remote(mine, theirs.at[o - 1], send_sem.at[o - 1], recv_sem.at[o - 1], lax.rem(me + o, n)) for o in range(1, n)]
    for c in copies:
        c.start()
    total[...] = jnp.zeros_like(total)

    @pl.loop(0, lines, step=SUB)
    def _(base):
        acc = None
        for r in range(0, SUB, 2):
            lhs, rhs = [], []
            for q in (base + r, base + r + 1):
                pick = down((slots, LANES)) == places[row(0, q), :]
                lhs.append(stack_rows([jnp.where(pick, values[row(i, q), :], 0.0) for i in range(len(planes))]))
                rhs.append(spot(LANES, 1, q))
            part = dot(stack_lanes(lhs).astype(BF16), stack_lanes(rhs).astype(BF16), COLS_A)
            acc = part if acc is None else acc + part
        total[...] += acc

    plane = lambda i: total[i * slots : (i + 1) * slots, :]
    high = plane(2).astype(jnp.int32)
    src_out[...] = ((high >> 3) * BYTE + plane(0).astype(jnp.int32)) * 2
    dst_out[...] = ((high & 7) * BYTE + plane(1).astype(jnp.int32)) * 2
    w_out[...] = (plane(3) + plane(4) + plane(5)) * 2.0
    for c in copies:
        c.wait()
    every = jnp.sum(mine[:SUB, :] + jnp.sum(theirs[:, :SUB, :], axis=0), keepdims=True)
    count[...] = jnp.maximum(jnp.broadcast_to(every, count.shape), 1.0)
    need[...] = jnp.maximum(mine[SUB:, :], jnp.max(theirs[:, SUB:, :], axis=0))


def local_kernel(chunk, backward, counts, src, dst, w, table, out, src_s, dst_s, sems, *accs):
    edges = Edges(0, counts[0], w, (src, dst), (src_s, dst_s), sems)
    edges.fetch()
    for a in accs:
        fill_zero(a)
    edges.walk(chunk, *((dst_s, src_s) if backward else (src_s, dst_s)), table, accs, True)

    @pl.loop(0, out.shape[0], step=STEP)
    def _(i):
        out[pl.ds(i, STEP), :] = functools.reduce(jnp.add, [a[pl.ds(i, STEP), :] for a in accs])


def forward_halo(chunk, edges, src_s, dst_s, from_prev, from_next, part, htab, accs, unpack):
    edges.fetch()
    unpack(from_prev, htab, 0)
    unpack(from_next, htab, htab.shape[0] // 4)
    copy_in(accs[0], part)
    for a in accs[1:]:
        fill_zero(a)
    edges.walk(chunk, src_s, dst_s, htab, accs, True)


def backward_halo(chunk, edges, src_s, dst_s, grad, back_prev, back_next, accs, wait, lists=None):
    for a in accs:
        fill_zero(a)
    edges.walk(chunk, dst_s, src_s, grad, accs, wait)
    split = accs[0].shape[0] // 2
    if lists is None:

        @pl.loop(0, back_prev.shape[0], step=BLOCK)
        def _(i):
            back_prev[pl.ds(i, BLOCK), :] = functools.reduce(jnp.add, [a[pl.ds(i, BLOCK), :] for a in accs])
            back_next[pl.ds(i, BLOCK), :] = functools.reduce(jnp.add, [a[pl.ds(split + i, BLOCK), :] for a in accs])
        return
    side = lists.shape[0] // 2
    half = (back_prev.shape[0] - side) // 3
    n = half // 2
    for k, out in enumerate((back_prev, back_next)):
        start = k * (split // 2)

        @pl.loop(0, half, step=n)
        def _(i):
            i = pl.multiple_of(i, n)
            pack_rows(out, i, half, *halves(accs, start + i, n), *halves(accs, start + half + i, n))

        out[3 * half : 3 * half + side, :] = lists[k * side : (k + 1) * side, :]


def padded(w, buf):
    low = w.shape[0] // SUB * SUB
    buf[low:, :] = jnp.zeros((buf.shape[0] - low, buf.shape[1]), F32)
    buf[0 : w.shape[0], :] = w[...]
    return buf[...].astype(BF16)


def hidden_kernel(chunk, counts, src, dst, w, send, from_prev, from_next, part, w2, hid, tab, to_prev, to_next, back, htab, tab_b, w2_pad, buf, idx, idx_sems, src_s, dst_s, sems, *accs):
    fetch = fetch_index(send, idx, idx_sems)
    for c in fetch:
        c.start()
    edges = Edges(counts[0], counts[1], w, (src, dst), (src_s, dst_s), sems)
    w2_b = padded(w2, w2_pad)
    per = send.shape[1] // LANES
    for i in range(2 * per):
        back[i : i + 1, :] = send[i // per : i // per + 1, (i % per) * LANES : (i % per + 1) * LANES] * 2
    forward_halo(chunk, edges, src_s, dst_s, from_prev, from_next, part, htab, accs, unpack_plain)

    @pl.loop(0, hid.shape[0], step=BLOCK)
    def _(i):
        even, odd = halves(accs, i, BLOCK)
        h = stack_lanes([jnp.maximum(even, 0.0), jnp.maximum(odd, 0.0)]).astype(BF16)
        hid[pl.ds(i, BLOCK), :] = h
        t = dot(h, w2_b, COLS_A).astype(BF16)
        tab_b[pl.ds(i, BLOCK), :] = t
        t = t.astype(F32)
        put_halves(tab, i, BLOCK, t[:, :LANES], t[:, LANES:])

    for c in fetch:
        c.wait()
    gather_packed(send, idx, tab_b, tab, buf, to_prev, to_next)


def loss_kernel(chunk, classes, counts, src, dst, w, src_back, lists, count, from_prev, from_next, part, labels, mask, loss, grad, back_prev, back_next, htab, src_s, dst_s, back_s, sems, *accs):
    edges = Edges(counts[0], counts[1], w, (src, dst, src_back), (src_s, dst_s, back_s), sems)
    forward_halo(chunk, edges, src_s, dst_s, from_prev, from_next, part, htab, accs, unpack_rows)
    lane = across(SQUARE)
    live = lane < classes - LANES
    scale = 1.0 / count[0:1, :]
    loss[...] = jnp.zeros_like(loss)

    @pl.loop(0, labels.shape[0] // 2)
    def _(pair):
        for b in (pair * 2, pair * 2 + 1):
            even, odd = halves(accs, b * LANES, LANES)
            label = spread(labels[pl.ds(b, 1), :])
            keep = spread(mask[pl.ds(b, 1), :]).astype(F32)
            odd = jnp.where(live, odd, -jnp.inf)
            top = jnp.max(jnp.maximum(even, odd), axis=1, keepdims=True)
            total = jnp.sum(jnp.exp(even - top) + jnp.exp(odd - top), axis=1, keepdims=True)
            norm = top + jnp.log(total)
            hit_even, hit_odd = lane == label, lane + LANES == label
            picked = jnp.where(hit_even, even, 0.0) + jnp.where(hit_odd, odd, 0.0)
            per_row = jnp.where(lane == 0, norm, 0.0) - picked
            loss[...] += jnp.sum((keep * per_row).reshape(LANES // SUB, *TILE), axis=0)
            d_even = (jnp.exp(even - norm) - hit_even.astype(F32)) * (keep * scale)
            d_odd = (jnp.exp(odd - norm) - hit_odd.astype(F32)) * (keep * scale)
            put_halves(grad, b * LANES, LANES, d_even, d_odd)

    backward_halo(chunk, edges, back_s, dst_s, grad, back_prev, back_next, accs, False, lists)


def take_returns(back, slots, counts, part, got_prev, got_next, accs):
    return_rows(back, slots, 0, counts[0], got_prev, accs)
    return_rows(back, slots, slots.shape[0] // 2, counts[1], got_next, accs)


def fetch_lines(lines, smem, sems):
    return [pltpu.make_async_copy(lines.at[i], smem.at[pl.ds(i * LANES, LANES)], sems.at[i]) for i in range(lines.shape[0])]


def middle_kernel(chunk, counts, src, dst, w, back, got_prev, got_next, part, hid, w2, grad_two, grad, back_prev, back_next, slots, n_back, returned, w2_pad, slot_s, slot_sems, src_s, dst_s, sems, *accs):
    edges = Edges(counts[0], counts[1], w, (src, dst), (src_s, dst_s), sems)
    edges.fetch()
    side = slots.shape[0] // 2
    half = (got_prev.shape[0] - side) // 3
    for k, got in enumerate((got_prev, got_next)):
        slot = got[3 * half :, :].astype(jnp.int32)
        slots[k * side : (k + 1) * side, :] = jnp.maximum(slot, 0) + (1 - k) * side * LANES
        n_back[k] = jnp.sum((slot >= 0).astype(F32)).astype(jnp.int32)
    w2_b = padded(w2, w2_pad)
    unpack_rows(got_prev, returned, 0, half)
    unpack_rows(got_next, returned, 2 * half, half)
    fetch = fetch_lines(slots, slot_s, slot_sems)
    for c in fetch:
        c.start()
    copy_in(accs[0], part)
    for a in accs[1:]:
        fill_zero(a)
    for c in fetch:
        c.wait()
    take_returns(back, slot_s, n_back, part, returned.at[pl.ds(0, 4 * half)], returned.at[pl.ds(4 * half, 4 * half)], accs)
    grad_two[...] = jnp.zeros_like(grad_two)

    @pl.loop(0, hid.shape[0], step=BLOCK)
    def _(i):
        even, odd = halves(accs, i, BLOCK)
        d_tab = stack_lanes([even, odd]).astype(BF16)
        h = hid[pl.ds(i, BLOCK), :]
        grad_two[...] += dot(d_tab, h, ROWS_A)
        d_hid = dot(d_tab, w2_b)
        d_pre = jnp.where(h > 0, d_hid, 0.0)
        put_halves(grad, i, BLOCK, d_pre[:, :LANES], d_pre[:, LANES:])

    backward_halo(chunk, edges, src_s, dst_s, grad, back_prev, back_next, accs, True)


def last_kernel(back, n_back, slots, got_prev, got_next, part, x, grad_one, slot_s, slot_sems, *accs):
    fetch = fetch_lines(slots, slot_s, slot_sems)
    for c in fetch:
        c.start()
    copy_in(accs[0], part)
    for a in accs[1:]:
        fill_zero(a)
    for c in fetch:
        c.wait()
    take_returns(back, slot_s, n_back, part, got_prev, got_next, accs)
    grad_one[...] = jnp.zeros_like(grad_one)

    @pl.loop(0, x.shape[0], step=BLOCK)
    def _(i):
        even, odd = halves(accs, i, BLOCK)
        d_tab = stack_lanes([even, odd]).astype(BF16)
        grad_one[...] += dot(x[pl.ds(i, BLOCK), :], d_tab, ROWS_A)


def call(body, name, outs, ins, scratch, out_specs=None, collective=None, vmem=14):
    extra = {} if collective is None else dict(collective_id=collective, has_side_effects=True)
    return pl.pallas_call(
        body, name=name, out_shape=outs, in_specs=ins, out_specs=out_specs or jax.tree.map(lambda _: VMEM, outs),
        scratch_shapes=[pltpu.VMEM(s, F32) if isinstance(s, tuple) else s for s in scratch],
        compiler_params=pltpu.CompilerParams(vmem_limit_bytes=vmem * 2**20, **extra),
        cost_estimate=pl.CostEstimate(flops=10**10, bytes_accessed=10**7, transcendentals=0),
    )


def solution(mesh):
    num_dev = mesh.shape[AXIS]
    to_next = [(d, (d + 1) % num_dev) for d in range(num_dev)]
    to_prev = [(d, (d - 1) % num_dev) for d in range(num_dev)]

    def step(x, w_one, w_two, send, edge_src, edge_dst, edge_w, labels, mask):
        rows, halo, edges, classes = x.shape[0], send.shape[1], edge_src.shape[0], w_two.shape[1]
        tab, half, w2_pad = (2 * rows, LANES), (2 * halo, LANES), (2 * LANES, 2 * LANES)
        sds = jax.ShapeDtypeStruct
        tab_f = sds(tab, F32)
        half_b, pack_b = sds((halo, 2 * LANES), BF16), sds((3 * halo // 2, LANES), BF16)
        tab_b = pltpu.VMEM((rows, 2 * LANES), BF16)
        one = sds(TILE, F32)
        dma = pltpu.SemaphoreType.DMA
        chunk_l, chunk_h = 64, 32
        lines = edges // LANES
        slots = lines + 8
        side = halo // LANES
        w2 = w_two.T
        mask = mask.reshape(-1, LANES)
        labels = labels.reshape(-1, LANES)
        packed = jnp.concatenate([(edge_src * 2048 + edge_dst).astype(F32), edge_w]).reshape(2 * lines, LANES)
        ints = sds((slots, LANES), jnp.int32)
        sided = sds((2 * side, LANES), F32)
        src, dst, w_lines, used, counts, count, need = call(
            functools.partial(prep_kernel, num_dev, PREP_CHUNK, rows), "prep",
            [ints, ints, sds((slots, LANES), F32), sided, sds((2,), jnp.int32), one, one], [VMEM] * 2,
            [(6 * slots, LANES), (6 * lines, LANES), pltpu.VMEM((4 * lines, LANES), jnp.int32), sided.shape, (16, LANES), (num_dev - 1, 16, LANES)]
            + [dma((num_dev - 1,))] * 2,
            out_specs=[VMEM] * 4 + [SMEM, VMEM, VMEM], vmem=8, collective=0,
        )(packed, mask)

        def run(limit):
            compact = limit < halo
            pack_f, half_f = sds((3 * limit // 2 + side, LANES), F32), sds((2 * limit, LANES), F32)
            list_s = [pltpu.SMEM((halo,), jnp.int32), dma((side,))]
            tab_one, to_p, to_n, w, src_back, lists = call(
                functools.partial(first_kernel, compact, halo), "first", [tab_f, half_b, half_b, sds((slots * LANES, LANES), F32), ints, sided],
                [VMEM] * 3 + [SMEM] + [VMEM] * 3, [tab_b, half] + list_s, vmem=8,
            )(x, w_one, send, counts, src, w_lines, used)
            from_prev = lax.ppermute(to_n, AXIS, to_next)
            from_next = lax.ppermute(to_p, AXIS, to_prev)
            flat, flat_dst, flat_back = src.reshape(-1), dst.reshape(-1), src_back.reshape(-1)

            walk = [SMEM, ANY, ANY, VMEM]
            index = pltpu.SMEM((slots * LANES,), jnp.int32)
            walk_s = lambda n: [index] * n + [dma((n, slots * LANES // SEGMENT))]
            slot_s = [pltpu.SMEM((2 * halo,), jnp.int32), dma((2 * side,))]
            local, local_back = (
                call(functools.partial(local_kernel, chunk_l, back), "local_edges", tab_f, walk + [VMEM], walk_s(2) + [tab] * 4)
                for back in (False, True)
            )
            part = local(counts, flat, flat_dst, w, tab_one)
            hid, tab_two, to_p, to_n, back = call(
                functools.partial(hidden_kernel, chunk_h), "hidden",
                [sds((rows, 2 * LANES), BF16), tab_f, pack_b, pack_b, sds((2 * side, LANES), jnp.int32)],
                walk + [VMEM] * 5, [tab, tab_b, w2_pad, half] + list_s + walk_s(2) + [tab] * 4,
            )(counts, flat, flat_dst, w, send, from_prev, from_next, part, w2)
            from_prev = lax.ppermute(to_n, AXIS, to_next)
            from_next = lax.ppermute(to_p, AXIS, to_prev)
            back = back.reshape(-1)
            part = local(counts, flat, flat_dst, w, tab_two)
            loss, grad, to_p, to_n = call(
                functools.partial(loss_kernel, chunk_h, classes), "loss", [one, tab_f, pack_f, pack_f],
                walk + [ANY] + [VMEM] * 7, [tab] + walk_s(3) + [tab] * 4,
            )(counts, flat, flat_dst, w, flat_back, lists, count, from_prev, from_next, part, labels, mask)
            got_prev = lax.ppermute(to_p, AXIS, to_prev)
            got_next = lax.ppermute(to_n, AXIS, to_next)
            part = local_back(counts, flat, flat_dst, w, grad)
            grad_two, grad, to_p, to_n, slot, n_back = call(
                functools.partial(middle_kernel, chunk_h), "middle",
                [sds(w2_pad, F32), tab_f, half_f, half_f, sds((2 * side, LANES), jnp.int32), sds((2,), jnp.int32)],
                walk + [SMEM] + [VMEM] * 5, [(4 * limit, LANES), w2_pad] + slot_s + walk_s(2) + [tab] * 4, out_specs=[VMEM] * 5 + [SMEM],
            )(counts, flat_back, flat_dst, w, back, got_prev, got_next, part, hid, w2)
            got_prev = lax.ppermute(to_p, AXIS, to_prev)
            got_next = lax.ppermute(to_n, AXIS, to_next)
            part = local_back(counts, flat, flat_dst, w, grad)
            grad_one = call(
                last_kernel, "last", sds((x.shape[1], 2 * LANES), F32), [SMEM, SMEM, ANY] + [VMEM] * 4, slot_s + [tab] * 4
            )(back, n_back, slot, got_prev, got_next, part, x)
            return grad_one, grad_two, loss

        few = halo * 5 // 8
        grad_one, grad_two, loss = lax.cond(need[0, 0] > few, lambda: run(halo), lambda: run(few))
        unit = SUB * num_dev
        lines = 2 * (x.shape[1] + -(-classes // SUB) * SUB) + SUB
        lines = -(-lines // unit) * unit
        grad_one, grad_two, mean = call(
            functools.partial(reduce_kernel, num_dev), "reduce", [sds(grad_one.shape, F32), sds((classes, 2 * LANES), F32), sds((1, 1), F32)],
            [VMEM] * 4, [(lines, LANES), (lines, LANES), (lines // 2, LANES), (num_dev // 2 - 1, lines // num_dev, LANES), dma((2, num_dev))],
            collective=1, vmem=8,
        )(grad_one, grad_two, loss, count)
        return mean.reshape(()), grad_one, grad_two.T

    row = P(AXIS)
    return jax.shard_map(
        step, mesh=mesh, in_specs=(row, P(), P(), row, row, row, row, row, row), out_specs=(P(), P(), P()), check_vma=False
    )
```

time: 140 us -> 126 us (0.900); the launches traced: 141 us -> 125 us
  Pallas kernels: 104 us -> 81.9 us
  starting transfers between devices: 10.2 us -> 15 us
    pallas_call x9, Pallas kernels: 78.1 us -> 56.6 us  [the longest x2 12 us: run(): part = local_back(counts, flat, flat_dst, w, grad)]
    ppermute x8, starting transfers between devices: 10.2 us -> 15 us  [the longest x2 7.86 us: run(): got_prev = lax.ppermute(to_p, AXIS, to_prev)]
  transfers between devices with their start and end apart: 8 -> 8, of which waited for: 3 -> 4; matrix products, arithmetic and copies ran while one was open for 0% -> 0% of each run, Pallas kernels for 28% -> 19%
where the time goes in v3:
time: 126 us; the launch traced here: 125 us
  Pallas kernels  81.9 us (65%)
  waiting for transfers between devices  21.5 us (17%)
  starting transfers between devices  15 us (12%)
  between operations  3.13 us (2%)
  local copies, waits for them, and re-layouts  1.87 us (1%)
  other arithmetic  1.55 us (1%)
    pallas_call x1, Pallas kernels, step(): call(functools.partial(reduce_kernel, num_dev), 'reduce', [sds(grad_one.s...  14.6 us
    ppermute x2, waiting for transfers between devices, run(): got_prev = lax.ppermute(to_p, AXIS, to_prev)  12.6 us
    pallas_call x2, Pallas kernels, run(): part = local_back(counts, flat, flat_dst, w, grad)  12 us
    pallas_call x1, Pallas kernels, step(): call(functools.partial(prep_kernel, num_dev, PREP_CHUNK, rows), 'prep', [...  10.6 us
    ppermute x2, waiting for transfers between devices, run(): from_prev = lax.ppermute(to_n, AXIS, to_next)  8.91 us
    ppermute x2, starting transfers between devices, run(): got_prev = lax.ppermute(to_p, AXIS, to_prev)  7.86 us
    pallas_call x1, Pallas kernels, run(): call(functools.partial(middle_kernel, chunk_h), 'middle', [sds(w2_pad, F3...  7.66 us
    pallas_call x1, Pallas kernels, run(): call(functools.partial(first_kernel, compact, halo), 'first', [tab_f, hal...  7.02 us
  transfers between devices with their start and end apart: 8, of which 4 were waited for; matrix products, arithmetic and copies ran while one was open for 0% of the time, Pallas kernels for 19%

profile of v3, /device:TPU:0, one launch (start us, length us, event | category | flops | bytes accessed | tf_op | source)
XLA Modules:
  0.0 125.3 jit_solution(13118151599916786466)
XLA Ops:
  0.6 0.8 convert_bitcast_fusion
  1.4 0.8 pad_maximum_fusion.packed
  2.2 0.0 copy-start
  2.2 0.0 copy-start.1
  2.2 0.0 copy-start.2
  2.2 0.0 copy-start.3
  2.2 0.0 copy-start.4
  2.2 0.0 copy-start.5
  2.2 10.6 %prep.1 = (s32[72,128]{1,0:T(8,128)S(1)}, s32[72,128]{1,0:T(8,128)S(1)}, f32[72,128]{1,0:T(8,128)S(1)}, f32[16,128]{1,0:T(8,128)S(1)}, s32[2]{0:T(128)S(1)}, /*index=5*/f32[8,128]{1,0:T(8,128)S(1)}, f32[8,128]{1,0:T(8,128)S(1)}) custom-call(f32[128,128]{1,0:T(8,128)S(1)} %pad_maximum_fusion.packed, s32[16,128]{1,0:T(8,128)} %bitcast.29), custom_call_target="tpu_custom_call" | custom-call | flops 10000000000 | bytes 10000000 | tf_op jit(solution)/shard_map/prep/pallas_call | solution.py:659
  12.9 0.5 slice.3
  14.0 0.0 copy-done
  14.1 0.0 copy-done.1
  14.1 0.0 copy-done.2
  14.1 0.0 copy-done.3
  14.1 0.0 copy-done.4
  14.1 0.0 copy-done.5
  14.1 93.5 %conditional.1 = (f32[128,256]{1,0:T(8,128)S(1)}, f32[256,256]{1,0:T(8,128)S(1)}, f32[8,128]{1,0:T(8,128)S(1)}) conditional(s32[]{:T(128)} %bitcast.11, (s32[72,128]{1,0:T(8,128)S(1)}, s32[72,128]{1,0:T(8,128)S(1)}, bf16[2048,128]{1,0:T(8,128)(2,1)S(1)}, f32[128,256]{1,0:T(8,128)S(1)}, s32[2,1024]{1,0:T(2,128)S(1)}, /*index=5*/s32[2]{0:T(128)S(1)}, ...), branch_computations={%region_0.0_spmd, %region_1.0_spmd} | conditional | flops 89999998976 | bytes 112053208 | solution.py:718
  14.1 7.0 %first.2 = (f32[4096,128]{1,0:T(8,128)S(1)}, bf16[1024,256]{1,0:T(8,128)(2,1)S(1)}, bf16[1024,256]{1,0:T(8,128)(2,1)S(1)}, f32[9216,128]{1,0:T(8,128)S(1)}, s32[...) custom-call(bf16[2048,128]{1,0:T(8,128)(2,1)S(1)} %get-tuple-element.51.x, f32[128,256]{1,0:T(8,128)S(1)} %get-tuple-element.52.w1, ...), custom_call_target="tpu_custom_call" | custom-call | flops 10000000000 | bytes 10000000 | tf_op jit(solution)/shard_map/cond/branch_0_fun/first/pallas_call | solution.py:671
  21.1 0.8 collective-permute-start
  21.9 2.8 %collective-permute-start.1 = (bf16[1024,256]{1,0:T(8,128)(2,1)S(1)}, bf16[1024,256]{1,0:T(8,128)(2,1)S(1)}, u32[]{:S(2)}, u32[]{:S(2)}) collective-permute-start(bf16[1024,256]{1,0:T(8,128)(2,1)S(1)} %get-tuple-element.58), channel_id=1, source_target_pairs={{0,15},{1,0},{2,1},{3,2},{4,3},{5,4},{6,5},{7,6},{8,7},{9,8},{10,9... | collective-permute-start | bytes 1572872 | tf_op jit(solution)/shard_map/cond/branch_0_fun/ppermute | solution.py:676
  24.7 6.0 %local_edges.8.part = f32[4096,128]{1,0:T(8,128)S(1)} custom-call(s32[2]{0:T(128)S(1)} %get-tuple-element.48.counts, s32[9216]{0:T(1024)S(1)} %bitcast.34, s32[9216]{0:T(1024)S(1)} %bitcast.46, f32[9216,128]{1,0:T(8,128)S(1)} %get-tuple-element.56.w, f32[4096,128]{1,0:T(8,128)S(1)} %get-tuple-element.59.table), custom_call_target="tpu_custom_call" | custom-call | flops 10000000000 | bytes 10000000 | tf_op jit(solution)/shard_map/cond/branch_0_fun/local_edges/pallas_call | solution.py:687
  30.7 5.6 %collective-permute-done.from_prev = bf16[1024,256]{1,0:T(8,128)(2,1)S(1)} collective-permute-done((bf16[1024,256]{1,0:T(8,128)(2,1)S(1)}, bf16[1024,256]{1,0:T(8,128)(2,1)S(1)}, u32[]{:S(2)}, u32[]{:S(2)}) %collective-permute-start) | collective-permute-done | bytes 524320 | tf_op jit(solution)/shard_map/cond/branch_0_fun/ppermute | solution.py:675
  36.3 0.0 collective-permute-done.1.from_next
  36.3 7.0 %hidden.2 = (bf16[2048,256]{1,0:T(8,128)(2,1)S(1)}, f32[4096,128]{1,0:T(8,128)S(1)}, bf16[1536,128]{1,0:T(8,128)(2,1)S(1)}, bf16[1536,128]{1,0:T(8,128)(2,1)S(1)}, s32[16,128]{1,0:T(8,128)S(1)}) custom-call(s32[2]{0:T(128)S(1)} %get-tuple-element.48.counts, s32[9216]{0:T(1024)S(1)} %bitcast.35, s32[9216]{0:T(1024)S(1)} %bitcast.47, ...), custom_call_target="tpu_custom_call" | custom-call | flops 10000000000 | bytes 10000000 | tf_op jit(solution)/shard_map/cond/branch_0_fun/hidden/pallas_call | solution.py:688
  43.2 0.9 collective-permute-start.2
  44.1 2.7 %collective-permute-start.3 = (bf16[1536,128]{1,0:T(8,128)(2,1)S(1)}, bf16[1536,128]{1,0:T(8,128)(2,1)S(1)}, u32[]{:S(2)}, u32[]{:S(2)}) collective-permute-start(bf16[1536,128]{1,0:T(8,128)(2,1)S(1)} %get-tuple-element.66), channel_id=1, source_target_pairs={{0,15},{1,0},{2,1},{3,2},{4,3},{5,4},{6,5},{7,6},{8,7},{9,8},{10,9... | collective-permute-start | bytes 1179656 | tf_op jit(solution)/shard_map/cond/branch_0_fun/ppermute | solution.py:694
  46.8 6.0 %local_edges.9.part = f32[4096,128]{1,0:T(8,128)S(1)} custom-call(s32[2]{0:T(128)S(1)} %get-tuple-element.48.counts, s32[9216]{0:T(1024)S(1)} %bitcast.36, s32[9216]{0:T(1024)S(1)} %bitcast.48, f32[9216,128]{1,0:T(8,128)S(1)} %get-tuple-element.56.w, f32[4096,128]{1,0:T(8,128)S(1)} %get-tuple-element.67.table), custom_call_target="tpu_custom_call" | custom-call | flops 10000000000 | bytes 10000000 | tf_op jit(solution)/shard_map/cond/branch_0_fun/local_edges/pallas_call | solution.py:696
  52.8 3.4 %collective-permute-done.2.from_prev = bf16[1536,128]{1,0:T(8,128)(2,1)S(1)} collective-permute-done((bf16[1536,128]{1,0:T(8,128)(2,1)S(1)}, bf16[1536,128]{1,0:T(8,128)(2,1)S(1)}, u32[]{:S(2)}, u32[]{:S(2)}) %collective-permute-start.2) | collective-permute-done | bytes 393248 | tf_op jit(solution)/shard_map/cond/branch_0_fun/ppermute | solution.py:693
  56.2 0.0 collective-permute-done.3.from_next
  56.2 6.7 %loss.2 = (f32[8,128]{1,0:T(8,128)S(1)}, f32[4096,128]{1,0:T(8,128)S(1)}, f32[968,128]{1,0:T(8,128)S(1)}, f32[968,128]{1,0:T(8,128)S(1)}) custom-call(s32[2]{0:T(128)S(1)} %get-tuple-element.48.counts, s32[9216]{0:T(1024)S(1)} %bitcast.37, s32[9216]{0:T(1024)S(1)} %bitcast.49, f32[9216,128]{1,0:T(8,128)S(1)} %get-tuple-element.56.w, s32[9216]{0:T(1024)S(1)} %bitcast.18, ...), custom_call_target="tpu_custom_call" | custom-call | flops 10000000000 | bytes 10000000 | tf_op jit(solution)/shard_map/cond/branch_0_fun/loss/pallas_call | solution.py:697
  62.9 3.7 %collective-permute-start.4 = (f32[968,128]{1,0:T(8,128)S(1)}, f32[968,128]{1,0:T(8,128)S(1)}, u32[]{:S(2)}, u32[]{:S(2)}) collective-permute-start(f32[968,128]{1,0:T(8,128)S(1)} %get-tuple-element.70), channel_id=1, source_target_pairs={{0,15},{1,0},{2,1},{3,2},{4,3},{5,4},{6,5},{7,6},{8,7},{9,8},{10,9... | collective-permute-start | bytes 1486856 | tf_op jit(solution)/shard_map/cond/branch_0_fun/ppermute | solution.py:701
  66.6 0.0 collective-permute-start.5
  66.6 6.0 %local_edges.10.part = f32[4096,128]{1,0:T(8,128)S(1)} custom-call(s32[2]{0:T(128)S(1)} %get-tuple-element.48.counts, s32[9216]{0:T(1024)S(1)} %bitcast.38, s32[9216]{0:T(1024)S(1)} %bitcast.50, f32[9216,128]{1,0:T(8,128)S(1)} %get-tuple-element.56.w, f32[4096,128]{1,0:T(8,128)S(1)} %get-tuple-element.72.table), custom_call_target="tpu_custom_call" | custom-call | flops 10000000000 | bytes 10000000 | tf_op jit(solution)/shard_map/cond/branch_0_fun/local_edges/pallas_call | solution.py:703
  72.6 5.1 %collective-permute-done.4.got_prev = f32[968,128]{1,0:T(8,128)S(1)} collective-permute-done((f32[968,128]{1,0:T(8,128)S(1)}, f32[968,128]{1,0:T(8,128)S(1)}, u32[]{:S(2)}, u32[]{:S(2)}) %collective-permute-start.4) | collective-permute-done | bytes 495648 | tf_op jit(solution)/shard_map/cond/branch_0_fun/ppermute | solution.py:701
  77.7 0.0 collective-permute-done.5.got_next
  77.7 7.7 %middle.2 = (f32[256,256]{1,0:T(8,128)S(1)}, f32[4096,128]{1,0:T(8,128)S(1)}, f32[1280,128]{1,0:T(8,128)S(1)}, f32[1280,128]{1,0:T(8,128)S(1)}, s32[16,128]{1,0:T(8,128)S(1)}, /*index=5*/s32[2]{0:T(128)S(1)}) custom-call(s32[2]{0:T(128)S(1)} %get-tuple-element.48.counts, s32[9216]{0:T(1024)S(1)} %bitcast.19, s32[9216]{0:T(1024)S(1)} %bitcast.51, ...), custom_call_target="tpu_custom_call" | custom-call | flops 10000000000 | bytes 10000000 | tf_op jit(solution)/shard_map/cond/branch_0_fun/middle/pallas_call | solution.py:704
  85.3 4.2 %collective-permute-start.6 = (f32[1280,128]{1,0:T(8,128)S(1)}, f32[1280,128]{1,0:T(8,128)S(1)}, u32[]{:S(2)}, u32[]{:S(2)}) collective-permute-start(f32[1280,128]{1,0:T(8,128)S(1)} %get-tuple-element.76), channel_id=1, source_target_pairs={{0,15},{1,0},{2,1},{3,2},{4,3},{5,4},{6,5},{7,6},{8,7},{9,8},{10,9... | collective-permute-start | bytes 1966088 | tf_op jit(solution)/shard_map/cond/branch_0_fun/ppermute | solution.py:709
  89.5 0.0 collective-permute-start.7
  89.5 6.0 %local_edges.11.part = f32[4096,128]{1,0:T(8,128)S(1)} custom-call(s32[2]{0:T(128)S(1)} %get-tuple-element.48.counts, s32[9216]{0:T(1024)S(1)} %bitcast.39, s32[9216]{0:T(1024)S(1)} %bitcast.52, f32[9216,128]{1,0:T(8,128)S(1)} %get-tuple-element.56.w, f32[4096,128]{1,0:T(8,128)S(1)} %get-tuple-element.78.table), custom_call_target="tpu_custom_call" | custom-call | flops 10000000000 | bytes 10000000 | tf_op jit(solution)/shard_map/cond/branch_0_fun/local_edges/pallas_call | solution.py:711
  95.5 7.5 %collective-permute-done.6.got_prev = f32[1280,128]{1,0:T(8,128)S(1)} collective-permute-done((f32[1280,128]{1,0:T(8,128)S(1)}, f32[1280,128]{1,0:T(8,128)S(1)}, u32[]{:S(2)}, u32[]{:S(2)}) %collective-permute-start.6) | collective-permute-done | bytes 655392 | tf_op jit(solution)/shard_map/cond/branch_0_fun/ppermute | solution.py:709
  103.0 0.0 collective-permute-done.7.got_next
  103.0 4.4 %last.2 = f32[128,256]{1,0:T(8,128)S(1)} custom-call(s32[2048]{0:T(1024)S(1)} %bitcast.23, s32[2]{0:T(128)S(1)} %get-tuple-element.74.n_back, s32[16,128]{1,0:T(8,128)S(1)} %get-tuple-element.75.slots, f32[1280,128]{1,0:T(8,128)S(1)} %collective-permute-done.6.got_prev, f32[1280,128]{1,0:T(8,128)S(1)} %collective-permute-done.7.got_next, ...), custom_call_target="tpu_custom_call" | custom-call | flops 10000000000 | bytes 10000000 | tf_op jit(solution)/shard_map/cond/branch_0_fun/last/pallas_call | solution.py:712
  107.6 14.6 %reduce.1 = (f32[128,256]{1,0:T(8,128)S(1)}, f32[172,256]{1,0:T(8,128)S(1)}, f32[1,1]{1,0:T(1,128)}) custom-call(f32[128,256]{1,0:T(8,128)S(1)} %get-tuple-element.137.one, f32[256,256]{1,0:T(8,128)S(1)} %get-tuple-element.138.two, f32[8,128]{1,0:T(8,128)S(1)} %get-tuple-element.139.loss, f32[8,128]{1,0:T(8,128)S(1)} %get-tuple-element.136.count), custom_call_target="tpu_custom_call" | custom-call | flops 10000000000 | bytes 10000000 | tf_op jit(solution)/shard_map/reduce/pallas_call | solution.py:722
  122.8 0.7 copy.22
  123.5 0.7 copy.23
Async XLA Ops:
  2.2 11.9 %copy-start = (bf16[2048,128]{1,0:T(8,128)(2,1)S(1)}, bf16[2048,128]{1,0:T(8,128)(2,1)}, u32[]{:S(2)}) copy-start(bf16[2048,128]{1,0:T(8,128)(2,1)} %param.11) | copy-start | bytes 1572868
  2.2 11.9 %copy-start.1 = (f32[256,172]{0,1:T(8,128)S(1)}, f32[256,172]{0,1:T(8,128)}, u32[]{:S(2)}) copy-start(f32[256,172]{0,1:T(8,128)} %param.13) | copy-start | bytes 528388
  2.2 11.9 %copy-start.2 = (f32[128,256]{1,0:T(8,128)S(1)}, f32[128,256]{1,0:T(8,128)}, u32[]{:S(2)}) copy-start(f32[128,256]{1,0:T(8,128)} %param.12) | copy-start | bytes 393220
  2.2 11.9 %copy-start.3 = (s32[2048]{0:T(1024)S(1)}, s32[2048]{0:T(1024)}, u32[]{:S(2)}) copy-start(s32[2048]{0:T(1024)} %param.19) | copy-start | bytes 24580
  2.2 11.9 %copy-start.4 = (s32[2,1024]{1,0:T(2,128)S(1)}, s32[2,1024]{1,0:T(2,128)}, u32[]{:S(2)}) copy-start(s32[2,1024]{1,0:T(2,128)} %param.14) | copy-start | bytes 24580
  2.2 11.9 %copy-start.5 = (s32[2048]{0:T(1024)S(1)}, s32[2048]{0:T(1024)}, u32[]{:S(2)}) copy-start(s32[2048]{0:T(1024)} %param.18) | copy-start | bytes 24580
  21.1 15.1 %collective-permute-start = (bf16[1024,256]{1,0:T(8,128)(2,1)S(1)}, bf16[1024,256]{1,0:T(8,128)(2,1)S(1)}, u32[]{:S(2)}, u32[]{:S(2)}) collective-permute-start(bf16[1024,256]{1,0:T(8,128)(2,1)S(1)} %get-tuple-element.57), channel_id=1, source_target_pairs={{0,1},{1,2},{2,3},{3,4},{4,5},{5,6},{6,7},{7,8},{8,9},{9,10},{10,1... | collective-permute-start | bytes 1572872 | tf_op jit(solution)/shard_map/cond/branch_0_fun/ppermute | solution.py:675
  21.9 14.4 %collective-permute-start.1 = (bf16[1024,256]{1,0:T(8,128)(2,1)S(1)}, bf16[1024,256]{1,0:T(8,128)(2,1)S(1)}, u32[]{:S(2)}, u32[]{:S(2)}) collective-permute-start(bf16[1024,256]{1,0:T(8,128)(2,1)S(1)} %get-tuple-element.58), channel_id=1, source_target_pairs={{0,15},{1,0},{2,1},{3,2},{4,3},{5,4},{6,5},{7,6},{8,7},{9,8},{10,9... | collective-permute-start | bytes 1572872 | tf_op jit(solution)/shard_map/cond/branch_0_fun/ppermute | solution.py:676
  43.2 12.9 %collective-permute-start.2 = (bf16[1536,128]{1,0:T(8,128)(2,1)S(1)}, bf16[1536,128]{1,0:T(8,128)(2,1)S(1)}, u32[]{:S(2)}, u32[]{:S(2)}) collective-permute-start(bf16[1536,128]{1,0:T(8,128)(2,1)S(1)} %get-tuple-element.65), channel_id=1, source_target_pairs={{0,1},{1,2},{2,3},{3,4},{4,5},{5,6},{6,7},{7,8},{8,9},{9,10},{10,1... | collective-permute-start | bytes 1179656 | tf_op jit(solution)/shard_map/cond/branch_0_fun/ppermute | solution.py:693
  44.1 12.1 %collective-permute-start.3 = (bf16[1536,128]{1,0:T(8,128)(2,1)S(1)}, bf16[1536,128]{1,0:T(8,128)(2,1)S(1)}, u32[]{:S(2)}, u32[]{:S(2)}) collective-permute-start(bf16[1536,128]{1,0:T(8,128)(2,1)S(1)} %get-tuple-element.66), channel_id=1, source_target_pairs={{0,15},{1,0},{2,1},{3,2},{4,3},{5,4},{6,5},{7,6},{8,7},{9,8},{10,9... | collective-permute-start | bytes 1179656 | tf_op jit(solution)/shard_map/cond/branch_0_fun/ppermute | solution.py:694
  62.9 14.8 %collective-permute-start.4 = (f32[968,128]{1,0:T(8,128)S(1)}, f32[968,128]{1,0:T(8,128)S(1)}, u32[]{:S(2)}, u32[]{:S(2)}) collective-permute-start(f32[968,128]{1,0:T(8,128)S(1)} %get-tuple-element.70), channel_id=1, source_target_pairs={{0,15},{1,0},{2,1},{3,2},{4,3},{5,4},{6,5},{7,6},{8,7},{9,8},{10,9... | collective-permute-start | bytes 1486856 | tf_op jit(solution)/shard_map/cond/branch_0_fun/ppermute | solution.py:701
  66.6 11.1 %collective-permute-start.5 = (f32[968,128]{1,0:T(8,128)S(1)}, f32[968,128]{1,0:T(8,128)S(1)}, u32[]{:S(2)}, u32[]{:S(2)}) collective-permute-start(f32[968,128]{1,0:T(8,128)S(1)} %get-tuple-element.71), channel_id=1, source_target_pairs={{0,1},{1,2},{2,3},{3,4},{4,5},{5,6},{6,7},{7,8},{8,9},{9,10},{10,1... | collective-permute-start | bytes 1486856 | tf_op jit(solution)/shard_map/cond/branch_0_fun/ppermute | solution.py:702
  85.3 17.7 %collective-permute-start.6 = (f32[1280,128]{1,0:T(8,128)S(1)}, f32[1280,128]{1,0:T(8,128)S(1)}, u32[]{:S(2)}, u32[]{:S(2)}) collective-permute-start(f32[1280,128]{1,0:T(8,128)S(1)} %get-tuple-element.76), channel_id=1, source_target_pairs={{0,15},{1,0},{2,1},{3,2},{4,3},{5,4},{6,5},{7,6},{8,7},{9,8},{10,9... | collective-permute-start | bytes 1966088 | tf_op jit(solution)/shard_map/cond/branch_0_fun/ppermute | solution.py:709
  89.5 13.5 %collective-permute-start.7 = (f32[1280,128]{1,0:T(8,128)S(1)}, f32[1280,128]{1,0:T(8,128)S(1)}, u32[]{:S(2)}, u32[]{:S(2)}) collective-permute-start(f32[1280,128]{1,0:T(8,128)S(1)} %get-tuple-element.77), channel_id=1, source_target_pairs={{0,1},{1,2},{2,3},{3,4},{4,5},{5,6},{6,7},{7,8},{8,9},{9,10},{10,1... | collective-permute-start | bytes 1966088 | tf_op jit(solution)/shard_map/cond/branch_0_fun/ppermute | solution.py:710

commit v4 on v3

--- a/solution.py
+++ b/solution.py
@@ -31,11 +31,11 @@
 
 
 def fill_zero(ref):
-    zero = jnp.zeros((STEP, LANES), F32)
-
-    @pl.loop(0, ref.shape[0], step=STEP)
-    def _(i):
-        ref[pl.ds(i, STEP), :] = zero
+    zero = jnp.zeros((BLOCK, LANES), F32)
+
+    @pl.loop(0, ref.shape[0], step=BLOCK)
+    def _(i):
+        ref[pl.ds(i, BLOCK), :] = zero
 
 
 def copy_in(dst, src):
@@ -245,17 +245,21 @@
     low, high = rank & (LANES - 1), rank >> 7
     table = stack_rows([low.astype(F32), high.astype(F32)]).astype(BF16)
 
-    def line(r, _):
-        slot = src[pl.ds(r, 1), :] >> 1
-        h, l = slot >> 7, slot & (LANES - 1)
-        got = dot(table, (down(SQUARE) == l).astype(F32).astype(BF16))
-        got = jnp.where(down((lines, LANES)) == h, got[:lines] + LANES * got[lines:], 0.0)
-        got = jnp.sum(got, axis=0, keepdims=True).astype(jnp.int32)
-        src_back[pl.ds(r, 1), :] = (got + jnp.where(h >= side, halo, 0)) * 2
+    quad = 4
+
+    def four(c, _):
+        slot = [src[pl.ds(c * quad + q, 1), :] >> 1 for q in range(quad)]
+        spots = stack_lanes([(down(SQUARE) == (t & (LANES - 1))).astype(F32) for t in slot]).astype(BF16)
+        got = dot(table, spots)
+        h = stack_lanes(slot) >> 7
+        got = jnp.where(down(got[:lines].shape) == h, got[:lines] + LANES * got[lines:], 0.0)
+        got = (jnp.sum(got, axis=0, keepdims=True).astype(jnp.int32) + jnp.where(h >= side, halo, 0)) * 2
+        for q in range(quad):
+            src_back[pl.ds(c * quad + q, 1), :] = got[:, q * LANES : (q + 1) * LANES]
         return 0
 
-    ratio = LANES // PREP_CHUNK
-    lax.fori_loop(counts[0] // ratio, (counts[1] + ratio - 1) // ratio, line, 0)
+    ratio = quad * LANES // PREP_CHUNK
+    lax.fori_loop(counts[0] // ratio, (counts[1] + ratio - 1) // ratio, four, 0)
     for k in range(2):
         acc = jnp.zeros((24, LANES), F32)
         for hh in range(side):
@@ -335,33 +339,39 @@
 
     half = work.shape[0] // 2
     piece = half // chips
-    rows = lambda start, size: pl.ds(pl.multiple_of(start, SUB), size)
-    mine, other = rows(core * half, half), rows((1 - core) * half, half)
-    swap = remote(work.at[other], got_pair, sems.at[0, 0], sems.at[1, 0], pair)
-    swap.start()
-    swap.wait()
-    work[mine, :] += got_pair[...]
-    scatter = [
-        remote(work.at[rows(core * half + c * piece, piece)], got_rest.at[o], sems.at[0, 1 + o], sems.at[1, 1 + o], 2 * c + core)
-        for o, c in enumerate(others)
-    ]
+    spot = lambda c, k: pl.ds(pl.multiple_of(k * half + c * piece, SUB), piece)
+    link = lambda kind, o, src, dst, peer: remote(src, dst, sems.at[0, kind * chips + o], sems.at[1, kind * chips + o], peer)
+    order = list(enumerate(others + [chip]))
+    swap = [link(0, o, work.at[spot(c, 1 - core)], got_pair.at[pl.ds(o * piece, piece)], pair) for o, c in order]
+    for c in swap:
+        c.start()
+    scatter = [link(1, o, work.at[spot(c, core)], got_rest.at[o], 2 * c + core) for o, c in order[:-1]]
+    for o, c in order:
+        swap[o].wait_recv()
+        work[spot(c, core), :] += got_pair[o * piece : (o + 1) * piece, :]
+        if o:
+            scatter[o - 1].start()
     for c in scatter:
-        c.start()
-    for c in scatter:
-        c.wait()
-    own = rows(core * half + chip * piece, piece)
+        c.wait_recv()
+    own = spot(chip, core)
     work[own, :] += jnp.sum(got_rest[...], axis=0)
     full[own, :] = work[own, :]
-    gather = [
-        remote(work.at[own], full.at[own], sems.at[0, chips + o], sems.at[1, chips + o], 2 * c + core) for o, c in enumerate(others)
-    ]
+    for c in swap + scatter:
+        c.wait_send()
+    gather = [link(2, o, work.at[own], full.at[own], 2 * c + core) for o, c in order[:-1]]
     for c in gather:
         c.start()
+    forward = [link(3, chips - 1, work.at[own], full.at[own], pair)]
+    forward[0].start()
+    for o, _ in order[:-1]:
+        gather[o].wait_recv()
+        came = spot(lax.rem(chip + chips - 1 - o, chips), core)
+        forward.append(link(3, o, full.at[came], full.at[came], pair))
+        forward[-1].start()
     for c in gather:
+        c.wait_send()
+    for c in forward:
         c.wait()
-    last = remote(full.at[mine], full.at[mine], sems.at[0, 2 * chips - 1], sems.at[1, 2 * chips - 1], pair)
-    last.start()
-    last.wait()
     one_out[:, :LANES] = full[0:top, :]
     one_out[:, LANES:] = full[top : 2 * top, :]
     two_out[:, :LANES] = full[2 * top : 2 * top + classes, :]
@@ -369,12 +379,10 @@
     mean[...] = jnp.sum(full[tail : tail + SUB, :], keepdims=True) / count[0:1, 0:1]
 
 
-def prep_kernel(n, chunk, rows, packed, mask, src_out, dst_out, w_out, used, counts, count, need, total, values, places, hits, mine, theirs, send_sem, recv_sem):
+def prep_kernel(n, chunk, rows, packed, weight, mask, src_out, dst_out, w_out, used, counts, count, need, total, values, places, hits, mine, theirs, send_sem, recv_sem):
     me, met = greet(n)
-    lines = packed.shape[0] // 2
-    slots = src_out.shape[0]
-    both = packed[:lines, :].astype(jnp.int32)
-    src, d, w = both >> 11, both & 2047, packed[lines:, :]
+    lines, slots = packed.shape[0], src_out.shape[0]
+    src, d, w = packed[...] >> 11, packed[...] & 2047, weight[...]
     live = w != 0.0
     halo = src >= rows
     above = (across((lines, lines)) < down((lines, lines))).astype(F32).astype(BF16)
@@ -415,8 +423,8 @@
     used[...] = flags
     side = hits.shape[0] // 2
     most = jnp.maximum(jnp.sum(flags[:side], keepdims=True), jnp.sum(flags[side:], keepdims=True))
-    mine[:SUB, :] = jnp.sum(mask[...].astype(F32).reshape(-1, *TILE), axis=0)
-    mine[SUB:, :] = jnp.broadcast_to(most, TILE)
+    mine[:1, :] = jnp.sum(mask[...].astype(F32), axis=0, keepdims=True)
+    mine[1:, :] = jnp.broadcast_to(most, (1, LANES))
     met()
     copies = [remote(mine, theirs.at[o - 1], send_sem.at[o - 1], recv_sem.at[o - 1], lax.rem(me + o, n)) for o in range(1, n)]
     for c in copies:
@@ -443,9 +451,9 @@
     w_out[...] = (plane(3) + plane(4) + plane(5)) * 2.0
     for c in copies:
         c.wait()
-    every = jnp.sum(mine[:SUB, :] + jnp.sum(theirs[:, :SUB, :], axis=0), keepdims=True)
+    every = jnp.sum(mine[:1, :] + jnp.sum(theirs[:, :1, :], axis=0), keepdims=True)
     count[...] = jnp.maximum(jnp.broadcast_to(every, count.shape), 1.0)
-    need[...] = jnp.maximum(mine[SUB:, :], jnp.max(theirs[:, SUB:, :], axis=0))
+    need[...] = jnp.broadcast_to(jnp.maximum(mine[1:, :], jnp.max(theirs[:, 1:, :], axis=0)), need.shape)
 
 
 def local_kernel(chunk, backward, counts, src, dst, w, table, out, src_s, dst_s, sems, *accs):
@@ -470,11 +478,12 @@
     edges.walk(chunk, src_s, dst_s, htab, accs, True)
 
 
-def backward_halo(chunk, edges, src_s, dst_s, grad, back_prev, back_next, accs, wait, lists=None):
+def backward_halo(limit, chunk, edges, src_s, dst_s, grad, back_prev, back_next, accs, wait, lists=None):
+    split = accs[0].shape[0] // 2
     for a in accs:
-        fill_zero(a)
+        for start in (0, split):
+            fill_zero(a.at[pl.ds(start, limit * 2)])
     edges.walk(chunk, dst_s, src_s, grad, accs, wait)
-    split = accs[0].shape[0] // 2
     if lists is None:
 
         @pl.loop(0, back_prev.shape[0], step=BLOCK)
@@ -514,22 +523,22 @@
         back[i : i + 1, :] = send[i // per : i // per + 1, (i % per) * LANES : (i % per + 1) * LANES] * 2
     forward_halo(chunk, edges, src_s, dst_s, from_prev, from_next, part, htab, accs, unpack_plain)
 
-    @pl.loop(0, hid.shape[0], step=BLOCK)
-    def _(i):
-        even, odd = halves(accs, i, BLOCK)
+    @pl.loop(0, hid.shape[0], step=STEP)
+    def _(i):
+        even, odd = halves(accs, i, STEP)
         h = stack_lanes([jnp.maximum(even, 0.0), jnp.maximum(odd, 0.0)]).astype(BF16)
-        hid[pl.ds(i, BLOCK), :] = h
+        hid[pl.ds(i, STEP), :] = h
         t = dot(h, w2_b, COLS_A).astype(BF16)
-        tab_b[pl.ds(i, BLOCK), :] = t
+        tab_b[pl.ds(i, STEP), :] = t
         t = t.astype(F32)
-        put_halves(tab, i, BLOCK, t[:, :LANES], t[:, LANES:])
+        put_halves(tab, i, STEP, t[:, :LANES], t[:, LANES:])
 
     for c in fetch:
         c.wait()
     gather_packed(send, idx, tab_b, tab, buf, to_prev, to_next)
 
 
-def loss_kernel(chunk, classes, counts, src, dst, w, src_back, lists, count, from_prev, from_next, part, labels, mask, loss, grad, back_prev, back_next, htab, src_s, dst_s, back_s, sems, *accs):
+def loss_kernel(limit, quad, chunk, classes, counts, src, dst, w, src_back, lists, count, from_prev, from_next, part, labels, mask, loss, grad, back_prev, back_next, htab, src_s, dst_s, back_s, sems, *accs):
     edges = Edges(counts[0], counts[1], w, (src, dst, src_back), (src_s, dst_s, back_s), sems)
     forward_halo(chunk, edges, src_s, dst_s, from_prev, from_next, part, htab, accs, unpack_rows)
     lane = across(SQUARE)
@@ -537,25 +546,26 @@
     scale = 1.0 / count[0:1, :]
     loss[...] = jnp.zeros_like(loss)
 
-    @pl.loop(0, labels.shape[0] // 2)
-    def _(pair):
-        for b in (pair * 2, pair * 2 + 1):
+    @pl.loop(0, labels.shape[0], step=quad)
+    def _(first):
+        for b in [first + q for q in range(quad)]:
             even, odd = halves(accs, b * LANES, LANES)
-            label = spread(labels[pl.ds(b, 1), :])
-            keep = spread(mask[pl.ds(b, 1), :]).astype(F32)
             odd = jnp.where(live, odd, -jnp.inf)
+            keep = spread(mask[pl.ds(b, 1), :])
+            label = jnp.where(keep > 0, spread(labels[pl.ds(b, 1), :]), -1)
+            hit_even, hit_odd = lane == label, lane + LANES == label
             top = jnp.max(jnp.maximum(even, odd), axis=1, keepdims=True)
-            total = jnp.sum(jnp.exp(even - top) + jnp.exp(odd - top), axis=1, keepdims=True)
-            norm = top + jnp.log(total)
-            hit_even, hit_odd = lane == label, lane + LANES == label
-            picked = jnp.where(hit_even, even, 0.0) + jnp.where(hit_odd, odd, 0.0)
-            per_row = jnp.where(lane == 0, norm, 0.0) - picked
-            loss[...] += jnp.sum((keep * per_row).reshape(LANES // SUB, *TILE), axis=0)
-            d_even = (jnp.exp(even - norm) - hit_even.astype(F32)) * (keep * scale)
-            d_odd = (jnp.exp(odd - norm) - hit_odd.astype(F32)) * (keep * scale)
-            put_halves(grad, b * LANES, LANES, d_even, d_odd)
-
-    backward_halo(chunk, edges, back_s, dst_s, grad, back_prev, back_next, accs, False, lists)
+            exp_even, exp_odd = jnp.exp(even - top), jnp.exp(odd - top)
+            total = jnp.sum(exp_even + exp_odd, axis=1, keepdims=True)
+            norm = jnp.where(jnp.logical_and(lane == 0, keep > 0), top + jnp.log(total), 0.0)
+            per_row = norm - jnp.where(hit_even, even, jnp.where(hit_odd, odd, 0.0))
+            loss[...] += jnp.sum(per_row.reshape(LANES // SUB, *TILE), axis=0)
+            share = keep.astype(F32) * scale * (1.0 / total)
+            put_halves(
+                grad, b * LANES, LANES, *(e * share - jnp.where(hit, scale, 0.0) for e, hit in ((exp_even, hit_even), (exp_odd, hit_odd)))
+            )
+
+    backward_halo(limit, chunk, edges, back_s, dst_s, grad, back_prev, back_next, accs, False, lists)
 
 
 def take_returns(back, slots, counts, part, got_prev, got_next, accs):
@@ -567,7 +577,7 @@
     return [pltpu.make_async_copy(lines.at[i], smem.at[pl.ds(i * LANES, LANES)], sems.at[i]) for i in range(lines.shape[0])]
 
 
-def middle_kernel(chunk, counts, src, dst, w, back, got_prev, got_next, part, hid, w2, grad_two, grad, back_prev, back_next, slots, n_back, returned, w2_pad, slot_s, slot_sems, src_s, dst_s, sems, *accs):
+def middle_kernel(limit, chunk, counts, src, dst, w, back, got_prev, got_next, part, hid, w2, grad_two, grad, back_prev, back_next, slots, n_back, returned, w2_pad, slot_s, slot_sems, src_s, dst_s, sems, *accs):
     edges = Edges(counts[0], counts[1], w, (src, dst), (src_s, dst_s), sems)
     edges.fetch()
     side = slots.shape[0] // 2
@@ -590,17 +600,17 @@
     take_returns(back, slot_s, n_back, part, returned.at[pl.ds(0, 4 * half)], returned.at[pl.ds(4 * half, 4 * half)], accs)
     grad_two[...] = jnp.zeros_like(grad_two)
 
-    @pl.loop(0, hid.shape[0], step=BLOCK)
-    def _(i):
-        even, odd = halves(accs, i, BLOCK)
+    @pl.loop(0, hid.shape[0], step=STEP)
+    def _(i):
+        even, odd = halves(accs, i, STEP)
         d_tab = stack_lanes([even, odd]).astype(BF16)
-        h = hid[pl.ds(i, BLOCK), :]
+        h = hid[pl.ds(i, STEP), :]
         grad_two[...] += dot(d_tab, h, ROWS_A)
         d_hid = dot(d_tab, w2_b)
         d_pre = jnp.where(h > 0, d_hid, 0.0)
-        put_halves(grad, i, BLOCK, d_pre[:, :LANES], d_pre[:, LANES:])
-
-    backward_halo(chunk, edges, src_s, dst_s, grad, back_prev, back_next, accs, True)
+        put_halves(grad, i, STEP, d_pre[:, :LANES], d_pre[:, LANES:])
+
+    backward_halo(limit, chunk, edges, src_s, dst_s, grad, back_prev, back_next, accs, True)
 
 
 def last_kernel(back, n_back, slots, got_prev, got_next, part, x, grad_one, slot_s, slot_sems, *accs):
@@ -615,11 +625,11 @@
     take_returns(back, slot_s, n_back, part, got_prev, got_next, accs)
     grad_one[...] = jnp.zeros_like(grad_one)
 
-    @pl.loop(0, x.shape[0], step=BLOCK)
-    def _(i):
-        even, odd = halves(accs, i, BLOCK)
+    @pl.loop(0, x.shape[0], step=STEP)
+    def _(i):
+        even, odd = halves(accs, i, STEP)
         d_tab = stack_lanes([even, odd]).astype(BF16)
-        grad_one[...] += dot(x[pl.ds(i, BLOCK), :], d_tab, ROWS_A)
+        grad_one[...] += dot(x[pl.ds(i, STEP), :], d_tab, ROWS_A)
 
 
 def call(body, name, outs, ins, scratch, out_specs=None, collective=None, vmem=14):
@@ -653,16 +663,16 @@
         w2 = w_two.T
         mask = mask.reshape(-1, LANES)
         labels = labels.reshape(-1, LANES)
-        packed = jnp.concatenate([(edge_src * 2048 + edge_dst).astype(F32), edge_w]).reshape(2 * lines, LANES)
+        packed = (edge_src * 2048 + edge_dst).reshape(lines, LANES)
         ints = sds((slots, LANES), jnp.int32)
         sided = sds((2 * side, LANES), F32)
         src, dst, w_lines, used, counts, count, need = call(
             functools.partial(prep_kernel, num_dev, PREP_CHUNK, rows), "prep",
-            [ints, ints, sds((slots, LANES), F32), sided, sds((2,), jnp.int32), one, one], [VMEM] * 2,
-            [(6 * slots, LANES), (6 * lines, LANES), pltpu.VMEM((4 * lines, LANES), jnp.int32), sided.shape, (16, LANES), (num_dev - 1, 16, LANES)]
+            [ints, ints, sds((slots, LANES), F32), sided, sds((2,), jnp.int32), one, one], [VMEM] * 3,
+            [(6 * slots, LANES), (6 * lines, LANES), pltpu.VMEM((4 * lines, LANES), jnp.int32), sided.shape, (2, LANES), (num_dev - 1, 2, LANES)]
             + [dma((num_dev - 1,))] * 2,
             out_specs=[VMEM] * 4 + [SMEM, VMEM, VMEM], vmem=8, collective=0,
-        )(packed, mask)
+        )(packed, edge_w.reshape(lines, LANES), mask)
 
         def run(limit):
             compact = limit < halo
@@ -676,41 +686,42 @@
             from_next = lax.ppermute(to_p, AXIS, to_prev)
             flat, flat_dst, flat_back = src.reshape(-1), dst.reshape(-1), src_back.reshape(-1)
 
+            four = [tab] * 4
             walk = [SMEM, ANY, ANY, VMEM]
             index = pltpu.SMEM((slots * LANES,), jnp.int32)
             walk_s = lambda n: [index] * n + [dma((n, slots * LANES // SEGMENT))]
             slot_s = [pltpu.SMEM((2 * halo,), jnp.int32), dma((2 * side,))]
             local, local_back = (
-                call(functools.partial(local_kernel, chunk_l, back), "local_edges", tab_f, walk + [VMEM], walk_s(2) + [tab] * 4)
+                call(functools.partial(local_kernel, chunk_l, back), "local_edges", tab_f, walk + [VMEM], walk_s(2) + four)
                 for back in (False, True)
             )
             part = local(counts, flat, flat_dst, w, tab_one)
             hid, tab_two, to_p, to_n, back = call(
                 functools.partial(hidden_kernel, chunk_h), "hidden",
                 [sds((rows, 2 * LANES), BF16), tab_f, pack_b, pack_b, sds((2 * side, LANES), jnp.int32)],
-                walk + [VMEM] * 5, [tab, tab_b, w2_pad, half] + list_s + walk_s(2) + [tab] * 4,
+                walk + [VMEM] * 5, [tab, tab_b, w2_pad, half] + list_s + walk_s(2) + four,
             )(counts, flat, flat_dst, w, send, from_prev, from_next, part, w2)
             from_prev = lax.ppermute(to_n, AXIS, to_next)
             from_next = lax.ppermute(to_p, AXIS, to_prev)
             back = back.reshape(-1)
             part = local(counts, flat, flat_dst, w, tab_two)
             loss, grad, to_p, to_n = call(
-                functools.partial(loss_kernel, chunk_h, classes), "loss", [one, tab_f, pack_f, pack_f],
-                walk + [ANY] + [VMEM] * 7, [tab] + walk_s(3) + [tab] * 4,
+                functools.partial(loss_kernel, limit, 4, chunk_h, classes), "loss", [one, tab_f, pack_f, pack_f],
+                walk + [ANY] + [VMEM] * 7, [tab] + walk_s(3) + four,
             )(counts, flat, flat_dst, w, flat_back, lists, count, from_prev, from_next, part, labels, mask)
             got_prev = lax.ppermute(to_p, AXIS, to_prev)
             got_next = lax.ppermute(to_n, AXIS, to_next)
             part = local_back(counts, flat, flat_dst, w, grad)
             grad_two, grad, to_p, to_n, slot, n_back = call(
-                functools.partial(middle_kernel, chunk_h), "middle",
+                functools.partial(middle_kernel, limit, chunk_h), "middle",
                 [sds(w2_pad, F32), tab_f, half_f, half_f, sds((2 * side, LANES), jnp.int32), sds((2,), jnp.int32)],
-                walk + [SMEM] + [VMEM] * 5, [(4 * limit, LANES), w2_pad] + slot_s + walk_s(2) + [tab] * 4, out_specs=[VMEM] * 5 + [SMEM],
+                walk + [SMEM] + [VMEM] * 5, [(4 * limit, LANES), w2_pad] + slot_s + walk_s(2) + four, out_specs=[VMEM] * 5 + [SMEM],
             )(counts, flat_back, flat_dst, w, back, got_prev, got_next, part, hid, w2)
             got_prev = lax.ppermute(to_p, AXIS, to_prev)
             got_next = lax.ppermute(to_n, AXIS, to_next)
             part = local_back(counts, flat, flat_dst, w, grad)
             grad_one = call(
-                last_kernel, "last", sds((x.shape[1], 2 * LANES), F32), [SMEM, SMEM, ANY] + [VMEM] * 4, slot_s + [tab] * 4
+                last_kernel, "last", sds((x.shape[1], 2 * LANES), F32), [SMEM, SMEM, ANY] + [VMEM] * 4, slot_s + four
             )(back, n_back, slot, got_prev, got_next, part, x)
             return grad_one, grad_two, loss
 
@@ -721,7 +732,7 @@
         lines = -(-lines // unit) * unit
         grad_one, grad_two, mean = call(
             functools.partial(reduce_kernel, num_dev), "reduce", [sds(grad_one.shape, F32), sds((classes, 2 * LANES), F32), sds((1, 1), F32)],
-            [VMEM] * 4, [(lines, LANES), (lines, LANES), (lines // 2, LANES), (num_dev // 2 - 1, lines // num_dev, LANES), dma((2, num_dev))],
+            [VMEM] * 4, [(lines, LANES), (lines, LANES), (lines // 2, LANES), (num_dev // 2 - 1, lines // num_dev, LANES), dma((2, 2 * num_dev))],
             collective=1, vmem=8,
         )(grad_one, grad_two, loss, count)
         return mean.reshape(()), grad_one, grad_two.T

time: 126 us -> 123 us (0.976)
  Pallas kernels: 81.9 us -> 94 us
  waiting for transfers between devices: 21.5 us -> 9.91 us
  starting transfers between devices: 15 us -> 11.7 us
    ppermute x2, waiting for transfers between devices: 12.6 us -> 3.9 us  [run(): got_prev = lax.ppermute(to_p, AXIS, to_prev)]
    pallas_call x1, Pallas kernels: 14.6 us -> 20.7 us  [step(): call(functools.partial(reduce_kernel, num_dev), 'reduce', [sds(grad_one.s...]
    ppermute x2, starting transfers between devices: 7.86 us -> 2.54 us  [run(): got_prev = lax.ppermute(to_p, AXIS, to_prev)]
    ppermute x2, waiting for transfers between devices: 8.91 us -> 4.13 us  [run(): from_prev = lax.ppermute(to_n, AXIS, to_next)]
    pallas_call x2, Pallas kernels: 12 us -> 16.2 us  [run(): part = local_back(counts, flat, flat_dst, w, grad)]
    pallas_call x1, Pallas kernels: 5.98 us -> 8.07 us  [run(): part = local(counts, flat, flat_dst, w, tab_two)]
    pallas_call x1, Pallas kernels: 5.98 us -> 8.07 us  [run(): part = local(counts, flat, flat_dst, w, tab_one)]
    ppermute x2, starting transfers between devices: 0.01 us -> 2.04 us  [run(): got_next = lax.ppermute(to_n, AXIS, to_next)]
  transfers between devices with their start and end apart: 8 -> 8, of which waited for: 4 -> 5; matrix products, arithmetic and copies ran while one was open for 0% -> 0% of each run, Pallas kernels for 19% -> 26%
where the time goes in v4:
time: 123 us
  Pallas kernels  94 us (76%)
  starting transfers between devices  11.7 us (10%)
  waiting for transfers between devices  9.91 us (8%)
  between operations  3.06 us (2%)
  local copies, waits for them, and re-layouts  2.63 us (2%)
    pallas_call x1, Pallas kernels, step(): call(functools.partial(reduce_kernel, num_dev), 'reduce', [sds(grad_one.s...  20.7 us
    pallas_call x2, Pallas kernels, run(): part = local_back(counts, flat, flat_dst, w, grad)  16.2 us
    pallas_call x1, Pallas kernels, step(): call(functools.partial(prep_kernel, num_dev, PREP_CHUNK, rows), 'prep', [...  10.6 us
    pallas_call x1, Pallas kernels, run(): part = local(counts, flat, flat_dst, w, tab_one)  8.07 us
    pallas_call x1, Pallas kernels, run(): part = local(counts, flat, flat_dst, w, tab_two)  8.07 us
    pallas_call x1, Pallas kernels, run(): call(functools.partial(loss_kernel, limit, 4, chunk_h, classes), 'loss',...  7.21 us
    ppermute x2, starting transfers between devices, run(): from_next = lax.ppermute(to_p, AXIS, to_prev)  7.06 us
    pallas_call x1, Pallas kernels, run(): call(functools.partial(first_kernel, compact, halo), 'first', [tab_f, hal...  6.87 us
  transfers between devices with their start and end apart: 8, of which 5 were waited for; matrix products, arithmetic and copies ran while one was open for 0% of the time, Pallas kernels for 26%

profile of v4, /device:TPU:0, one launch (start us, length us, event | category | flops | bytes accessed | tf_op | source)
XLA Modules:
  0.0 122.5 jit_solution(11434151924887115472)
XLA Ops:
  0.6 0.8 add_bitcast_fusion.packed
  1.4 0.0 copy-start
  1.4 0.8 copy-done
  2.2 0.0 copy-start.1
  2.2 0.0 copy-start.2
  2.2 0.0 copy-start.3
  2.2 0.0 copy-start.4
  2.2 0.0 copy-start.5
  2.2 0.0 copy-start.6
  2.2 10.6 %prep.1 = (s32[72,128]{1,0:T(8,128)S(1)}, s32[72,128]{1,0:T(8,128)S(1)}, f32[72,128]{1,0:T(8,128)S(1)}, f32[16,128]{1,0:T(8,128)S(1)}, s32[2]{0:T(128)S(1)}, /*index=5*/f32[8,128]{1,0:T(8,128)S(1)}, f32[8,128]{1,0:T(8,128)S(1)}) custom-call(s32[64,128]{1,0:T(8,128)S(1)} %add_bitcast_fusion.packed, f32[64,128]{1,0:T(8,128)S(1)} %bitcast.18, s32[16,128]{1,0:T(8,128)} %bitcast.29), custom_call_target="tpu_custom_call" | custom-call | flops 10000000000 | bytes 10000000 | tf_op jit(solution)/shard_map/prep/pallas_call | solution.py:669
  12.8 0.5 slice.3
  13.9 0.0 copy-done.1
  14.0 0.0 copy-done.2
  14.0 0.0 copy-done.3
  14.0 0.0 copy-done.4
  14.0 0.0 copy-done.5
  14.0 0.0 copy-done.6
  14.0 84.8 %conditional.1 = (f32[128,256]{1,0:T(8,128)S(1)}, f32[256,256]{1,0:T(8,128)S(1)}, f32[8,128]{1,0:T(8,128)S(1)}) conditional(s32[]{:T(128)} %bitcast.11, (s32[72,128]{1,0:T(8,128)S(1)}, s32[72,128]{1,0:T(8,128)S(1)}, bf16[2048,128]{1,0:T(8,128)(2,1)S(1)}, f32[128,256]{1,0:T(8,128)S(1)}, s32[2,1024]{1,0:T(2,128)S(1)}, /*index=5*/s32[2]{0:T(128)S(1)}, ...), branch_computations={%region_0.0_spmd, %region_1.0_spmd} | conditional | flops 89999998976 | bytes 112053208 | solution.py:729
  14.0 6.9 %first.2 = (f32[4096,128]{1,0:T(8,128)S(1)}, bf16[1024,256]{1,0:T(8,128)(2,1)S(1)}, bf16[1024,256]{1,0:T(8,128)(2,1)S(1)}, f32[9216,128]{1,0:T(8,128)S(1)}, s32[...) custom-call(bf16[2048,128]{1,0:T(8,128)(2,1)S(1)} %get-tuple-element.51.x, f32[128,256]{1,0:T(8,128)S(1)} %get-tuple-element.52.w1, ...), custom_call_target="tpu_custom_call" | custom-call | flops 10000000000 | bytes 10000000 | tf_op jit(solution)/shard_map/cond/branch_0_fun/first/pallas_call | solution.py:681
  20.9 0.1 collective-permute-start
  21.0 3.5 %collective-permute-start.1 = (bf16[1024,256]{1,0:T(8,128)(2,1)S(1)}, bf16[1024,256]{1,0:T(8,128)(2,1)S(1)}, u32[]{:S(2)}, u32[]{:S(2)}) collective-permute-start(bf16[1024,256]{1,0:T(8,128)(2,1)S(1)} %get-tuple-element.58), channel_id=1, source_target_pairs={{0,15},{1,0},{2,1},{3,2},{4,3},{5,4},{6,5},{7,6},{8,7},{9,8},{10,9... | collective-permute-start | bytes 1572872 | tf_op jit(solution)/shard_map/cond/branch_0_fun/ppermute | solution.py:686
  24.5 8.1 %local_edges.8.part = f32[4096,128]{1,0:T(8,128)S(1)} custom-call(s32[2]{0:T(128)S(1)} %get-tuple-element.48.counts, s32[9216]{0:T(1024)S(1)} %bitcast.34, s32[9216]{0:T(1024)S(1)} %bitcast.46, f32[9216,128]{1,0:T(8,128)S(1)} %get-tuple-element.56.w, f32[4096,128]{1,0:T(8,128)S(1)} %get-tuple-element.59.table), custom_call_target="tpu_custom_call" | custom-call | flops 10000000000 | bytes 10000000 | tf_op jit(solution)/shard_map/cond/branch_0_fun/local_edges/pallas_call | solution.py:698
  32.6 4.1 %collective-permute-done.from_prev = bf16[1024,256]{1,0:T(8,128)(2,1)S(1)} collective-permute-done((bf16[1024,256]{1,0:T(8,128)(2,1)S(1)}, bf16[1024,256]{1,0:T(8,128)(2,1)S(1)}, u32[]{:S(2)}, u32[]{:S(2)}) %collective-permute-start) | collective-permute-done | bytes 524320 | tf_op jit(solution)/shard_map/cond/branch_0_fun/ppermute | solution.py:685
  36.7 0.0 collective-permute-done.1.from_next
  36.7 6.7 %hidden.2 = (bf16[2048,256]{1,0:T(8,128)(2,1)S(1)}, f32[4096,128]{1,0:T(8,128)S(1)}, bf16[1536,128]{1,0:T(8,128)(2,1)S(1)}, bf16[1536,128]{1,0:T(8,128)(2,1)S(1)}, s32[16,128]{1,0:T(8,128)S(1)}) custom-call(s32[2]{0:T(128)S(1)} %get-tuple-element.48.counts, s32[9216]{0:T(1024)S(1)} %bitcast.35, s32[9216]{0:T(1024)S(1)} %bitcast.47, ...), custom_call_target="tpu_custom_call" | custom-call | flops 10000000000 | bytes 10000000 | tf_op jit(solution)/shard_map/cond/branch_0_fun/hidden/pallas_call | solution.py:699
  43.4 0.1 collective-permute-start.2
  43.5 3.5 %collective-permute-start.3 = (bf16[1536,128]{1,0:T(8,128)(2,1)S(1)}, bf16[1536,128]{1,0:T(8,128)(2,1)S(1)}, u32[]{:S(2)}, u32[]{:S(2)}) collective-permute-start(bf16[1536,128]{1,0:T(8,128)(2,1)S(1)} %get-tuple-element.66), channel_id=1, source_target_pairs={{0,15},{1,0},{2,1},{3,2},{4,3},{5,4},{6,5},{7,6},{8,7},{9,8},{10,9... | collective-permute-start | bytes 1179656 | tf_op jit(solution)/shard_map/cond/branch_0_fun/ppermute | solution.py:705
  47.0 8.1 %local_edges.9.part = f32[4096,128]{1,0:T(8,128)S(1)} custom-call(s32[2]{0:T(128)S(1)} %get-tuple-element.48.counts, s32[9216]{0:T(1024)S(1)} %bitcast.36, s32[9216]{0:T(1024)S(1)} %bitcast.48, f32[9216,128]{1,0:T(8,128)S(1)} %get-tuple-element.56.w, f32[4096,128]{1,0:T(8,128)S(1)} %get-tuple-element.67.table), custom_call_target="tpu_custom_call" | custom-call | flops 10000000000 | bytes 10000000 | tf_op jit(solution)/shard_map/cond/branch_0_fun/local_edges/pallas_call | solution.py:707
  55.1 0.0 collective-permute-done.2.from_prev
  55.1 0.0 collective-permute-done.3.from_next
  55.1 7.2 %loss.2 = (f32[8,128]{1,0:T(8,128)S(1)}, f32[4096,128]{1,0:T(8,128)S(1)}, f32[968,128]{1,0:T(8,128)S(1)}, f32[968,128]{1,0:T(8,128)S(1)}) custom-call(s32[2]{0:T(128)S(1)} %get-tuple-element.48.counts, s32[9216]{0:T(1024)S(1)} %bitcast.37, s32[9216]{0:T(1024)S(1)} %bitcast.49, f32[9216,128]{1,0:T(8,128)S(1)} %get-tuple-element.56.w, s32[9216]{0:T(1024)S(1)} %bitcast.19, ...), custom_call_target="tpu_custom_call" | custom-call | flops 10000000000 | bytes 10000000 | tf_op jit(solution)/shard_map/cond/branch_0_fun/loss/pallas_call | solution.py:708
  62.3 0.1 collective-permute-start.4
  62.4 0.5 collective-permute-start.5
  62.9 8.1 %local_edges.10.part = f32[4096,128]{1,0:T(8,128)S(1)} custom-call(s32[2]{0:T(128)S(1)} %get-tuple-element.48.counts, s32[9216]{0:T(1024)S(1)} %bitcast.38, s32[9216]{0:T(1024)S(1)} %bitcast.50, f32[9216,128]{1,0:T(8,128)S(1)} %get-tuple-element.56.w, f32[4096,128]{1,0:T(8,128)S(1)} %get-tuple-element.72.table), custom_call_target="tpu_custom_call" | custom-call | flops 10000000000 | bytes 10000000 | tf_op jit(solution)/shard_map/cond/branch_0_fun/local_edges/pallas_call | solution.py:714
  71.0 1.0 collective-permute-done.4.got_prev
  71.9 1.2 collective-permute-done.5.got_next
  73.1 6.5 %middle.2 = (f32[256,256]{1,0:T(8,128)S(1)}, f32[4096,128]{1,0:T(8,128)S(1)}, f32[1280,128]{1,0:T(8,128)S(1)}, f32[1280,128]{1,0:T(8,128)S(1)}, s32[16,128]{1,0:T(8,128)S(1)}, /*index=5*/s32[2]{0:T(128)S(1)}) custom-call(s32[2]{0:T(128)S(1)} %get-tuple-element.48.counts, s32[9216]{0:T(1024)S(1)} %bitcast.20, s32[9216]{0:T(1024)S(1)} %bitcast.51, ...), custom_call_target="tpu_custom_call" | custom-call | flops 10000000000 | bytes 10000000 | tf_op jit(solution)/shard_map/cond/branch_0_fun/middle/pallas_call | solution.py:715
  79.6 2.5 %collective-permute-start.6 = (f32[1280,128]{1,0:T(8,128)S(1)}, f32[1280,128]{1,0:T(8,128)S(1)}, u32[]{:S(2)}, u32[]{:S(2)}) collective-permute-start(f32[1280,128]{1,0:T(8,128)S(1)} %get-tuple-element.76), channel_id=1, source_target_pairs={{0,15},{1,0},{2,1},{3,2},{4,3},{5,4},{6,5},{7,6},{8,7},{9,8},{10,9... | collective-permute-start | bytes 1966088 | tf_op jit(solution)/shard_map/cond/branch_0_fun/ppermute | solution.py:720
  82.1 1.5 %collective-permute-start.7 = (f32[1280,128]{1,0:T(8,128)S(1)}, f32[1280,128]{1,0:T(8,128)S(1)}, u32[]{:S(2)}, u32[]{:S(2)}) collective-permute-start(f32[1280,128]{1,0:T(8,128)S(1)} %get-tuple-element.77), channel_id=1, source_target_pairs={{0,1},{1,2},{2,3},{3,4},{4,5},{5,6},{6,7},{7,8},{8,9},{9,10},{10,1... | collective-permute-start | bytes 1966088 | tf_op jit(solution)/shard_map/cond/branch_0_fun/ppermute | solution.py:721
  83.7 8.1 %local_edges.11.part = f32[4096,128]{1,0:T(8,128)S(1)} custom-call(s32[2]{0:T(128)S(1)} %get-tuple-element.48.counts, s32[9216]{0:T(1024)S(1)} %bitcast.39, s32[9216]{0:T(1024)S(1)} %bitcast.52, f32[9216,128]{1,0:T(8,128)S(1)} %get-tuple-element.56.w, f32[4096,128]{1,0:T(8,128)S(1)} %get-tuple-element.78.table), custom_call_target="tpu_custom_call" | custom-call | flops 10000000000 | bytes 10000000 | tf_op jit(solution)/shard_map/cond/branch_0_fun/local_edges/pallas_call | solution.py:722
  91.8 2.9 %collective-permute-done.6.got_prev = f32[1280,128]{1,0:T(8,128)S(1)} collective-permute-done((f32[1280,128]{1,0:T(8,128)S(1)}, f32[1280,128]{1,0:T(8,128)S(1)}, u32[]{:S(2)}, u32[]{:S(2)}) %collective-permute-start.6) | collective-permute-done | bytes 655392 | tf_op jit(solution)/shard_map/cond/branch_0_fun/ppermute | solution.py:720
  94.7 0.7 collective-permute-done.7.got_next
  95.4 3.2 %last.2 = f32[128,256]{1,0:T(8,128)S(1)} custom-call(s32[2048]{0:T(1024)S(1)} %bitcast.24, s32[2]{0:T(128)S(1)} %get-tuple-element.74.n_back, s32[16,128]{1,0:T(8,128)S(1)} %get-tuple-element.75.slots, f32[1280,128]{1,0:T(8,128)S(1)} %collective-permute-done.6.got_prev, f32[1280,128]{1,0:T(8,128)S(1)} %collective-permute-done.7.got_next, ...), custom_call_target="tpu_custom_call" | custom-call | flops 10000000000 | bytes 10000000 | tf_op jit(solution)/shard_map/cond/branch_0_fun/last/pallas_call | solution.py:723
  98.8 20.7 %reduce.1 = (f32[128,256]{1,0:T(8,128)S(1)}, f32[172,256]{1,0:T(8,128)S(1)}, f32[1,1]{1,0:T(1,128)}) custom-call(f32[128,256]{1,0:T(8,128)S(1)} %get-tuple-element.137.one, f32[256,256]{1,0:T(8,128)S(1)} %get-tuple-element.138.two, f32[8,128]{1,0:T(8,128)S(1)} %get-tuple-element.139.loss, f32[8,128]{1,0:T(8,128)S(1)} %get-tuple-element.136.count), custom_call_target="tpu_custom_call" | custom-call | flops 10000000000 | bytes 10000000 | tf_op jit(solution)/shard_map/reduce/pallas_call | solution.py:733
  120.0 0.7 copy.22
  120.7 0.7 copy.23
Async XLA Ops:
  1.4 0.8 copy-start
  2.2 11.8 %copy-start.1 = (bf16[2048,128]{1,0:T(8,128)(2,1)S(1)}, bf16[2048,128]{1,0:T(8,128)(2,1)}, u32[]{:S(2)}) copy-start(bf16[2048,128]{1,0:T(8,128)(2,1)} %param.11) | copy-start | bytes 1572868
  2.2 11.8 %copy-start.2 = (f32[256,172]{0,1:T(8,128)S(1)}, f32[256,172]{0,1:T(8,128)}, u32[]{:S(2)}) copy-start(f32[256,172]{0,1:T(8,128)} %param.13) | copy-start | bytes 528388
  2.2 11.8 %copy-start.3 = (f32[128,256]{1,0:T(8,128)S(1)}, f32[128,256]{1,0:T(8,128)}, u32[]{:S(2)}) copy-start(f32[128,256]{1,0:T(8,128)} %param.12) | copy-start | bytes 393220
  2.2 11.8 %copy-start.4 = (s32[2048]{0:T(1024)S(1)}, s32[2048]{0:T(1024)}, u32[]{:S(2)}) copy-start(s32[2048]{0:T(1024)} %param.19) | copy-start | bytes 24580
  2.2 11.8 %copy-start.5 = (s32[2,1024]{1,0:T(2,128)S(1)}, s32[2,1024]{1,0:T(2,128)}, u32[]{:S(2)}) copy-start(s32[2,1024]{1,0:T(2,128)} %param.14) | copy-start | bytes 24580
  2.2 11.8 %copy-start.6 = (s32[2048]{0:T(1024)S(1)}, s32[2048]{0:T(1024)}, u32[]{:S(2)}) copy-start(s32[2048]{0:T(1024)} %param.18) | copy-start | bytes 24580
  20.9 15.8 %collective-permute-start = (bf16[1024,256]{1,0:T(8,128)(2,1)S(1)}, bf16[1024,256]{1,0:T(8,128)(2,1)S(1)}, u32[]{:S(2)}, u32[]{:S(2)}) collective-permute-start(bf16[1024,256]{1,0:T(8,128)(2,1)S(1)} %get-tuple-element.57), channel_id=1, source_target_pairs={{0,1},{1,2},{2,3},{3,4},{4,5},{5,6},{6,7},{7,8},{8,9},{9,10},{10,1... | collective-permute-start | bytes 1572872 | tf_op jit(solution)/shard_map/cond/branch_0_fun/ppermute | solution.py:685
  21.0 15.7 %collective-permute-start.1 = (bf16[1024,256]{1,0:T(8,128)(2,1)S(1)}, bf16[1024,256]{1,0:T(8,128)(2,1)S(1)}, u32[]{:S(2)}, u32[]{:S(2)}) collective-permute-start(bf16[1024,256]{1,0:T(8,128)(2,1)S(1)} %get-tuple-element.58), channel_id=1, source_target_pairs={{0,15},{1,0},{2,1},{3,2},{4,3},{5,4},{6,5},{7,6},{8,7},{9,8},{10,9... | collective-permute-start | bytes 1572872 | tf_op jit(solution)/shard_map/cond/branch_0_fun/ppermute | solution.py:686
  43.4 11.7 %collective-permute-start.2 = (bf16[1536,128]{1,0:T(8,128)(2,1)S(1)}, bf16[1536,128]{1,0:T(8,128)(2,1)S(1)}, u32[]{:S(2)}, u32[]{:S(2)}) collective-permute-start(bf16[1536,128]{1,0:T(8,128)(2,1)S(1)} %get-tuple-element.65), channel_id=1, source_target_pairs={{0,1},{1,2},{2,3},{3,4},{4,5},{5,6},{6,7},{7,8},{8,9},{9,10},{10,1... | collective-permute-start | bytes 1179656 | tf_op jit(solution)/shard_map/cond/branch_0_fun/ppermute | solution.py:704
  43.5 11.6 %collective-permute-start.3 = (bf16[1536,128]{1,0:T(8,128)(2,1)S(1)}, bf16[1536,128]{1,0:T(8,128)(2,1)S(1)}, u32[]{:S(2)}, u32[]{:S(2)}) collective-permute-start(bf16[1536,128]{1,0:T(8,128)(2,1)S(1)} %get-tuple-element.66), channel_id=1, source_target_pairs={{0,15},{1,0},{2,1},{3,2},{4,3},{5,4},{6,5},{7,6},{8,7},{9,8},{10,9... | collective-permute-start | bytes 1179656 | tf_op jit(solution)/shard_map/cond/branch_0_fun/ppermute | solution.py:705
  62.3 9.6 %collective-permute-start.4 = (f32[968,128]{1,0:T(8,128)S(1)}, f32[968,128]{1,0:T(8,128)S(1)}, u32[]{:S(2)}, u32[]{:S(2)}) collective-permute-start(f32[968,128]{1,0:T(8,128)S(1)} %get-tuple-element.70), channel_id=1, source_target_pairs={{0,15},{1,0},{2,1},{3,2},{4,3},{5,4},{6,5},{7,6},{8,7},{9,8},{10,9... | collective-permute-start | bytes 1486856 | tf_op jit(solution)/shard_map/cond/branch_0_fun/ppermute | solution.py:712
  62.4 10.7 %collective-permute-start.5 = (f32[968,128]{1,0:T(8,128)S(1)}, f32[968,128]{1,0:T(8,128)S(1)}, u32[]{:S(2)}, u32[]{:S(2)}) collective-permute-start(f32[968,128]{1,0:T(8,128)S(1)} %get-tuple-element.71), channel_id=1, source_target_pairs={{0,1},{1,2},{2,3},{3,4},{4,5},{5,6},{6,7},{7,8},{8,9},{9,10},{10,1... | collective-permute-start | bytes 1486856 | tf_op jit(solution)/shard_map/cond/branch_0_fun/ppermute | solution.py:713
  79.6 15.1 %collective-permute-start.6 = (f32[1280,128]{1,0:T(8,128)S(1)}, f32[1280,128]{1,0:T(8,128)S(1)}, u32[]{:S(2)}, u32[]{:S(2)}) collective-permute-start(f32[1280,128]{1,0:T(8,128)S(1)} %get-tuple-element.76), channel_id=1, source_target_pairs={{0,15},{1,0},{2,1},{3,2},{4,3},{5,4},{6,5},{7,6},{8,7},{9,8},{10,9... | collective-permute-start | bytes 1966088 | tf_op jit(solution)/shard_map/cond/branch_0_fun/ppermute | solution.py:720
  82.1 13.3 %collective-permute-start.7 = (f32[1280,128]{1,0:T(8,128)S(1)}, f32[1280,128]{1,0:T(8,128)S(1)}, u32[]{:S(2)}, u32[]{:S(2)}) collective-permute-start(f32[1280,128]{1,0:T(8,128)S(1)} %get-tuple-element.77), channel_id=1, source_target_pairs={{0,1},{1,2},{2,3},{3,4},{4,5},{5,6},{6,7},{7,8},{8,9},{9,10},{10,1... | collective-permute-start | bytes 1966088 | tf_op jit(solution)/shard_map/cond/branch_0_fun/ppermute | solution.py:721

commit v5 on v4

--- a/solution.py
+++ b/solution.py
@@ -17,11 +17,12 @@
 ANY = pl.BlockSpec(memory_space=pl.ANY)
 STEP = 512
 BLOCK = 256
-BYTE = 256
+BYTE = BLOCK
 SUB = 8
 TILE = (SUB, LANES)
 SQUARE = (LANES, LANES)
 PREP_CHUNK = 64
+SMALL = PREP_CHUNK
 SEGMENT = 1024
 MESH = pl.DeviceIdType.MESH
 
@@ -31,11 +32,12 @@
 
 
 def fill_zero(ref):
-    zero = jnp.zeros((BLOCK, LANES), F32)
-
-    @pl.loop(0, ref.shape[0], step=BLOCK)
-    def _(i):
-        ref[pl.ds(i, BLOCK), :] = zero
+    step = BLOCK if ref.shape[0] % BLOCK == 0 else SMALL
+    zero = jnp.zeros((step, LANES), F32)
+
+    @pl.loop(0, ref.shape[0], step=step)
+    def _(i):
+        ref[pl.ds(i, step), :] = zero
 
 
 def copy_in(dst, src):
@@ -379,11 +381,11 @@
     mean[...] = jnp.sum(full[tail : tail + SUB, :], keepdims=True) / count[0:1, 0:1]
 
 
-def prep_kernel(n, chunk, rows, packed, weight, mask, src_out, dst_out, w_out, used, counts, count, need, total, values, places, hits, mine, theirs, send_sem, recv_sem):
+def prep_kernel(n, chunk, rows, src_in, dst_in, w_in, mask, src_out, dst_out, w_out, used, counts, count, need, total, values, places, hits, mine, theirs, send_sem, recv_sem):
     me, met = greet(n)
-    lines, slots = packed.shape[0], src_out.shape[0]
-    src, d, w = packed[...] >> 11, packed[...] & 2047, weight[...]
-    live = w != 0.0
+    lines, slots = src_in.shape[0], src_out.shape[0]
+    src, d, half_w = src_in[...], dst_in[...], w_in[...] * 0.5
+    live = w_in[...] != 0.0
     halo = src >= rows
     above = (across((lines, lines)) < down((lines, lines))).astype(F32).astype(BF16)
     is_local, is_halo = jnp.logical_and(live, jnp.logical_not(halo)), jnp.logical_and(live, halo)
@@ -395,7 +397,6 @@
     counts[1] = local_chunks + (n_halo + chunk - 1) // chunk
     pos = jnp.where(is_local, rank(is_local), jnp.where(is_halo, rank(is_halo) + local_chunks * chunk, -1))
     s = jnp.where(halo, src - rows, src)
-    half_w = w * 0.5
     w_a = half_w.astype(BF16).astype(F32)
     w_b = (half_w - w_a).astype(BF16).astype(F32)
     w_c = half_w - w_a - w_b
@@ -453,7 +454,7 @@
         c.wait()
     every = jnp.sum(mine[:1, :] + jnp.sum(theirs[:, :1, :], axis=0), keepdims=True)
     count[...] = jnp.maximum(jnp.broadcast_to(every, count.shape), 1.0)
-    need[...] = jnp.broadcast_to(jnp.maximum(mine[1:, :], jnp.max(theirs[:, 1:, :], axis=0)), need.shape)
+    need[0] = jnp.max(jnp.maximum(mine[1:, :], jnp.max(theirs[:, 1:, :], axis=0))).astype(jnp.int32)
 
 
 def local_kernel(chunk, backward, counts, src, dst, w, table, out, src_s, dst_s, sems, *accs):
@@ -486,10 +487,10 @@
     edges.walk(chunk, dst_s, src_s, grad, accs, wait)
     if lists is None:
 
-        @pl.loop(0, back_prev.shape[0], step=BLOCK)
+        @pl.loop(0, back_prev.shape[0], step=SMALL)
         def _(i):
-            back_prev[pl.ds(i, BLOCK), :] = functools.reduce(jnp.add, [a[pl.ds(i, BLOCK), :] for a in accs])
-            back_next[pl.ds(i, BLOCK), :] = functools.reduce(jnp.add, [a[pl.ds(split + i, BLOCK), :] for a in accs])
+            back_prev[pl.ds(i, SMALL), :] = functools.reduce(jnp.add, [a[pl.ds(i, SMALL), :] for a in accs])
+            back_next[pl.ds(i, SMALL), :] = functools.reduce(jnp.add, [a[pl.ds(split + i, SMALL), :] for a in accs])
         return
     side = lists.shape[0] // 2
     half = (back_prev.shape[0] - side) // 3
@@ -663,16 +664,16 @@
         w2 = w_two.T
         mask = mask.reshape(-1, LANES)
         labels = labels.reshape(-1, LANES)
-        packed = (edge_src * 2048 + edge_dst).reshape(lines, LANES)
+        lined = [a.reshape(lines, LANES) for a in (edge_src, edge_dst, edge_w)]
         ints = sds((slots, LANES), jnp.int32)
         sided = sds((2 * side, LANES), F32)
         src, dst, w_lines, used, counts, count, need = call(
             functools.partial(prep_kernel, num_dev, PREP_CHUNK, rows), "prep",
-            [ints, ints, sds((slots, LANES), F32), sided, sds((2,), jnp.int32), one, one], [VMEM] * 3,
+            [ints, ints, sds((slots, LANES), F32), sided, sds((2,), jnp.int32), one, sds((1,), jnp.int32)], [VMEM] * 4,
             [(6 * slots, LANES), (6 * lines, LANES), pltpu.VMEM((4 * lines, LANES), jnp.int32), sided.shape, (2, LANES), (num_dev - 1, 2, LANES)]
             + [dma((num_dev - 1,))] * 2,
-            out_specs=[VMEM] * 4 + [SMEM, VMEM, VMEM], vmem=8, collective=0,
-        )(packed, edge_w.reshape(lines, LANES), mask)
+            out_specs=[VMEM] * 4 + [SMEM, VMEM, SMEM], vmem=60, collective=0,
+        )(*lined, mask)
 
         def run(limit):
             compact = limit < halo
@@ -725,8 +726,8 @@
             )(back, n_back, slot, got_prev, got_next, part, x)
             return grad_one, grad_two, loss
 
-        few = halo * 5 // 8
-        grad_one, grad_two, loss = lax.cond(need[0, 0] > few, lambda: run(halo), lambda: run(few))
+        few = halo // 32 * 19
+        grad_one, grad_two, loss = lax.cond(need.reshape(()) > few, lambda: run(halo), lambda: run(few))
         unit = SUB * num_dev
         lines = 2 * (x.shape[1] + -(-classes // SUB) * SUB) + SUB
         lines = -(-lines // unit) * unit

time: 123 us -> 125 us (1.016)
  Pallas kernels: 94 us -> 108 us
  waiting for transfers between devices: 9.91 us -> 2.17 us
  starting transfers between devices: 11.7 us -> 10 us
  local copies, waits for them, and re-layouts: 2.63 us -> 1.35 us
    pallas_call x2, Pallas kernels: 16.2 us -> 23.8 us  [run(): part = local_back(counts, flat, flat_dst, w, grad)]
    pallas_call x1, Pallas kernels: 20.7 us -> 14.8 us  [step(): call(functools.partial(reduce_kernel, num_dev), 'reduce', [sds(grad_one.s...]
    pallas_call x1, Pallas kernels: 8.07 us -> 11.9 us  [run(): part = local(counts, flat, flat_dst, w, tab_one)]
    pallas_call x1, Pallas kernels: 8.07 us -> 11.9 us  [run(): part = local(counts, flat, flat_dst, w, tab_two)]
    ppermute x2, waiting for transfers between devices: 4.13 us -> 0.53 us  [run(): from_prev = lax.ppermute(to_n, AXIS, to_next)]
    ppermute x2, waiting for transfers between devices: 3.9 us -> 1.62 us  [run(): got_prev = lax.ppermute(to_p, AXIS, to_prev)]
    ppermute x2, waiting for transfers between devices: 1.88 us -> 0.01 us  [run(): got_next = lax.ppermute(to_n, AXIS, to_next)]
    pallas_call x1, Pallas kernels: 7.21 us -> 9.07 us  [run(): call(functools.partial(loss_kernel, limit, 4, chunk_h, classes), 'loss',...]
  transfers between devices with their start and end apart: 8 -> 8, of which waited for: 5 -> 2; matrix products, arithmetic and copies ran while one was open for 0% -> 0% of each run, Pallas kernels for 26% -> 38%
where the time goes in v5:
time: 125 us
  Pallas kernels  108 us (86%)
  starting transfers between devices  10 us (8%)
  between operations  3.1 us (2%)
  waiting for transfers between devices  2.17 us (2%)
  local copies, waits for them, and re-layouts  1.35 us (1%)
    pallas_call x2, Pallas kernels, run(): part = local_back(counts, flat, flat_dst, w, grad)  23.8 us
    pallas_call x1, Pallas kernels, step(): call(functools.partial(reduce_kernel, num_dev), 'reduce', [sds(grad_one.s...  14.8 us
    pallas_call x1, Pallas kernels, run(): part = local(counts, flat, flat_dst, w, tab_one)  11.9 us
    pallas_call x1, Pallas kernels, run(): part = local(counts, flat, flat_dst, w, tab_two)  11.9 us
    pallas_call x1, Pallas kernels, step(): call(functools.partial(prep_kernel, num_dev, PREP_CHUNK, rows), 'prep', [...  10.7 us
    pallas_call x1, Pallas kernels, run(): call(functools.partial(loss_kernel, limit, 4, chunk_h, classes), 'loss',...  9.07 us
    pallas_call x1, Pallas kernels, run(): call(functools.partial(middle_kernel, limit, chunk_h), 'middle', [sds(w2_...  8.24 us
    pallas_call x1, Pallas kernels, run(): call(functools.partial(hidden_kernel, chunk_h), 'hidden', [sds((rows, 2 *...  7.41 us
  transfers between devices with their start and end apart: 8, of which 2 were waited for; matrix products, arithmetic and copies ran while one was open for 0% of the time, Pallas kernels for 38%

profile of v5, /device:TPU:0, one launch (start us, length us, event | category | flops | bytes accessed | tf_op | source)
XLA Modules:
  0.0 125.4 jit_solution(15313358991252158069)
XLA Ops:
  0.6 0.0 copy-start
  0.6 0.0 copy-start.1
  0.7 0.0 copy-start.2
  0.7 0.0 copy-start.3
  0.7 0.0 copy-start.4
  0.7 0.0 copy-start.5
  0.7 10.7 %prep.1 = (s32[72,128]{1,0:T(8,128)S(1)}, s32[72,128]{1,0:T(8,128)S(1)}, f32[72,128]{1,0:T(8,128)S(1)}, f32[16,128]{1,0:T(8,128)S(1)}, s32[2]{0:T(128)S(1)}, /*index=5*/f32[8,128]{1,0:T(8,128)S(1)}, s32[1]{0:T(128)}) custom-call(s32[64,128]{1,0:T(8,128)} %bitcast.28, s32[64,128]{1,0:T(8,128)} %bitcast.29, f32[64,128]{1,0:T(8,128)} %bitcast.30, ...), custom_call_target="tpu_custom_call" | custom-call | flops 10000000000 | bytes 10000000 | tf_op jit(solution)/shard_map/prep/pallas_call | solution.py:670
  12.0 0.0 copy-done
  12.0 0.0 copy-done.1
  12.0 0.0 copy-done.2
  12.0 0.0 copy-done.3
  12.1 0.0 copy-done.4
  12.1 0.0 copy-done.5
  12.1 95.4 %conditional.1 = (f32[128,256]{1,0:T(8,128)S(1)}, f32[256,256]{1,0:T(8,128)S(1)}, f32[8,128]{1,0:T(8,128)S(1)}) conditional(s32[]{:T(128)} %bitcast.12, (s32[72,128]{1,0:T(8,128)S(1)}, s32[72,128]{1,0:T(8,128)S(1)}, bf16[2048,128]{1,0:T(8,128)(2,1)S(1)}, f32[128,256]{1,0:T(8,128)S(1)}, s32[2,1024]{1,0:T(2,128)S(1)}, /*index=5*/s32[2]{0:T(128)S(1)}, ...), branch_computations={%region_0.0_spmd, %region_1.0_spmd} | conditional | flops 89999998976 | bytes 112053208 | solution.py:730
  12.1 7.0 %first.2 = (f32[4096,128]{1,0:T(8,128)S(1)}, bf16[1024,256]{1,0:T(8,128)(2,1)S(1)}, bf16[1024,256]{1,0:T(8,128)(2,1)S(1)}, f32[9216,128]{1,0:T(8,128)S(1)}, s32[...) custom-call(bf16[2048,128]{1,0:T(8,128)(2,1)S(1)} %get-tuple-element.51.x, f32[128,256]{1,0:T(8,128)S(1)} %get-tuple-element.52.w1, ...), custom_call_target="tpu_custom_call" | custom-call | flops 10000000000 | bytes 10000000 | tf_op jit(solution)/shard_map/cond/branch_0_fun/first/pallas_call | solution.py:682
  19.1 0.1 collective-permute-start
  19.2 3.5 %collective-permute-start.1 = (bf16[1024,256]{1,0:T(8,128)(2,1)S(1)}, bf16[1024,256]{1,0:T(8,128)(2,1)S(1)}, u32[]{:S(2)}, u32[]{:S(2)}) collective-permute-start(bf16[1024,256]{1,0:T(8,128)(2,1)S(1)} %get-tuple-element.58), channel_id=1, source_target_pairs={{0,15},{1,0},{2,1},{3,2},{4,3},{5,4},{6,5},{7,6},{8,7},{9,8},{10,9... | collective-permute-start | bytes 1572872 | tf_op jit(solution)/shard_map/cond/branch_0_fun/ppermute | solution.py:687
  22.7 11.9 %local_edges.8.part = f32[4096,128]{1,0:T(8,128)S(1)} custom-call(s32[2]{0:T(128)S(1)} %get-tuple-element.48.counts, s32[9216]{0:T(1024)S(1)} %bitcast.36, s32[9216]{0:T(1024)S(1)} %bitcast.48, f32[9216,128]{1,0:T(8,128)S(1)} %get-tuple-element.56.w, f32[4096,128]{1,0:T(8,128)S(1)} %get-tuple-element.59.table), custom_call_target="tpu_custom_call" | custom-call | flops 10000000000 | bytes 10000000 | tf_op jit(solution)/shard_map/cond/branch_0_fun/local_edges/pallas_call | solution.py:699
  34.6 0.5 collective-permute-done.from_prev
  35.1 0.0 collective-permute-done.1.from_next
  35.1 7.4 %hidden.2 = (bf16[2048,256]{1,0:T(8,128)(2,1)S(1)}, f32[4096,128]{1,0:T(8,128)S(1)}, bf16[1536,128]{1,0:T(8,128)(2,1)S(1)}, bf16[1536,128]{1,0:T(8,128)(2,1)S(1)}, s32[16,128]{1,0:T(8,128)S(1)}) custom-call(s32[2]{0:T(128)S(1)} %get-tuple-element.48.counts, s32[9216]{0:T(1024)S(1)} %bitcast.37, s32[9216]{0:T(1024)S(1)} %bitcast.49, ...), custom_call_target="tpu_custom_call" | custom-call | flops 10000000000 | bytes 10000000 | tf_op jit(solution)/shard_map/cond/branch_0_fun/hidden/pallas_call | solution.py:700
  42.6 0.1 collective-permute-start.2
  42.6 3.5 %collective-permute-start.3 = (bf16[1536,128]{1,0:T(8,128)(2,1)S(1)}, bf16[1536,128]{1,0:T(8,128)(2,1)S(1)}, u32[]{:S(2)}, u32[]{:S(2)}) collective-permute-start(bf16[1536,128]{1,0:T(8,128)(2,1)S(1)} %get-tuple-element.66), channel_id=1, source_target_pairs={{0,15},{1,0},{2,1},{3,2},{4,3},{5,4},{6,5},{7,6},{8,7},{9,8},{10,9... | collective-permute-start | bytes 1179656 | tf_op jit(solution)/shard_map/cond/branch_0_fun/ppermute | solution.py:706
  46.1 11.9 %local_edges.9.part = f32[4096,128]{1,0:T(8,128)S(1)} custom-call(s32[2]{0:T(128)S(1)} %get-tuple-element.48.counts, s32[9216]{0:T(1024)S(1)} %bitcast.38, s32[9216]{0:T(1024)S(1)} %bitcast.50, f32[9216,128]{1,0:T(8,128)S(1)} %get-tuple-element.56.w, f32[4096,128]{1,0:T(8,128)S(1)} %get-tuple-element.67.table), custom_call_target="tpu_custom_call" | custom-call | flops 10000000000 | bytes 10000000 | tf_op jit(solution)/shard_map/cond/branch_0_fun/local_edges/pallas_call | solution.py:708
  58.0 0.0 collective-permute-done.2.from_prev
  58.0 0.0 collective-permute-done.3.from_next
  58.0 9.1 %loss.2 = (f32[8,128]{1,0:T(8,128)S(1)}, f32[4096,128]{1,0:T(8,128)S(1)}, f32[920,128]{1,0:T(8,128)S(1)}, f32[920,128]{1,0:T(8,128)S(1)}) custom-call(s32[2]{0:T(128)S(1)} %get-tuple-element.48.counts, s32[9216]{0:T(1024)S(1)} %bitcast.39, s32[9216]{0:T(1024)S(1)} %bitcast.51, f32[9216,128]{1,0:T(8,128)S(1)} %get-tuple-element.56.w, s32[9216]{0:T(1024)S(1)} %bitcast.18, ...), custom_call_target="tpu_custom_call" | custom-call | flops 10000000000 | bytes 10000000 | tf_op jit(solution)/shard_map/cond/branch_0_fun/loss/pallas_call | solution.py:709
  67.1 0.1 collective-permute-start.4
  67.2 0.5 collective-permute-start.5
  67.7 11.9 %local_edges.10.part = f32[4096,128]{1,0:T(8,128)S(1)} custom-call(s32[2]{0:T(128)S(1)} %get-tuple-element.48.counts, s32[9216]{0:T(1024)S(1)} %bitcast.40, s32[9216]{0:T(1024)S(1)} %bitcast.52, f32[9216,128]{1,0:T(8,128)S(1)} %get-tuple-element.56.w, f32[4096,128]{1,0:T(8,128)S(1)} %get-tuple-element.72.table), custom_call_target="tpu_custom_call" | custom-call | flops 10000000000 | bytes 10000000 | tf_op jit(solution)/shard_map/cond/branch_0_fun/local_edges/pallas_call | solution.py:715
  79.6 0.0 collective-permute-done.4.got_prev
  79.6 0.0 collective-permute-done.5.got_next
  79.6 8.2 %middle.2 = (f32[256,256]{1,0:T(8,128)S(1)}, f32[4096,128]{1,0:T(8,128)S(1)}, f32[1216,128]{1,0:T(8,128)S(1)}, f32[1216,128]{1,0:T(8,128)S(1)}, s32[16,128]{1,0:T(8,128)S(1)}, /*index=5*/s32[2]{0:T(128)S(1)}) custom-call(s32[2]{0:T(128)S(1)} %get-tuple-element.48.counts, s32[9216]{0:T(1024)S(1)} %bitcast.19, s32[9216]{0:T(1024)S(1)} %bitcast.53, ...), custom_call_target="tpu_custom_call" | custom-call | flops 10000000000 | bytes 10000000 | tf_op jit(solution)/shard_map/cond/branch_0_fun/middle/pallas_call | solution.py:716
  87.8 2.3 %collective-permute-start.6 = (f32[1216,128]{1,0:T(8,128)S(1)}, f32[1216,128]{1,0:T(8,128)S(1)}, u32[]{:S(2)}, u32[]{:S(2)}) collective-permute-start(f32[1216,128]{1,0:T(8,128)S(1)} %get-tuple-element.76), channel_id=1, source_target_pairs={{0,15},{1,0},{2,1},{3,2},{4,3},{5,4},{6,5},{7,6},{8,7},{9,8},{10,9... | collective-permute-start | bytes 1867784 | tf_op jit(solution)/shard_map/cond/branch_0_fun/ppermute | solution.py:721
  90.1 0.0 collective-permute-start.7
  90.1 11.9 %local_edges.11.part = f32[4096,128]{1,0:T(8,128)S(1)} custom-call(s32[2]{0:T(128)S(1)} %get-tuple-element.48.counts, s32[9216]{0:T(1024)S(1)} %bitcast.41, s32[9216]{0:T(1024)S(1)} %bitcast.54, f32[9216,128]{1,0:T(8,128)S(1)} %get-tuple-element.56.w, f32[4096,128]{1,0:T(8,128)S(1)} %get-tuple-element.78.table), custom_call_target="tpu_custom_call" | custom-call | flops 10000000000 | bytes 10000000 | tf_op jit(solution)/shard_map/cond/branch_0_fun/local_edges/pallas_call | solution.py:723
  102.0 1.6 %collective-permute-done.6.got_prev = f32[1216,128]{1,0:T(8,128)S(1)} collective-permute-done((f32[1216,128]{1,0:T(8,128)S(1)}, f32[1216,128]{1,0:T(8,128)S(1)}, u32[]{:S(2)}, u32[]{:S(2)}) %collective-permute-start.6) | collective-permute-done | bytes 622624 | tf_op jit(solution)/shard_map/cond/branch_0_fun/ppermute | solution.py:721
  103.6 0.0 collective-permute-done.7.got_next
  103.6 3.6 %last.2 = f32[128,256]{1,0:T(8,128)S(1)} custom-call(s32[2048]{0:T(1024)S(1)} %bitcast.23, s32[2]{0:T(128)S(1)} %get-tuple-element.74.n_back, s32[16,128]{1,0:T(8,128)S(1)} %get-tuple-element.75.slots, f32[1216,128]{1,0:T(8,128)S(1)} %collective-permute-done.6.got_prev, f32[1216,128]{1,0:T(8,128)S(1)} %collective-permute-done.7.got_next, ...), custom_call_target="tpu_custom_call" | custom-call | flops 10000000000 | bytes 10000000 | tf_op jit(solution)/shard_map/cond/branch_0_fun/last/pallas_call | solution.py:724
  107.5 14.8 %reduce.1 = (f32[128,256]{1,0:T(8,128)S(1)}, f32[172,256]{1,0:T(8,128)S(1)}, f32[1,1]{1,0:T(1,128)}) custom-call(f32[128,256]{1,0:T(8,128)S(1)} %get-tuple-element.137.one, f32[256,256]{1,0:T(8,128)S(1)} %get-tuple-element.138.two, f32[8,128]{1,0:T(8,128)S(1)} %get-tuple-element.139.loss, f32[8,128]{1,0:T(8,128)S(1)} %get-tuple-element.136.count), custom_call_target="tpu_custom_call" | custom-call | flops 10000000000 | bytes 10000000 | tf_op jit(solution)/shard_map/reduce/pallas_call | solution.py:734
  123.0 0.7 copy.22
  123.6 0.7 copy.23
Async XLA Ops:
  0.6 11.4 %copy-start = (bf16[2048,128]{1,0:T(8,128)(2,1)S(1)}, bf16[2048,128]{1,0:T(8,128)(2,1)}, u32[]{:S(2)}) copy-start(bf16[2048,128]{1,0:T(8,128)(2,1)} %param.11) | copy-start | bytes 1572868
  0.6 11.4 %copy-start.1 = (f32[256,172]{0,1:T(8,128)S(1)}, f32[256,172]{0,1:T(8,128)}, u32[]{:S(2)}) copy-start(f32[256,172]{0,1:T(8,128)} %param.13) | copy-start | bytes 528388
  0.7 11.4 %copy-start.2 = (f32[128,256]{1,0:T(8,128)S(1)}, f32[128,256]{1,0:T(8,128)}, u32[]{:S(2)}) copy-start(f32[128,256]{1,0:T(8,128)} %param.12) | copy-start | bytes 393220
  0.7 11.4 %copy-start.3 = (s32[2048]{0:T(1024)S(1)}, s32[2048]{0:T(1024)}, u32[]{:S(2)}) copy-start(s32[2048]{0:T(1024)} %param.19) | copy-start | bytes 24580
  0.7 11.4 %copy-start.4 = (s32[2,1024]{1,0:T(2,128)S(1)}, s32[2,1024]{1,0:T(2,128)}, u32[]{:S(2)}) copy-start(s32[2,1024]{1,0:T(2,128)} %param.14) | copy-start | bytes 24580
  0.7 11.4 %copy-start.5 = (s32[2048]{0:T(1024)S(1)}, s32[2048]{0:T(1024)}, u32[]{:S(2)}) copy-start(s32[2048]{0:T(1024)} %param.18) | copy-start | bytes 24580
  19.1 16.0 %collective-permute-start = (bf16[1024,256]{1,0:T(8,128)(2,1)S(1)}, bf16[1024,256]{1,0:T(8,128)(2,1)S(1)}, u32[]{:S(2)}, u32[]{:S(2)}) collective-permute-start(bf16[1024,256]{1,0:T(8,128)(2,1)S(1)} %get-tuple-element.57), channel_id=1, source_target_pairs={{0,1},{1,2},{2,3},{3,4},{4,5},{5,6},{6,7},{7,8},{8,9},{9,10},{10,1... | collective-permute-start | bytes 1572872 | tf_op jit(solution)/shard_map/cond/branch_0_fun/ppermute | solution.py:686
  19.2 16.0 %collective-permute-start.1 = (bf16[1024,256]{1,0:T(8,128)(2,1)S(1)}, bf16[1024,256]{1,0:T(8,128)(2,1)S(1)}, u32[]{:S(2)}, u32[]{:S(2)}) collective-permute-start(bf16[1024,256]{1,0:T(8,128)(2,1)S(1)} %get-tuple-element.58), channel_id=1, source_target_pairs={{0,15},{1,0},{2,1},{3,2},{4,3},{5,4},{6,5},{7,6},{8,7},{9,8},{10,9... | collective-permute-start | bytes 1572872 | tf_op jit(solution)/shard_map/cond/branch_0_fun/ppermute | solution.py:687
  42.6 15.5 %collective-permute-start.2 = (bf16[1536,128]{1,0:T(8,128)(2,1)S(1)}, bf16[1536,128]{1,0:T(8,128)(2,1)S(1)}, u32[]{:S(2)}, u32[]{:S(2)}) collective-permute-start(bf16[1536,128]{1,0:T(8,128)(2,1)S(1)} %get-tuple-element.65), channel_id=1, source_target_pairs={{0,1},{1,2},{2,3},{3,4},{4,5},{5,6},{6,7},{7,8},{8,9},{9,10},{10,1... | collective-permute-start | bytes 1179656 | tf_op jit(solution)/shard_map/cond/branch_0_fun/ppermute | solution.py:705
  42.6 15.4 %collective-permute-start.3 = (bf16[1536,128]{1,0:T(8,128)(2,1)S(1)}, bf16[1536,128]{1,0:T(8,128)(2,1)S(1)}, u32[]{:S(2)}, u32[]{:S(2)}) collective-permute-start(bf16[1536,128]{1,0:T(8,128)(2,1)S(1)} %get-tuple-element.66), channel_id=1, source_target_pairs={{0,15},{1,0},{2,1},{3,2},{4,3},{5,4},{6,5},{7,6},{8,7},{9,8},{10,9... | collective-permute-start | bytes 1179656 | tf_op jit(solution)/shard_map/cond/branch_0_fun/ppermute | solution.py:706
  67.1 12.4 %collective-permute-start.4 = (f32[920,128]{1,0:T(8,128)S(1)}, f32[920,128]{1,0:T(8,128)S(1)}, u32[]{:S(2)}, u32[]{:S(2)}) collective-permute-start(f32[920,128]{1,0:T(8,128)S(1)} %get-tuple-element.70), channel_id=1, source_target_pairs={{0,15},{1,0},{2,1},{3,2},{4,3},{5,4},{6,5},{7,6},{8,7},{9,8},{10,9... | collective-permute-start | bytes 1413128 | tf_op jit(solution)/shard_map/cond/branch_0_fun/ppermute | solution.py:713
  67.2 12.4 %collective-permute-start.5 = (f32[920,128]{1,0:T(8,128)S(1)}, f32[920,128]{1,0:T(8,128)S(1)}, u32[]{:S(2)}, u32[]{:S(2)}) collective-permute-start(f32[920,128]{1,0:T(8,128)S(1)} %get-tuple-element.71), channel_id=1, source_target_pairs={{0,1},{1,2},{2,3},{3,4},{4,5},{5,6},{6,7},{7,8},{8,9},{9,10},{10,1... | collective-permute-start | bytes 1413128 | tf_op jit(solution)/shard_map/cond/branch_0_fun/ppermute | solution.py:714
  87.8 15.8 %collective-permute-start.6 = (f32[1216,128]{1,0:T(8,128)S(1)}, f32[1216,128]{1,0:T(8,128)S(1)}, u32[]{:S(2)}, u32[]{:S(2)}) collective-permute-start(f32[1216,128]{1,0:T(8,128)S(1)} %get-tuple-element.76), channel_id=1, source_target_pairs={{0,15},{1,0},{2,1},{3,2},{4,3},{5,4},{6,5},{7,6},{8,7},{9,8},{10,9... | collective-permute-start | bytes 1867784 | tf_op jit(solution)/shard_map/cond/branch_0_fun/ppermute | solution.py:721
  90.1 13.5 %collective-permute-start.7 = (f32[1216,128]{1,0:T(8,128)S(1)}, f32[1216,128]{1,0:T(8,128)S(1)}, u32[]{:S(2)}, u32[]{:S(2)}) collective-permute-start(f32[1216,128]{1,0:T(8,128)S(1)} %get-tuple-element.77), channel_id=1, source_target_pairs={{0,1},{1,2},{2,3},{3,4},{4,5},{5,6},{6,7},{7,8},{8,9},{9,10},{10,1... | collective-permute-start | bytes 1867784 | tf_op jit(solution)/shard_map/cond/branch_0_fun/ppermute | solution.py:722

commit v6 on v5

--- a/solution.py
+++ b/solution.py
@@ -23,7 +23,7 @@
 SQUARE = (LANES, LANES)
 PREP_CHUNK = 64
 SMALL = PREP_CHUNK
-SEGMENT = 1024
+SEGMENT = 384
 MESH = pl.DeviceIdType.MESH
 
 
@@ -48,52 +48,58 @@
 
 class Edges:
     def __init__(self, first, last, w, arrays, smem, sems):
-        self.first, self.last, self.w = first, last, w
-        self.pairs = tuple(zip(arrays, smem))
-        self.sems = sems
+        self.first, self.last, self.w, self.sems = first, last, w, sems
+        self.size = smem[0].shape[0]
+        self.smem = [smem[k * SUB : (k + 1) * SUB] for k in range(len(arrays))]
+        self.arrays = arrays
 
     def copies(self, seg):
-        part = pl.ds(pl.multiple_of(seg * SEGMENT, SEGMENT), SEGMENT)
-        return [pltpu.make_async_copy(a.at[part], b.at[part], self.sems.at[i, seg]) for i, (a, b) in enumerate(self.pairs)]
+        done = []
+        for a, parts in zip(self.arrays, self.smem):
+            for t, part in enumerate(parts):
+                start = pl.multiple_of(seg * SEGMENT, LANES)
+                src = a.at[pl.ds(pl.multiple_of(t * self.size + start, LANES), SEGMENT)]
+                done.append(pltpu.make_async_copy(src, part.at[pl.ds(start, SEGMENT)], self.sems.at[len(done), seg]))
+        return done
 
     def fetch(self):
-        per = SEGMENT // PREP_CHUNK
-        for seg in range(self.pairs[0][1].shape[0] // SEGMENT):
+        per = SEGMENT * SUB // PREP_CHUNK
+        for seg in range(self.size // SEGMENT):
 
             @pl.when(jnp.logical_and(seg * per < self.last, (seg + 1) * per > self.first))
             def _():
                 for c in self.copies(seg):
                     c.start()
 
-    def walk(self, chunk, from_idx, to_idx, table, accs, wait):
-        group, per, ratio = len(accs), SEGMENT // chunk, PREP_CHUNK // chunk
-        first, last = self.first * ratio, self.last * ratio
+    def walk(self, source, target, table, accs, wait):
+        group, per, rows = len(accs), SEGMENT * SUB // PREP_CHUNK, PREP_CHUNK // SUB
+        from_idx, to_idx = self.smem[source], self.smem[target]
 
         def body(c, _):
-            base = c * chunk
-            w_chunk = self.w.at[pl.ds(pl.multiple_of(base, chunk), chunk)]
-            for g in range(0, chunk, group):
-                pend = []
-                for u in range(group):
-                    k = base + g + u
-                    s = pl.multiple_of(from_idx[k], 2)
-                    d = pl.multiple_of(to_idx[k], 2)
-                    pend.append((d, accs[u][pl.ds(d, 2), :] + table[pl.ds(s, 2), :] * w_chunk[g + u : g + u + 1, :]))
-                for u in range(group):
-                    accs[u][pl.ds(pend[u][0], 2), :] = pend[u][1]
+            weights = [self.w.at[pl.ds(pl.multiple_of(c * rows + t * self.size, SUB), rows)] for t in range(SUB)]
+            for v in range(rows):
+                i = c * rows + v
+                for g in range(0, SUB, group):
+                    pend = []
+                    for u in range(group):
+                        s = pl.multiple_of(from_idx[g + u][i], 2)
+                        d = pl.multiple_of(to_idx[g + u][i], 2)
+                        pend.append((d, accs[u][pl.ds(d, 2), :] + table[pl.ds(s, 2), :] * weights[g + u][v : v + 1, :]))
+                    for u in range(group):
+                        accs[u][pl.ds(pend[u][0], 2), :] = pend[u][1]
             return 0
 
         if not wait:
-            lax.fori_loop(first, last, body, 0)
+            lax.fori_loop(self.first, self.last, body, 0)
             return
 
         def segment(seg, _):
             for c in self.copies(seg):
                 c.wait()
-            lax.fori_loop(jnp.maximum(first, seg * per), jnp.minimum(last, (seg + 1) * per), body, 0)
+            lax.fori_loop(jnp.maximum(self.first, seg * per), jnp.minimum(self.last, (seg + 1) * per), body, 0)
             return 0
 
-        lax.fori_loop(first // per, (last + per - 1) // per, segment, 0)
+        lax.fori_loop(self.first // per, (self.last + per - 1) // per, segment, 0)
 
 
 def one_hot_rows(idx, which, start, table):
@@ -129,11 +135,12 @@
     return got
 
 
-def gather_rows(send, idx, table_b, table, buf, to_prev, to_next):
+def gather_rows(send, idx, table_b, table, buf, to_prev, to_next, also):
     @pl.loop(0, to_prev.shape[0], step=BLOCK)
     def _(i):
         i = pl.multiple_of(i, BLOCK)
         to_prev[pl.ds(i, BLOCK), :] = gather_block(send, idx, i, table_b, table, buf).astype(BF16)
+        also(i)
 
     @pl.loop(0, to_next.shape[0], step=BLOCK)
     def _(i):
@@ -247,21 +254,22 @@
     low, high = rank & (LANES - 1), rank >> 7
     table = stack_rows([low.astype(F32), high.astype(F32)]).astype(BF16)
 
-    quad = 4
-
-    def four(c, _):
-        slot = [src[pl.ds(c * quad + q, 1), :] >> 1 for q in range(quad)]
+    per = src.shape[0] // SUB
+
+    def eight(c, _):
+        rows = [pl.ds(t * per + c, 1) for t in range(SUB)]
+        slot = [src[r, :] >> 1 for r in rows]
         spots = stack_lanes([(down(SQUARE) == (t & (LANES - 1))).astype(F32) for t in slot]).astype(BF16)
         got = dot(table, spots)
         h = stack_lanes(slot) >> 7
         got = jnp.where(down(got[:lines].shape) == h, got[:lines] + LANES * got[lines:], 0.0)
         got = (jnp.sum(got, axis=0, keepdims=True).astype(jnp.int32) + jnp.where(h >= side, halo, 0)) * 2
-        for q in range(quad):
-            src_back[pl.ds(c * quad + q, 1), :] = got[:, q * LANES : (q + 1) * LANES]
+        for q, r in enumerate(rows):
+            src_back[r, :] = got[:, q * LANES : (q + 1) * LANES]
         return 0
 
-    ratio = quad * LANES // PREP_CHUNK
-    lax.fori_loop(counts[0] // ratio, (counts[1] + ratio - 1) // ratio, four, 0)
+    ratio = SUB * LANES // PREP_CHUNK
+    lax.fori_loop(counts[0] // ratio, (counts[1] + ratio - 1) // ratio, eight, 0)
     for k in range(2):
         acc = jnp.zeros((24, LANES), F32)
         for hh in range(side):
@@ -269,7 +277,7 @@
             pick = jnp.where(down(TILE) == high[q : q + 1, :], used[q : q + 1, :], 0.0)
             lhs = stack_rows([pick * across(TILE).astype(F32), pick * hh, pick]).astype(BF16)
             acc += dot(lhs, (down(SQUARE) == low[q : q + 1, :]).astype(F32).astype(BF16), COLS_A)
-        slots = acc[0:8] + LANES * acc[8:16]
+        slots = acc[:SUB] + LANES * acc[SUB:16]
         lists[k * side : (k + 1) * side, :] = jnp.where(acc[16:24] > 0.0, slots[:side], -1.0)
 
 
@@ -286,11 +294,6 @@
         tab_b[pl.ds(i, BLOCK), :] = t
         t = t.astype(F32)
         put_halves(tab, i, BLOCK, t[:, :LANES], t[:, LANES:])
-
-    @pl.loop(0, w.shape[0] // SUB)
-    def _(r):
-        for q in range(SUB):
-            w_out[pl.ds(pl.multiple_of((r * SUB + q) * LANES, LANES), LANES), :] = spread(w[pl.ds(r * SUB + q, 1), :])
 
     src_back[...] = src[...]
     if compact:
@@ -301,7 +304,14 @@
         lists[...] = (line * LANES + across(lists.shape)).astype(F32)
     for c in fetch:
         c.wait()
-    gather_rows(send, idx, tab_b, tab, buf, to_prev, to_next)
+    share = w.shape[0] * BLOCK // halo
+
+    def widen(i):
+        for q in range(share):
+            r = i // BLOCK * share + q
+            w_out[pl.ds(pl.multiple_of(r * LANES, LANES), LANES), :] = spread(w[pl.ds(r, 1), :])
+
+    gather_rows(send, idx, tab_b, tab, buf, to_prev, to_next, widen)
 
 
 def greet(n):
@@ -330,7 +340,7 @@
     classes = two_out.shape[0]
     lines = -(-classes // SUB) * SUB
     top, wide = one.shape
-    work[0:top, :] = one[:, :LANES]
+    work[:top, :] = one[:, :LANES]
     work[top : 2 * top, :] = one[:, LANES:]
     work[2 * top : 2 * top + lines, :] = two[:lines, :LANES]
     work[2 * top + lines : 2 * top + 2 * lines, :] = two[:lines, LANES:]
@@ -374,11 +384,11 @@
         c.wait_send()
     for c in forward:
         c.wait()
-    one_out[:, :LANES] = full[0:top, :]
+    one_out[:, :LANES] = full[:top, :]
     one_out[:, LANES:] = full[top : 2 * top, :]
     two_out[:, :LANES] = full[2 * top : 2 * top + classes, :]
     two_out[:, LANES:] = full[2 * top + lines : 2 * top + lines + classes, :]
-    mean[...] = jnp.sum(full[tail : tail + SUB, :], keepdims=True) / count[0:1, 0:1]
+    mean[...] = jnp.sum(full[tail : tail + SUB, :], keepdims=True) / count[:1, :1]
 
 
 def prep_kernel(n, chunk, rows, src_in, dst_in, w_in, mask, src_out, dst_out, w_out, used, counts, count, need, total, values, places, hits, mine, theirs, send_sem, recv_sem):
@@ -396,6 +406,7 @@
     counts[0] = local_chunks
     counts[1] = local_chunks + (n_halo + chunk - 1) // chunk
     pos = jnp.where(is_local, rank(is_local), jnp.where(is_halo, rank(is_halo) + local_chunks * chunk, -1))
+    pos = jnp.where(pos < 0, pos, (pos & (SUB - 1)) * (slots * LANES // SUB) + (pos >> 3))
     s = jnp.where(halo, src - rows, src)
     w_a = half_w.astype(BF16).astype(F32)
     w_b = (half_w - w_a).astype(BF16).astype(F32)
@@ -457,34 +468,40 @@
     need[0] = jnp.max(jnp.maximum(mine[1:, :], jnp.max(theirs[:, 1:, :], axis=0))).astype(jnp.int32)
 
 
-def local_kernel(chunk, backward, counts, src, dst, w, table, out, src_s, dst_s, sems, *accs):
-    edges = Edges(0, counts[0], w, (src, dst), (src_s, dst_s), sems)
+def split_scratch(scratch, arrays):
+    n = arrays * SUB
+    return scratch[:n], scratch[n], scratch[n + 1 :]
+
+
+def local_kernel(backward, counts, src, dst, w, table, out, *scratch):
+    smem, sems, accs = split_scratch(scratch, 2)
+    edges = Edges(0, counts[0], w, (src, dst), smem, sems)
     edges.fetch()
     for a in accs:
         fill_zero(a)
-    edges.walk(chunk, *((dst_s, src_s) if backward else (src_s, dst_s)), table, accs, True)
+    edges.walk(int(backward), int(not backward), table, accs, True)
 
     @pl.loop(0, out.shape[0], step=STEP)
     def _(i):
         out[pl.ds(i, STEP), :] = functools.reduce(jnp.add, [a[pl.ds(i, STEP), :] for a in accs])
 
 
-def forward_halo(chunk, edges, src_s, dst_s, from_prev, from_next, part, htab, accs, unpack):
+def forward_halo(edges, from_prev, from_next, part, htab, accs, unpack):
     edges.fetch()
     unpack(from_prev, htab, 0)
     unpack(from_next, htab, htab.shape[0] // 4)
     copy_in(accs[0], part)
     for a in accs[1:]:
         fill_zero(a)
-    edges.walk(chunk, src_s, dst_s, htab, accs, True)
-
-
-def backward_halo(limit, chunk, edges, src_s, dst_s, grad, back_prev, back_next, accs, wait, lists=None):
+    edges.walk(0, 1, htab, accs, True)
+
+
+def backward_halo(limit, edges, target, grad, back_prev, back_next, accs, wait, lists=None):
     split = accs[0].shape[0] // 2
     for a in accs:
         for start in (0, split):
             fill_zero(a.at[pl.ds(start, limit * 2)])
-    edges.walk(chunk, dst_s, src_s, grad, accs, wait)
+    edges.walk(1, target, grad, accs, wait)
     if lists is None:
 
         @pl.loop(0, back_prev.shape[0], step=SMALL)
@@ -509,20 +526,21 @@
 def padded(w, buf):
     low = w.shape[0] // SUB * SUB
     buf[low:, :] = jnp.zeros((buf.shape[0] - low, buf.shape[1]), F32)
-    buf[0 : w.shape[0], :] = w[...]
+    buf[:w.shape[0], :] = w[...]
     return buf[...].astype(BF16)
 
 
-def hidden_kernel(chunk, counts, src, dst, w, send, from_prev, from_next, part, w2, hid, tab, to_prev, to_next, back, htab, tab_b, w2_pad, buf, idx, idx_sems, src_s, dst_s, sems, *accs):
+def hidden_kernel(counts, src, dst, w, send, from_prev, from_next, part, w2, hid, tab, to_prev, to_next, back, htab, tab_b, w2_pad, buf, idx, idx_sems, *scratch):
+    smem, sems, accs = split_scratch(scratch, 2)
     fetch = fetch_index(send, idx, idx_sems)
     for c in fetch:
         c.start()
-    edges = Edges(counts[0], counts[1], w, (src, dst), (src_s, dst_s), sems)
+    edges = Edges(counts[0], counts[1], w, (src, dst), smem, sems)
     w2_b = padded(w2, w2_pad)
     per = send.shape[1] // LANES
     for i in range(2 * per):
         back[i : i + 1, :] = send[i // per : i // per + 1, (i % per) * LANES : (i % per + 1) * LANES] * 2
-    forward_halo(chunk, edges, src_s, dst_s, from_prev, from_next, part, htab, accs, unpack_plain)
+    forward_halo(edges, from_prev, from_next, part, htab, accs, unpack_plain)
 
     @pl.loop(0, hid.shape[0], step=STEP)
     def _(i):
@@ -539,12 +557,13 @@
     gather_packed(send, idx, tab_b, tab, buf, to_prev, to_next)
 
 
-def loss_kernel(limit, quad, chunk, classes, counts, src, dst, w, src_back, lists, count, from_prev, from_next, part, labels, mask, loss, grad, back_prev, back_next, htab, src_s, dst_s, back_s, sems, *accs):
-    edges = Edges(counts[0], counts[1], w, (src, dst, src_back), (src_s, dst_s, back_s), sems)
-    forward_halo(chunk, edges, src_s, dst_s, from_prev, from_next, part, htab, accs, unpack_rows)
+def loss_kernel(limit, quad, classes, counts, src, dst, w, src_back, lists, count, from_prev, from_next, part, labels, mask, loss, grad, back_prev, back_next, htab, *scratch):
+    smem, sems, accs = split_scratch(scratch, 3)
+    edges = Edges(counts[0], counts[1], w, (src, dst, src_back), smem, sems)
+    forward_halo(edges, from_prev, from_next, part, htab, accs, unpack_rows)
     lane = across(SQUARE)
     live = lane < classes - LANES
-    scale = 1.0 / count[0:1, :]
+    scale = 1.0 / count[:1, :]
     loss[...] = jnp.zeros_like(loss)
 
     @pl.loop(0, labels.shape[0], step=quad)
@@ -566,7 +585,7 @@
                 grad, b * LANES, LANES, *(e * share - jnp.where(hit, scale, 0.0) for e, hit in ((exp_even, hit_even), (exp_odd, hit_odd)))
             )
 
-    backward_halo(limit, chunk, edges, back_s, dst_s, grad, back_prev, back_next, accs, False, lists)
+    backward_halo(limit, edges, 2, grad, back_prev, back_next, accs, False, lists)
 
 
 def take_returns(back, slots, counts, part, got_prev, got_next, accs):
@@ -578,8 +597,9 @@
     return [pltpu.make_async_copy(lines.at[i], smem.at[pl.ds(i * LANES, LANES)], sems.at[i]) for i in range(lines.shape[0])]
 
 
-def middle_kernel(limit, chunk, counts, src, dst, w, back, got_prev, got_next, part, hid, w2, grad_two, grad, back_prev, back_next, slots, n_back, returned, w2_pad, slot_s, slot_sems, src_s, dst_s, sems, *accs):
-    edges = Edges(counts[0], counts[1], w, (src, dst), (src_s, dst_s), sems)
+def middle_kernel(limit, counts, src, dst, w, back, got_prev, got_next, part, hid, w2, grad_two, grad, back_prev, back_next, slots, n_back, returned, w2_pad, slot_s, slot_sems, *scratch):
+    smem, sems, accs = split_scratch(scratch, 2)
+    edges = Edges(counts[0], counts[1], w, (src, dst), smem, sems)
     edges.fetch()
     side = slots.shape[0] // 2
     half = (got_prev.shape[0] - side) // 3
@@ -611,7 +631,7 @@
         d_pre = jnp.where(h > 0, d_hid, 0.0)
         put_halves(grad, i, STEP, d_pre[:, :LANES], d_pre[:, LANES:])
 
-    backward_halo(limit, chunk, edges, src_s, dst_s, grad, back_prev, back_next, accs, True)
+    backward_halo(limit, edges, 0, grad, back_prev, back_next, accs, True)
 
 
 def last_kernel(back, n_back, slots, got_prev, got_next, part, x, grad_one, slot_s, slot_sems, *accs):
@@ -657,7 +677,6 @@
         tab_b = pltpu.VMEM((rows, 2 * LANES), BF16)
         one = sds(TILE, F32)
         dma = pltpu.SemaphoreType.DMA
-        chunk_l, chunk_h = 64, 32
         lines = edges // LANES
         slots = lines + 8
         side = halo // LANES
@@ -689,16 +708,16 @@
 
             four = [tab] * 4
             walk = [SMEM, ANY, ANY, VMEM]
-            index = pltpu.SMEM((slots * LANES,), jnp.int32)
-            walk_s = lambda n: [index] * n + [dma((n, slots * LANES // SEGMENT))]
+            size = slots * LANES // SUB
+            walk_s = lambda n: [pltpu.SMEM((size,), jnp.int32)] * (n * SUB) + [dma((n * SUB, size // SEGMENT))]
             slot_s = [pltpu.SMEM((2 * halo,), jnp.int32), dma((2 * side,))]
             local, local_back = (
-                call(functools.partial(local_kernel, chunk_l, back), "local_edges", tab_f, walk + [VMEM], walk_s(2) + four)
+                call(functools.partial(local_kernel, back), "local_edges", tab_f, walk + [VMEM], walk_s(2) + four + four, vmem=22)
                 for back in (False, True)
             )
             part = local(counts, flat, flat_dst, w, tab_one)
             hid, tab_two, to_p, to_n, back = call(
-                functools.partial(hidden_kernel, chunk_h), "hidden",
+                hidden_kernel, "hidden",
                 [sds((rows, 2 * LANES), BF16), tab_f, pack_b, pack_b, sds((2 * side, LANES), jnp.int32)],
                 walk + [VMEM] * 5, [tab, tab_b, w2_pad, half] + list_s + walk_s(2) + four,
             )(counts, flat, flat_dst, w, send, from_prev, from_next, part, w2)
@@ -707,14 +726,14 @@
             back = back.reshape(-1)
             part = local(counts, flat, flat_dst, w, tab_two)
             loss, grad, to_p, to_n = call(
-                functools.partial(loss_kernel, limit, 4, chunk_h, classes), "loss", [one, tab_f, pack_f, pack_f],
+                functools.partial(loss_kernel, limit, 4, classes), "loss", [one, tab_f, pack_f, pack_f],
                 walk + [ANY] + [VMEM] * 7, [tab] + walk_s(3) + four,
             )(counts, flat, flat_dst, w, flat_back, lists, count, from_prev, from_next, part, labels, mask)
             got_prev = lax.ppermute(to_p, AXIS, to_prev)
             got_next = lax.ppermute(to_n, AXIS, to_next)
             part = local_back(counts, flat, flat_dst, w, grad)
             grad_two, grad, to_p, to_n, slot, n_back = call(
-                functools.partial(middle_kernel, limit, chunk_h), "middle",
+                functools.partial(middle_kernel, limit), "middle",
                 [sds(w2_pad, F32), tab_f, half_f, half_f, sds((2 * side, LANES), jnp.int32), sds((2,), jnp.int32)],
                 walk + [SMEM] + [VMEM] * 5, [(4 * limit, LANES), w2_pad] + slot_s + walk_s(2) + four, out_specs=[VMEM] * 5 + [SMEM],
             )(counts, flat_back, flat_dst, w, back, got_prev, got_next, part, hid, w2)

time: 125 us -> 121 us (0.968)
  Pallas kernels: 108 us -> 75.8 us
  waiting for transfers between devices: 2.17 us -> 27.1 us
  starting transfers between devices: 10 us -> 13.6 us
    pallas_call x2, Pallas kernels: 23.8 us -> 11 us  [run(): part = local_back(counts, flat, flat_dst, w, grad)]
    ppermute x2, waiting for transfers between devices: 0.53 us -> 10.1 us  [run(): from_prev = lax.ppermute(to_n, AXIS, to_next)]
    ppermute x2, waiting for transfers between devices: 0.01 us -> 9.16 us  [run(): got_next = lax.ppermute(to_n, AXIS, to_next)]
    pallas_call x1, Pallas kernels: 11.9 us -> 5.51 us  [run(): part = local(counts, flat, flat_dst, w, tab_one)]
    pallas_call x1, Pallas kernels: 11.9 us -> 5.51 us  [run(): part = local(counts, flat, flat_dst, w, tab_two)]
    ppermute x2, waiting for transfers between devices: 1.62 us -> 7.85 us  [run(): got_prev = lax.ppermute(to_p, AXIS, to_prev)]
    ppermute x2, starting transfers between devices: 2.34 us -> 6.39 us  [run(): got_prev = lax.ppermute(to_p, AXIS, to_prev)]
    pallas_call x3, Pallas kernels: 24.7 us -> 20.7 us  [the longest x1 7.33 us: run(): call(functools.partial(middle_kernel, limit), 'middle', [sds(w2_pad, F32)...]
  transfers between devices with their start and end apart: 8 -> 8, of which waited for: 2 -> 6; matrix products, arithmetic and copies ran while one was open for 0% -> 0% of each run, Pallas kernels for 38% -> 18%
where the time goes in v6:
time: 121 us
  Pallas kernels  75.8 us (63%)
  waiting for transfers between devices  27.1 us (22%)
  starting transfers between devices  13.6 us (11%)
  between operations  3.1 us (3%)
  local copies, waits for them, and re-layouts  1.35 us (1%)
    pallas_call x1, Pallas kernels, step(): call(functools.partial(reduce_kernel, num_dev), 'reduce', [sds(grad_one.s...  12.8 us
    pallas_call x2, Pallas kernels, run(): part = local_back(counts, flat, flat_dst, w, grad)  11 us
    pallas_call x1, Pallas kernels, step(): call(functools.partial(prep_kernel, num_dev, PREP_CHUNK, rows), 'prep', [...  10.7 us
    ppermute x2, waiting for transfers between devices, run(): from_prev = lax.ppermute(to_n, AXIS, to_next)  10.1 us
    ppermute x2, waiting for transfers between devices, run(): got_next = lax.ppermute(to_n, AXIS, to_next)  9.16 us
    ppermute x2, waiting for transfers between devices, run(): got_prev = lax.ppermute(to_p, AXIS, to_prev)  7.85 us
    pallas_call x1, Pallas kernels, run(): call(functools.partial(middle_kernel, limit), 'middle', [sds(w2_pad, F32)...  7.33 us
    ppermute x2, starting transfers between devices, run(): from_next = lax.ppermute(to_p, AXIS, to_prev)  6.95 us
  transfers between devices with their start and end apart: 8, of which 6 were waited for; matrix products, arithmetic and copies ran while one was open for 0% of the time, Pallas kernels for 18%

profile of v6, /device:TPU:0, one launch (start us, length us, event | category | flops | bytes accessed | tf_op | source)
XLA Modules:
  0.0 121.3 jit_solution(15784205584676324486)
XLA Ops:
  0.6 0.0 copy-start
  0.6 0.0 copy-start.1
  0.7 0.0 copy-start.2
  0.7 0.0 copy-start.3
  0.7 0.0 copy-start.4
  0.7 0.0 copy-start.5
  0.7 10.7 %prep.1 = (s32[72,128]{1,0:T(8,128)S(1)}, s32[72,128]{1,0:T(8,128)S(1)}, f32[72,128]{1,0:T(8,128)S(1)}, f32[16,128]{1,0:T(8,128)S(1)}, s32[2]{0:T(128)S(1)}, /*index=5*/f32[8,128]{1,0:T(8,128)S(1)}, s32[1]{0:T(128)}) custom-call(s32[64,128]{1,0:T(8,128)} %bitcast.28, s32[64,128]{1,0:T(8,128)} %bitcast.29, f32[64,128]{1,0:T(8,128)} %bitcast.30, ...), custom_call_target="tpu_custom_call" | custom-call | flops 10000000000 | bytes 10000000 | tf_op jit(solution)/shard_map/prep/pallas_call | solution.py:689
  12.0 0.0 copy-done
  12.0 0.0 copy-done.1
  12.0 0.0 copy-done.2
  12.1 0.0 copy-done.3
  12.1 0.0 copy-done.4
  12.1 0.0 copy-done.5
  12.1 93.3 %conditional.1 = (f32[128,256]{1,0:T(8,128)S(1)}, f32[256,256]{1,0:T(8,128)S(1)}, f32[8,128]{1,0:T(8,128)S(1)}) conditional(s32[]{:T(128)} %bitcast.12, (s32[72,128]{1,0:T(8,128)S(1)}, s32[72,128]{1,0:T(8,128)S(1)}, bf16[2048,128]{1,0:T(8,128)(2,1)S(1)}, f32[128,256]{1,0:T(8,128)S(1)}, s32[2,1024]{1,0:T(2,128)S(1)}, /*index=5*/s32[2]{0:T(128)S(1)}, ...), branch_computations={%region_0.0_spmd, %region_1.0_spmd} | conditional | flops 89999998976 | bytes 112053208 | solution.py:749
  12.1 5.8 %first.2 = (f32[4096,128]{1,0:T(8,128)S(1)}, bf16[1024,256]{1,0:T(8,128)(2,1)S(1)}, bf16[1024,256]{1,0:T(8,128)(2,1)S(1)}, f32[9216,128]{1,0:T(8,128)S(1)}, s32[...) custom-call(bf16[2048,128]{1,0:T(8,128)(2,1)S(1)} %get-tuple-element.51.x, f32[128,256]{1,0:T(8,128)S(1)} %get-tuple-element.52.w1, ...), custom_call_target="tpu_custom_call" | custom-call | flops 10000000000 | bytes 10000000 | tf_op jit(solution)/shard_map/cond/branch_0_fun/first/pallas_call | solution.py:701
  17.9 0.2 collective-permute-start
  18.1 3.4 %collective-permute-start.1 = (bf16[1024,256]{1,0:T(8,128)(2,1)S(1)}, bf16[1024,256]{1,0:T(8,128)(2,1)S(1)}, u32[]{:S(2)}, u32[]{:S(2)}) collective-permute-start(bf16[1024,256]{1,0:T(8,128)(2,1)S(1)} %get-tuple-element.58), channel_id=1, source_target_pairs={{0,15},{1,0},{2,1},{3,2},{4,3},{5,4},{6,5},{7,6},{8,7},{9,8},{10,9... | collective-permute-start | bytes 1572872 | tf_op jit(solution)/shard_map/cond/branch_0_fun/ppermute | solution.py:706
  21.5 5.5 %local_edges.8.part = f32[4096,128]{1,0:T(8,128)S(1)} custom-call(s32[2]{0:T(128)S(1)} %get-tuple-element.48.counts, s32[9216]{0:T(1024)S(1)} %bitcast.36, s32[9216]{0:T(1024)S(1)} %bitcast.48, f32[9216,128]{1,0:T(8,128)S(1)} %get-tuple-element.56.w, f32[4096,128]{1,0:T(8,128)S(1)} %get-tuple-element.59.table), custom_call_target="tpu_custom_call" | custom-call | flops 10000000000 | bytes 10000000 | tf_op jit(solution)/shard_map/cond/branch_0_fun/local_edges/pallas_call | solution.py:718
  27.0 6.9 %collective-permute-done.from_prev = bf16[1024,256]{1,0:T(8,128)(2,1)S(1)} collective-permute-done((bf16[1024,256]{1,0:T(8,128)(2,1)S(1)}, bf16[1024,256]{1,0:T(8,128)(2,1)S(1)}, u32[]{:S(2)}, u32[]{:S(2)}) %collective-permute-start) | collective-permute-done | bytes 524320 | tf_op jit(solution)/shard_map/cond/branch_0_fun/ppermute | solution.py:705
  33.9 0.0 collective-permute-done.1.from_next
  33.9 6.4 %hidden.2 = (bf16[2048,256]{1,0:T(8,128)(2,1)S(1)}, f32[4096,128]{1,0:T(8,128)S(1)}, bf16[1536,128]{1,0:T(8,128)(2,1)S(1)}, bf16[1536,128]{1,0:T(8,128)(2,1)S(1)}, s32[16,128]{1,0:T(8,128)S(1)}) custom-call(s32[2]{0:T(128)S(1)} %get-tuple-element.48.counts, s32[9216]{0:T(1024)S(1)} %bitcast.37, s32[9216]{0:T(1024)S(1)} %bitcast.49, ...), custom_call_target="tpu_custom_call" | custom-call | flops 10000000000 | bytes 10000000 | tf_op jit(solution)/shard_map/cond/branch_0_fun/hidden/pallas_call | solution.py:719
  40.4 0.1 collective-permute-start.2
  40.4 3.5 %collective-permute-start.3 = (bf16[1536,128]{1,0:T(8,128)(2,1)S(1)}, bf16[1536,128]{1,0:T(8,128)(2,1)S(1)}, u32[]{:S(2)}, u32[]{:S(2)}) collective-permute-start(bf16[1536,128]{1,0:T(8,128)(2,1)S(1)} %get-tuple-element.66), channel_id=1, source_target_pairs={{0,15},{1,0},{2,1},{3,2},{4,3},{5,4},{6,5},{7,6},{8,7},{9,8},{10,9... | collective-permute-start | bytes 1179656 | tf_op jit(solution)/shard_map/cond/branch_0_fun/ppermute | solution.py:725
  44.0 5.5 %local_edges.9.part = f32[4096,128]{1,0:T(8,128)S(1)} custom-call(s32[2]{0:T(128)S(1)} %get-tuple-element.48.counts, s32[9216]{0:T(1024)S(1)} %bitcast.38, s32[9216]{0:T(1024)S(1)} %bitcast.50, f32[9216,128]{1,0:T(8,128)S(1)} %get-tuple-element.56.w, f32[4096,128]{1,0:T(8,128)S(1)} %get-tuple-element.67.table), custom_call_target="tpu_custom_call" | custom-call | flops 10000000000 | bytes 10000000 | tf_op jit(solution)/shard_map/cond/branch_0_fun/local_edges/pallas_call | solution.py:727
  49.5 3.2 %collective-permute-done.2.from_prev = bf16[1536,128]{1,0:T(8,128)(2,1)S(1)} collective-permute-done((bf16[1536,128]{1,0:T(8,128)(2,1)S(1)}, bf16[1536,128]{1,0:T(8,128)(2,1)S(1)}, u32[]{:S(2)}, u32[]{:S(2)}) %collective-permute-start.2) | collective-permute-done | bytes 393248 | tf_op jit(solution)/shard_map/cond/branch_0_fun/ppermute | solution.py:724
  52.7 0.0 collective-permute-done.3.from_next
  52.7 6.9 %loss.2 = (f32[8,128]{1,0:T(8,128)S(1)}, f32[4096,128]{1,0:T(8,128)S(1)}, f32[920,128]{1,0:T(8,128)S(1)}, f32[920,128]{1,0:T(8,128)S(1)}) custom-call(s32[2]{0:T(128)S(1)} %get-tuple-element.48.counts, s32[9216]{0:T(1024)S(1)} %bitcast.39, s32[9216]{0:T(1024)S(1)} %bitcast.51, f32[9216,128]{1,0:T(8,128)S(1)} %get-tuple-element.56.w, s32[9216]{0:T(1024)S(1)} %bitcast.18, ...), custom_call_target="tpu_custom_call" | custom-call | flops 10000000000 | bytes 10000000 | tf_op jit(solution)/shard_map/cond/branch_0_fun/loss/pallas_call | solution.py:728
  59.6 3.4 %collective-permute-start.4 = (f32[920,128]{1,0:T(8,128)S(1)}, f32[920,128]{1,0:T(8,128)S(1)}, u32[]{:S(2)}, u32[]{:S(2)}) collective-permute-start(f32[920,128]{1,0:T(8,128)S(1)} %get-tuple-element.70), channel_id=1, source_target_pairs={{0,15},{1,0},{2,1},{3,2},{4,3},{5,4},{6,5},{7,6},{8,7},{9,8},{10,9... | collective-permute-start | bytes 1413128 | tf_op jit(solution)/shard_map/cond/branch_0_fun/ppermute | solution.py:732
  63.0 0.0 collective-permute-start.5
  63.1 5.5 %local_edges.10.part = f32[4096,128]{1,0:T(8,128)S(1)} custom-call(s32[2]{0:T(128)S(1)} %get-tuple-element.48.counts, s32[9216]{0:T(1024)S(1)} %bitcast.40, s32[9216]{0:T(1024)S(1)} %bitcast.52, f32[9216,128]{1,0:T(8,128)S(1)} %get-tuple-element.56.w, f32[4096,128]{1,0:T(8,128)S(1)} %get-tuple-element.72.table), custom_call_target="tpu_custom_call" | custom-call | flops 10000000000 | bytes 10000000 | tf_op jit(solution)/shard_map/cond/branch_0_fun/local_edges/pallas_call | solution.py:734
  68.6 2.1 %collective-permute-done.4.got_prev = f32[920,128]{1,0:T(8,128)S(1)} collective-permute-done((f32[920,128]{1,0:T(8,128)S(1)}, f32[920,128]{1,0:T(8,128)S(1)}, u32[]{:S(2)}, u32[]{:S(2)}) %collective-permute-start.4) | collective-permute-done | bytes 471072 | tf_op jit(solution)/shard_map/cond/branch_0_fun/ppermute | solution.py:732
  70.7 3.2 %collective-permute-done.5.got_next = f32[920,128]{1,0:T(8,128)S(1)} collective-permute-done((f32[920,128]{1,0:T(8,128)S(1)}, f32[920,128]{1,0:T(8,128)S(1)}, u32[]{:S(2)}, u32[]{:S(2)}) %collective-permute-start.5) | collective-permute-done | bytes 471072 | tf_op jit(solution)/shard_map/cond/branch_0_fun/ppermute | solution.py:733
  73.8 7.3 %middle.2 = (f32[256,256]{1,0:T(8,128)S(1)}, f32[4096,128]{1,0:T(8,128)S(1)}, f32[1216,128]{1,0:T(8,128)S(1)}, f32[1216,128]{1,0:T(8,128)S(1)}, s32[16,128]{1,0:T(8,128)S(1)}, /*index=5*/s32[2]{0:T(128)S(1)}) custom-call(s32[2]{0:T(128)S(1)} %get-tuple-element.48.counts, s32[9216]{0:T(1024)S(1)} %bitcast.19, s32[9216]{0:T(1024)S(1)} %bitcast.53, ...), custom_call_target="tpu_custom_call" | custom-call | flops 10000000000 | bytes 10000000 | tf_op jit(solution)/shard_map/cond/branch_0_fun/middle/pallas_call | solution.py:735
  81.2 3.0 %collective-permute-start.6 = (f32[1216,128]{1,0:T(8,128)S(1)}, f32[1216,128]{1,0:T(8,128)S(1)}, u32[]{:S(2)}, u32[]{:S(2)}) collective-permute-start(f32[1216,128]{1,0:T(8,128)S(1)} %get-tuple-element.76), channel_id=1, source_target_pairs={{0,15},{1,0},{2,1},{3,2},{4,3},{5,4},{6,5},{7,6},{8,7},{9,8},{10,9... | collective-permute-start | bytes 1867784 | tf_op jit(solution)/shard_map/cond/branch_0_fun/ppermute | solution.py:740
  84.2 0.0 collective-permute-start.7
  84.2 5.5 %local_edges.11.part = f32[4096,128]{1,0:T(8,128)S(1)} custom-call(s32[2]{0:T(128)S(1)} %get-tuple-element.48.counts, s32[9216]{0:T(1024)S(1)} %bitcast.41, s32[9216]{0:T(1024)S(1)} %bitcast.54, f32[9216,128]{1,0:T(8,128)S(1)} %get-tuple-element.56.w, f32[4096,128]{1,0:T(8,128)S(1)} %get-tuple-element.78.table), custom_call_target="tpu_custom_call" | custom-call | flops 10000000000 | bytes 10000000 | tf_op jit(solution)/shard_map/cond/branch_0_fun/local_edges/pallas_call | solution.py:742
  89.7 5.8 %collective-permute-done.6.got_prev = f32[1216,128]{1,0:T(8,128)S(1)} collective-permute-done((f32[1216,128]{1,0:T(8,128)S(1)}, f32[1216,128]{1,0:T(8,128)S(1)}, u32[]{:S(2)}, u32[]{:S(2)}) %collective-permute-start.6) | collective-permute-done | bytes 622624 | tf_op jit(solution)/shard_map/cond/branch_0_fun/ppermute | solution.py:740
  95.4 6.0 %collective-permute-done.7.got_next = f32[1216,128]{1,0:T(8,128)S(1)} collective-permute-done((f32[1216,128]{1,0:T(8,128)S(1)}, f32[1216,128]{1,0:T(8,128)S(1)}, u32[]{:S(2)}, u32[]{:S(2)}) %collective-permute-start.7) | collective-permute-done | bytes 622624 | tf_op jit(solution)/shard_map/cond/branch_0_fun/ppermute | solution.py:741
  101.4 3.7 %last.2 = f32[128,256]{1,0:T(8,128)S(1)} custom-call(s32[2048]{0:T(1024)S(1)} %bitcast.23, s32[2]{0:T(128)S(1)} %get-tuple-element.74.n_back, s32[16,128]{1,0:T(8,128)S(1)} %get-tuple-element.75.slots, f32[1216,128]{1,0:T(8,128)S(1)} %collective-permute-done.6.got_prev, f32[1216,128]{1,0:T(8,128)S(1)} %collective-permute-done.7.got_next, ...), custom_call_target="tpu_custom_call" | custom-call | flops 10000000000 | bytes 10000000 | tf_op jit(solution)/shard_map/cond/branch_0_fun/last/pallas_call | solution.py:743
  105.4 12.8 %reduce.1 = (f32[128,256]{1,0:T(8,128)S(1)}, f32[172,256]{1,0:T(8,128)S(1)}, f32[1,1]{1,0:T(1,128)}) custom-call(f32[128,256]{1,0:T(8,128)S(1)} %get-tuple-element.137.one, f32[256,256]{1,0:T(8,128)S(1)} %get-tuple-element.138.two, f32[8,128]{1,0:T(8,128)S(1)} %get-tuple-element.139.loss, f32[8,128]{1,0:T(8,128)S(1)} %get-tuple-element.136.count), custom_call_target="tpu_custom_call" | custom-call | flops 10000000000 | bytes 10000000 | tf_op jit(solution)/shard_map/reduce/pallas_call | solution.py:753
  118.8 0.7 copy.22
  119.5 0.7 copy.23
Async XLA Ops:
  0.6 11.4 %copy-start = (bf16[2048,128]{1,0:T(8,128)(2,1)S(1)}, bf16[2048,128]{1,0:T(8,128)(2,1)}, u32[]{:S(2)}) copy-start(bf16[2048,128]{1,0:T(8,128)(2,1)} %param.11) | copy-start | bytes 1572868
  0.6 11.4 %copy-start.1 = (f32[256,172]{0,1:T(8,128)S(1)}, f32[256,172]{0,1:T(8,128)}, u32[]{:S(2)}) copy-start(f32[256,172]{0,1:T(8,128)} %param.13) | copy-start | bytes 528388
  0.7 11.4 %copy-start.2 = (f32[128,256]{1,0:T(8,128)S(1)}, f32[128,256]{1,0:T(8,128)}, u32[]{:S(2)}) copy-start(f32[128,256]{1,0:T(8,128)} %param.12) | copy-start | bytes 393220
  0.7 11.4 %copy-start.3 = (s32[2048]{0:T(1024)S(1)}, s32[2048]{0:T(1024)}, u32[]{:S(2)}) copy-start(s32[2048]{0:T(1024)} %param.19) | copy-start | bytes 24580
  0.7 11.4 %copy-start.4 = (s32[2,1024]{1,0:T(2,128)S(1)}, s32[2,1024]{1,0:T(2,128)}, u32[]{:S(2)}) copy-start(s32[2,1024]{1,0:T(2,128)} %param.14) | copy-start | bytes 24580
  0.7 11.4 %copy-start.5 = (s32[2048]{0:T(1024)S(1)}, s32[2048]{0:T(1024)}, u32[]{:S(2)}) copy-start(s32[2048]{0:T(1024)} %param.18) | copy-start | bytes 24580
  17.9 16.0 %collective-permute-start = (bf16[1024,256]{1,0:T(8,128)(2,1)S(1)}, bf16[1024,256]{1,0:T(8,128)(2,1)S(1)}, u32[]{:S(2)}, u32[]{:S(2)}) collective-permute-start(bf16[1024,256]{1,0:T(8,128)(2,1)S(1)} %get-tuple-element.57), channel_id=1, source_target_pairs={{0,1},{1,2},{2,3},{3,4},{4,5},{5,6},{6,7},{7,8},{8,9},{9,10},{10,1... | collective-permute-start | bytes 1572872 | tf_op jit(solution)/shard_map/cond/branch_0_fun/ppermute | solution.py:705
  18.1 15.8 %collective-permute-start.1 = (bf16[1024,256]{1,0:T(8,128)(2,1)S(1)}, bf16[1024,256]{1,0:T(8,128)(2,1)S(1)}, u32[]{:S(2)}, u32[]{:S(2)}) collective-permute-start(bf16[1024,256]{1,0:T(8,128)(2,1)S(1)} %get-tuple-element.58), channel_id=1, source_target_pairs={{0,15},{1,0},{2,1},{3,2},{4,3},{5,4},{6,5},{7,6},{8,7},{9,8},{10,9... | collective-permute-start | bytes 1572872 | tf_op jit(solution)/shard_map/cond/branch_0_fun/ppermute | solution.py:706
  40.4 12.3 %collective-permute-start.2 = (bf16[1536,128]{1,0:T(8,128)(2,1)S(1)}, bf16[1536,128]{1,0:T(8,128)(2,1)S(1)}, u32[]{:S(2)}, u32[]{:S(2)}) collective-permute-start(bf16[1536,128]{1,0:T(8,128)(2,1)S(1)} %get-tuple-element.65), channel_id=1, source_target_pairs={{0,1},{1,2},{2,3},{3,4},{4,5},{5,6},{6,7},{7,8},{8,9},{9,10},{10,1... | collective-permute-start | bytes 1179656 | tf_op jit(solution)/shard_map/cond/branch_0_fun/ppermute | solution.py:724
  40.4 12.3 %collective-permute-start.3 = (bf16[1536,128]{1,0:T(8,128)(2,1)S(1)}, bf16[1536,128]{1,0:T(8,128)(2,1)S(1)}, u32[]{:S(2)}, u32[]{:S(2)}) collective-permute-start(bf16[1536,128]{1,0:T(8,128)(2,1)S(1)} %get-tuple-element.66), channel_id=1, source_target_pairs={{0,15},{1,0},{2,1},{3,2},{4,3},{5,4},{6,5},{7,6},{8,7},{9,8},{10,9... | collective-permute-start | bytes 1179656 | tf_op jit(solution)/shard_map/cond/branch_0_fun/ppermute | solution.py:725
  59.6 11.0 %collective-permute-start.4 = (f32[920,128]{1,0:T(8,128)S(1)}, f32[920,128]{1,0:T(8,128)S(1)}, u32[]{:S(2)}, u32[]{:S(2)}) collective-permute-start(f32[920,128]{1,0:T(8,128)S(1)} %get-tuple-element.70), channel_id=1, source_target_pairs={{0,15},{1,0},{2,1},{3,2},{4,3},{5,4},{6,5},{7,6},{8,7},{9,8},{10,9... | collective-permute-start | bytes 1413128 | tf_op jit(solution)/shard_map/cond/branch_0_fun/ppermute | solution.py:732
  63.0 10.8 %collective-permute-start.5 = (f32[920,128]{1,0:T(8,128)S(1)}, f32[920,128]{1,0:T(8,128)S(1)}, u32[]{:S(2)}, u32[]{:S(2)}) collective-permute-start(f32[920,128]{1,0:T(8,128)S(1)} %get-tuple-element.71), channel_id=1, source_target_pairs={{0,1},{1,2},{2,3},{3,4},{4,5},{5,6},{6,7},{7,8},{8,9},{9,10},{10,1... | collective-permute-start | bytes 1413128 | tf_op jit(solution)/shard_map/cond/branch_0_fun/ppermute | solution.py:733
  81.2 14.3 %collective-permute-start.6 = (f32[1216,128]{1,0:T(8,128)S(1)}, f32[1216,128]{1,0:T(8,128)S(1)}, u32[]{:S(2)}, u32[]{:S(2)}) collective-permute-start(f32[1216,128]{1,0:T(8,128)S(1)} %get-tuple-element.76), channel_id=1, source_target_pairs={{0,15},{1,0},{2,1},{3,2},{4,3},{5,4},{6,5},{7,6},{8,7},{9,8},{10,9... | collective-permute-start | bytes 1867784 | tf_op jit(solution)/shard_map/cond/branch_0_fun/ppermute | solution.py:740
  84.2 17.3 %collective-permute-start.7 = (f32[1216,128]{1,0:T(8,128)S(1)}, f32[1216,128]{1,0:T(8,128)S(1)}, u32[]{:S(2)}, u32[]{:S(2)}) collective-permute-start(f32[1216,128]{1,0:T(8,128)S(1)} %get-tuple-element.77), channel_id=1, source_target_pairs={{0,1},{1,2},{2,3},{3,4},{4,5},{5,6},{6,7},{7,8},{8,9},{9,10},{10,1... | collective-permute-start | bytes 1867784 | tf_op jit(solution)/shard_map/cond/branch_0_fun/ppermute | solution.py:741
